TPU v7x, 32 devices: a whole 2x2x4 slice. The times are simulated.
32 devices in a mesh: layer: 4 (over y, x), energy: 8 (over z, core).
Axes of the slice: x: 2, y: 2, z: 4, core: 2. Of those that a mesh axis runs over, the one named last changes fastest.
Arguments:
- onsite: float32 [4, 256], P('layer'), may hold values from -1 to 1
- broadening: float32 [4, 256], P('layer'), may hold values from 1 to 2
- hamiltonian: float32 [4, 2, 256, 256], P('layer'), may hold values from -0.078125 to 0.078125
- coupling: float32 [4, 2, 256, 256], P('layer'), may hold values from -0.21875 to 0.21875
- coupling_mask: int32 [4, 256, 256], P('layer'), may hold values 0 or 1
- prior_sigma: float32 [4, 32, 2, 256, 256], P('layer', 'energy'), may hold values from -0.4 to 0.4, as said below
- kernel_weights: float32 [8], replicated, may hold values from 0.1 to 0.6
- kernel_offsets: int32 [8], replicated, may hold values from -7 to 7
Outputs:
- self_energy: float32 [4, 32, 2, 256, 256], P('layer', 'energy')
Inputs may be any that keep to these rules, and one draw needn't show every extreme that they name: `prior_sigma`: real and imaginary parts of the blocks.
All inputs are finite; a program needn't handle non-finite values. No bound on the sum of `coupling_mask` on one device may be relied on, other than what follows from the above.
Results may differ from a plain program's by a relative error of at most 0.0001.
Values sent between devices are 32-bit elements; how exact they have to be, the bound alone decides.
No kernel may reach another device: no remote copies, remote signals or barrier semaphores. Data moves between devices by JAX's collectives and lax.ppermute only.
A program may use at most 128 MiB of HBM per device.

v0:
```python
import jax
import jax.numpy as jnp
from jax import lax
from jax.sharding import PartitionSpec as P

NS_ITERS = 3


exact_mode = lax.Precision.HIGHEST


def matmul_high(first_op, second_op):
    return jnp.matmul(first_op, second_op, precision=exact_mode)


def complex_product(first_op, second_op):
    first_real = first_op[..., 0, :, :]
    first_imag = first_op[..., 1, :, :]
    second_real = second_op[..., 0, :, :]
    second_imag = second_op[..., 1, :, :]
    real_part = matmul_high(first_real, second_real) - matmul_high(first_imag, second_imag)
    imag_part = matmul_high(first_real, second_imag) + matmul_high(first_imag, second_real)
    return jnp.stack([real_part, imag_part], axis=-3)


def adjoint(matrix):
    return jnp.stack(
        [jnp.swapaxes(matrix[..., 0, :, :], -1, -2), -jnp.swapaxes(matrix[..., 1, :, :], -1, -2)],
        axis=-3,
    )


def lead_block(batch_size, orbitals):
    identity = jnp.eye(orbitals, dtype=jnp.float32)
    single = jnp.stack([jnp.zeros_like(identity), -0.5 * identity])
    return jnp.broadcast_to(single, (batch_size, 2, orbitals, orbitals))


def energy_levels(positions, grid_size):
    return -1.0 + 2.0 * (positions.astype(jnp.float32) + 0.5) / grid_size


def solve_layer(
    levels, onsite_row, damping_row, hamilton, coupler, pattern, previous, incoming, sweeps
):
    orbitals = hamilton.shape[-1]
    identity = jnp.eye(orbitals, dtype=jnp.float32)
    hermitian = 0.5 * (hamilton + adjoint(hamilton))
    masked = coupler * pattern[None]
    contact = complex_product(complex_product(masked[None], incoming), adjoint(masked)[None])
    real_diag = levels[:, None] - onsite_row[None, :]
    imag_diag = damping_row[None, :]
    shifted = jnp.stack([real_diag, imag_diag], axis=1)[..., None, :] * identity
    system = shifted - hermitian[None] - contact - previous
    diag_real = jnp.diagonal(system[:, 0], axis1=-2, axis2=-1)
    diag_imag = jnp.diagonal(system[:, 1], axis1=-2, axis2=-1)
    modulus = diag_real * diag_real + diag_imag * diag_imag
    inverse = (
        jnp.stack([diag_real / modulus, -diag_imag / modulus], axis=1)[..., None, :] * identity
    )
    for sweep_no in range(sweeps):
        residue = complex_product(system, inverse)
        inverse = 2.0 * inverse - complex_product(inverse, residue)
    return inverse


def kernel_columns(weights, offsets, row_count, column_energy):
    row_idx = jnp.arange(row_count, dtype=jnp.int32)
    matches = column_energy[None, None, :] == row_idx[None, :, None] + offsets[:, None, None]
    return jnp.sum(jnp.where(matches, weights[:, None, None], jnp.float32(0.0)), axis=0)


def solve_all_layers(gathered, previous, levels_now, orbitals, layer_count):
    incoming = lead_block(levels_now.shape[0], orbitals)
    stacked = []
    for layer_no in range(layer_count):
        incoming = solve_layer(
            levels_now,
            gathered[0][layer_no],
            gathered[1][layer_no],
            gathered[2][layer_no],
            gathered[3][layer_no],
            gathered[4][layer_no],
            previous[layer_no],
            incoming,
            NS_ITERS,
        )
        stacked.append(incoming)
    return stacked


def local(
    onsite,
    broadening,
    hamiltonian,
    coupling,
    coupling_mask,
    prior_sigma,
    kernel_weights,
    kernel_offsets,
):
    layer_count = lax.axis_size("layer")
    group_count = lax.axis_size("energy")
    per_device = prior_sigma.shape[1]
    orbitals = prior_sigma.shape[-1]
    grid_size = per_device * group_count
    sub_count = per_device // layer_count
    first_level = lax.axis_index("energy") * per_device
    own_levels = energy_levels(first_level + jnp.arange(per_device, dtype=jnp.int32), grid_size)
    gathered = (
        lax.all_gather(onsite, "layer", axis=0, tiled=True),
        lax.all_gather(broadening, "layer", axis=0, tiled=True),
        lax.all_gather(hamiltonian, "layer", axis=0, tiled=True),
        lax.all_gather(coupling, "layer", axis=0, tiled=True),
        lax.all_gather(coupling_mask.astype(jnp.float32), "layer", axis=0, tiled=True),
    )
    previous = lax.all_to_all(prior_sigma, "layer", split_axis=1, concat_axis=0, tiled=True)
    levels_now = lax.dynamic_slice_in_dim(
        own_levels, lax.axis_index("layer") * sub_count, sub_count, 0
    )
    stacked = solve_all_layers(gathered, previous, levels_now, orbitals, layer_count)
    joined = jnp.concatenate(stacked, axis=2)
    arrived = lax.all_to_all(joined, ("layer", "energy"), split_axis=2, concat_axis=0, tiled=True)
    slot = jnp.arange(arrived.shape[0], dtype=jnp.int32)
    sender_layer = slot // (group_count * sub_count)
    sender_group = slot // sub_count % group_count
    column_energy = sender_group * per_device + sender_layer * sub_count + slot % sub_count
    kernel = kernel_columns(kernel_weights, kernel_offsets, grid_size, column_energy)
    blended = jnp.einsum("fe,epij->fpij", kernel, arrived, precision=exact_mode)
    scattering = lax.all_to_all(blended, "energy", split_axis=0, concat_axis=2, tiled=True)
    return scattering[None]


def solution(mesh):
    placed = (
        P("layer", None),
        P("layer", None),
        P("layer", None, None, None),
        P("layer", None, None, None),
        P("layer", None, None),
        P("layer", "energy", None, None, None),
        P(),
        P(),
    )
    return jax.shard_map(
        local,
        mesh=mesh,
        in_specs=placed,
        out_specs=P("layer", "energy", None, None, None),
        check_vma=False,
    )
```

profile of v0, /device:TPU:0, one launch (start us, length us, event | category | flops | bytes accessed | tf_op | source)
XLA Modules:
  0.0 352.6 jit_solution(5748276882402703983)
XLA Ops:
  6.5 1.7 convert_element_type.33
  9.7 5.2 %all-to-all-start = ((f32[1,4,2,256,256]{4,3,2,0,1:T(8,128)}), f32[1,4,2,256,256]{4,3,2,0,1:T(8,128)}, u32[]{:S(2)}, u32[]{:S(2)}) async-start(f32[1,4,2,256,256]{4,3,2,0,1:T(8,128)} %bitcast.628), calls=%async_computation | async-start | bytes 4194304 | tf_op jit(solution)/shard_map/all_to_all | solution.py:117
  15.5 30.2 %all-gather = f32[4,1,256]{2,1,0:T(1,128)S(1)} all-gather(f32[1,1,256]{2,1,0:T(1,128)S(1)} %bitcast.645), channel_id=1, replica_groups=mesh['layer'=4,'energy'=8] {'layer'}, dimensions={0}, use_global_device_ids=true | all-gather | bytes 5120 | tf_op jit(solution)/shard_map/all_gather | solution.py:111
  45.7 8.6 %all-gather.1 = f32[4,1,256]{2,1,0:T(1,128)S(1)} all-gather(f32[1,1,256]{2,1,0:T(1,128)S(1)} %bitcast.646), channel_id=1, replica_groups=mesh['layer'=4,'energy'=8] {'layer'}, dimensions={0}, use_global_device_ids=true | all-gather | bytes 5120 | tf_op jit(solution)/shard_map/all_gather | solution.py:112
  56.4 30.5 %all-gather.8.cloned.1.call-done = f32[4,2,256,256]{3,2,1,0:T(8,128)} async-done(((f32[1,2,256,256]{3,2,1,0:T(8,128)}), f32[4,2,256,256]{3,2,1,0:T(8,128)}) %all-gather.8.cloned.1.call-update) | async-done | bytes 2097168 | tf_op jit(solution)/shard_map/all_gather | solution.py:114
  86.9 2.8 slice_multiply_fusion.3
  91.9 32.1 %all-gather.6.cloned.1.call-done = f32[4,2,256,256]{3,2,1,0:T(8,128)} async-done(((f32[1,2,256,256]{3,2,1,0:T(8,128)}), f32[4,2,256,256]{3,2,1,0:T(8,128)}) %all-gather.6.cloned.1.call-update) | async-done | bytes 2097168 | tf_op jit(solution)/shard_map/all_gather | solution.py:113
  123.9 2.8 fusion.132
  126.8 1.8 copy.76
  128.6 1.8 copy.75
  130.3 2.5 bitcast_multiply_fusion
  139.1 2.3 gather_fusion.1
  141.5 2.6 gather_fusion
  157.4 1.5 fusion.25
  159.8 1.7 negate_bitcast_fusion.2
  162.3 1.5 fusion.43
  164.7 2.6 gather_fusion.3
  167.3 2.6 gather_fusion.2
  186.2 1.7 negate_bitcast_fusion.1
  188.8 1.5 fusion.39
  191.1 2.6 gather_fusion.5
  193.7 2.6 gather_fusion.4
  211.8 1.7 negate_bitcast_fusion
  214.3 1.5 fusion.35
  215.9 2.3 gather_fusion.7
  218.3 2.3 gather_fusion.6
  230.7 2.9 copy.67
  233.6 4.8 %all-to-all-start.1 = ((f32[1,2,1024,256]{3,1,0,2:T(2,128)}), f32[1,2,1024,256]{3,1,0,2:T(2,128)S(1)}, u32[]{:S(2)}, u32[]{:S(2)}) async-start(f32[1,2,1024,256]{3,1,0,2:T(2,128)} %copy.67), calls=%async_computation.1 | async-start | bytes 4194304 | tf_op jit(solution)/shard_map/all_to_all | solution.py:123
  238.7 49.8 %all-to-all-done.1 = f32[1,2,1024,256]{3,1,0,2:T(2,128)S(1)} async-done(((f32[1,2,1024,256]{3,1,0,2:T(2,128)}), f32[1,2,1024,256]{3,1,0,2:T(2,128)S(1)}, u32[]{:S(2)}, u32[]{:S(2)}) %all-to-all-start.1) | async-done | bytes 2097184 | tf_op jit(solution)/shard_map/all_to_all | solution.py:123
  288.5 3.0 fusion
  292.7 51.5 %all_to_all.45 = f32[32,2,32,256]{3,2,1,0:T(8,128)S(1)} all-to-all(f32[32,2,32,256]{3,2,1,0:T(8,128)S(1)} %copy.70), channel_id=1, replica_groups=mesh['layer'=4,'energy'=8] {'energy'}, dimensions={0} | all-to-all | bytes 4194304 | tf_op jit(solution)/shard_map/all_to_all | solution.py:130
  344.2 1.5 copy.71
  (263 shorter events, 73.1 us)
Async XLA Ops:
  6.5 48.5 %all-gather.10.cloned.1.call-start = ((), (), s32[]{:S(2)}) async-start(), calls=%async_computation.5 | async-start | bytes 1310720 | tf_op jit(solution)/shard_map/all_gather | solution.py:115
  8.2 78.6 %all-gather.8.cloned.1.call-start = ((), (), s32[]{:S(2)}) async-start(), calls=%async_computation.4 | async-start | bytes 2621440 | tf_op jit(solution)/shard_map/all_gather | solution.py:114
  9.0 115.0 %all-gather.6.cloned.1.call-start = ((), (), s32[]{:S(2)}) async-start(), calls=%async_computation.3 | async-start | bytes 2621440 | tf_op jit(solution)/shard_map/all_gather | solution.py:113
  9.7 5.8 %copy-start.29 = (f32[1,256]{1,0:T(1,128)S(1)}, f32[1,256]{1,0:T(1,128)}, u32[]{:S(2)}) copy-start(f32[1,256]{1,0:T(1,128)} %param.8) | copy-start | bytes 3076
  9.7 36.0 %copy-start.30 = (f32[1,256]{1,0:T(1,128)S(1)}, f32[1,256]{1,0:T(1,128)}, u32[]{:S(2)}) copy-start(f32[1,256]{1,0:T(1,128)} %param.9) | copy-start | bytes 3076
  9.7 128.0 %all-to-all-start = ((f32[1,4,2,256,256]{4,3,2,0,1:T(8,128)}), f32[1,4,2,256,256]{4,3,2,0,1:T(8,128)}, u32[]{:S(2)}, u32[]{:S(2)}) async-start(f32[1,4,2,256,256]{4,3,2,0,1:T(8,128)} %bitcast.628), calls=%async_computation | async-start | bytes 4194304 | tf_op jit(solution)/shard_map/all_to_all | solution.py:117
  56.3 33.3 %copy-start.9 = (f32[256,256]{1,0:T(8,128)}, f32[256,256]{1,0:T(8,128)S(1)}, u32[]{:S(2)}) copy-start(f32[256,256]{1,0:T(8,128)S(1)} %get-tuple-element.21) | copy-start | bytes 786436
  56.4 33.3 %copy-start.10 = (f32[256,256]{1,0:T(8,128)}, f32[256,256]{1,0:T(8,128)S(1)}, u32[]{:S(2)}) copy-start(f32[256,256]{1,0:T(8,128)S(1)} %get-tuple-element.22) | copy-start | bytes 786436
  56.4 33.3 %copy-start.11 = (f32[256,256]{1,0:T(8,128)}, f32[256,256]{1,0:T(8,128)S(1)}, u32[]{:S(2)}) copy-start(f32[256,256]{1,0:T(8,128)S(1)} %get-tuple-element.23) | copy-start | bytes 786436
  56.4 33.3 %copy-start.12 = (f32[256,256]{1,0:T(8,128)}, f32[256,256]{1,0:T(8,128)S(1)}, u32[]{:S(2)}) copy-start(f32[256,256]{1,0:T(8,128)S(1)} %get-tuple-element.24) | copy-start | bytes 786436
  91.9 38.5 %copy-start.1 = (f32[4,2,256,256]{3,2,1,0:T(8,128)S(1)}, f32[4,2,256,256]{3,2,1,0:T(8,128)}, u32[]{:S(2)}) copy-start(f32[4,2,256,256]{3,2,1,0:T(8,128)} %all-gather.8.cloned.1.call-done) | copy-start | bytes 6291460
  132.8 1.8 copy-start.22
  134.6 3.1 copy-start.23
  134.6 3.1 copy-start
  135.0 2.8 copy-start.21
  153.6 1.4 copy-start.25
  153.6 1.4 copy-start.26
  155.5 3.5 copy-start.20
  155.9 5.6 %copy-start.19 = (f32[1,1,256,256]{3,2,1,0:T(8,128)S(1)}, f32[1,1,256,256]{3,2,1,0:T(8,128)}, u32[]{:S(2)}) copy-start(f32[1,1,256,256]{3,2,1,0:T(8,128)} %get-tuple-element.18) | copy-start | bytes 786436
  179.4 1.6 copy-start.13
  179.4 1.6 copy-start.14
  179.5 3.2 copy-start.2
  182.3 3.1 copy-start.18
  182.8 5.2 %copy-start.17 = (f32[1,1,256,256]{3,2,1,0:T(8,128)S(1)}, f32[1,1,256,256]{3,2,1,0:T(8,128)}, u32[]{:S(2)}) copy-start(f32[1,1,256,256]{3,2,1,0:T(8,128)} %get-tuple-element.16) | copy-start | bytes 786436
  206.0 1.4 copy-start.27
  206.0 1.4 copy-start.28
  206.1 2.2 copy-start.4
  207.9 3.1 copy-start.16
  208.3 5.2 %copy-start.15 = (f32[1,1,256,256]{3,2,1,0:T(8,128)S(1)}, f32[1,1,256,256]{3,2,1,0:T(8,128)}, u32[]{:S(2)}) copy-start(f32[1,1,256,256]{3,2,1,0:T(8,128)} %get-tuple-element.14) | copy-start | bytes 786436
  233.6 4.9 %copy-start.31 = (s32[8]{0:T(128)S(1)}, s32[8]{0:T(128)}, u32[]{:S(2)}) copy-start(s32[8]{0:T(128)} %param.15) | copy-start | bytes 100
  233.6 5.0 %copy-start.32 = (f32[8]{0:T(128)S(1)}, f32[8]{0:T(128)}, u32[]{:S(2)}) copy-start(f32[8]{0:T(128)} %param.14) | copy-start | bytes 100
  233.6 54.9 %all-to-all-start.1 = ((f32[1,2,1024,256]{3,1,0,2:T(2,128)}), f32[1,2,1024,256]{3,1,0,2:T(2,128)S(1)}, u32[]{:S(2)}, u32[]{:S(2)}) async-start(f32[1,2,1024,256]{3,1,0,2:T(2,128)} %copy.67), calls=%async_computation.1 | async-start | bytes 4194304 | tf_op jit(solution)/shard_map/all_to_all | solution.py:123
  (6 other events, 6.3 us)
Sparse Core Ops, SparseCore 0:
  9.2 40.0 all-gather.9
  51.1 35.6 all-gather.7
  88.7 35.1 all-gather.5
where the time goes:
time: 358 us; the launch traced here: 353 us
  waiting for transfers between devices  114 us (32%)
  blocking collectives  90.2 us (25%)
  matrix products  59.9 us (17%)
  local copies, waits for them, and re-layouts  41.3 us (12%)
  other arithmetic  22.2 us (6%)
  between operations  15.2 us (4%)
  starting transfers between devices  10.1 us (3%)
    dot_general x128, matrix products, matmul_high(): return jnp.matmul(first_op, second_op, precision=exact_mode)  56.9 us
    all_to_all x1, blocking collectives, local(): lax.all_to_all(blended, 'energy', split_axis=0, concat_axis=2, tiled=True)  51.5 us
    all_to_all x1, waiting for transfers between devices, local(): lax.all_to_all(joined, ('layer', 'energy'), split_axis=2, concat_axis=0,...  49.8 us
    all_gather x1, waiting for transfers between devices, local(): lax.all_gather(hamiltonian, 'layer', axis=0, tiled=True)  32.1 us
    all_gather x1, waiting for transfers between devices, local(): lax.all_gather(coupling, 'layer', axis=0, tiled=True)  30.5 us
    all_gather x1, blocking collectives, local(): lax.all_gather(onsite, 'layer', axis=0, tiled=True)  30.2 us
    gather x4, local copies, waits for them, and re-layouts, solve_layer(): diag_real = jnp.diagonal(system[:, 0], axis1=-2, axis2=-1)  10 us
    gather x4, local copies, waits for them, and re-layouts, solve_layer(): diag_imag = jnp.diagonal(system[:, 1], axis1=-2, axis2=-1)  9.82 us
  transfers between devices with their start and end apart: 5, of which 3 were waited for; matrix products, arithmetic and copies ran while one was open for 6% of the time, Pallas kernels for 0%

commit v1 on v0

v1 whole, which is shorter than its diff:
```python
import functools

import jax
import jax.numpy as jnp
from jax import lax
from jax.experimental import pallas as pl
from jax.experimental.pallas import tpu as pltpu
from jax.sharding import PartitionSpec as P

NS_ITERS = 3
REACH = 7

AXES = ("layer", "energy")
F32 = jnp.float32
BF16 = jnp.bfloat16
HBM = pltpu.HBM
VMEM = pltpu.VMEM


def split(x):
    high = x.astype(BF16)
    low = (x - high.astype(F32)).astype(BF16)
    return high, low


def dot(a, b, transposed):
    dims = (((1,), (1 if transposed else 0,)), ((), ()))
    return lax.dot_general(a, b, dims, preferred_element_type=F32)


def dot3(a, b, transposed=False):
    return (
        dot(a[0], b[0], transposed) + dot(a[0], b[1], transposed) + dot(a[1], b[0], transposed)
    )


def negated(a):
    return (-a[0], -a[1])


def product(a, b):
    real = dot3(a[0], b[0]) + dot3(negated(a[1]), b[1])
    imag = dot3(a[0], b[1]) + dot3(a[1], b[0])
    return real, imag


def product_adjoint(a, c):
    real = dot3(a[0], c[0], True) + dot3(a[1], c[1], True)
    imag = dot3(a[1], c[0], True) + dot3(negated(a[0]), c[1], True)
    return real, imag


def split_pair(pair):
    return split(pair[0]), split(pair[1])


def eye_mask(n):
    return lax.broadcasted_iota(jnp.int32, (n, n), 0) == lax.broadcasted_iota(
        jnp.int32, (n, n), 1
    )


def inverse_of(real, imag):
    n = real.shape[0]
    eye = eye_mask(n)
    zero = jnp.zeros_like(real)
    diag_real = jnp.where(eye, real, zero)
    diag_imag = jnp.where(eye, imag, zero)

    def reciprocal(axis):
        dr = jnp.sum(diag_real, axis=axis, keepdims=True)
        di = jnp.sum(diag_imag, axis=axis, keepdims=True)
        modulus = dr * dr + di * di
        return dr / modulus, -di / modulus

    row_r, row_i = reciprocal(0)
    col_r, col_i = reciprocal(1)
    e_r = jnp.where(eye, zero, real * -row_r + imag * row_i)
    e_i = jnp.where(eye, zero, real * -row_i - imag * row_r)
    unit = jnp.where(eye, 1.0, 0.0).astype(F32)
    f_r, f_i = unit + e_r, e_i
    for _ in range(NS_ITERS - 1):
        es = split_pair((e_r, e_i))
        e_r, e_i = product(es, es)
        es = split_pair((e_r, e_i))
        g_r, g_i = product(split_pair((f_r, f_i)), es)
        f_r, f_i = f_r + g_r, f_i + g_i
    return col_r * f_r - col_i * f_i, col_r * f_i + col_i * f_r


def prep_kernel(
    where_ref, levels_ref, onsite_ref, broad_ref, ham_ref, coup_ref, mask_ref, prior_ref,
    *out_refs
):
    layer_count = prior_ref.shape[1]
    base_refs = out_refs[:layer_count]
    masked_ref, send_ref = out_refs[layer_count:]
    layer, core = where_ref[0], where_ref[1]
    n = ham_ref.shape[-1]
    mask = mask_ref[0].astype(F32)
    c_r, c_i = coup_ref[0, 0] * mask, coup_ref[0, 1] * mask
    masked_ref[0], masked_ref[1] = c_r, c_i
    send_ref[...] = masked_ref[core]
    h_r, h_i = ham_ref[0, 0], ham_ref[0, 1]
    eye = eye_mask(n)
    cs = split_pair((c_r, c_i))
    q_r, q_i = product_adjoint(cs, cs)
    first = jnp.where(layer == 0, 0.5, 0.0).astype(F32)
    fixed_r = -0.5 * (h_r + h_r.T) - first * q_i + jnp.where(eye, -onsite_ref[...], 0.0)
    fixed_i = -0.5 * (h_i - h_i.T) + first * q_r + jnp.where(eye, broad_ref[...], 0.0)
    for k in range(layer_count):
        mine = jnp.bitwise_xor(layer, k)
        level = levels_ref[mine]
        base_refs[k][0] = fixed_r - prior_ref[0, mine, 0] + jnp.where(eye, level, 0.0)
        base_refs[k][1] = fixed_i - prior_ref[0, mine, 1]


def first_kernel(where_ref, *refs):
    layer_count = len(refs) - 3
    base_refs, green_ref, base, sem = refs[:layer_count], refs[-3], refs[-2], refs[-1]
    mine = where_ref[0]
    for k in range(layer_count):
        @pl.when(mine == k)
        def _(k=k):
            copy = pltpu.make_async_copy(base_refs[k], base, sem)
            copy.start()
            copy.wait()
    green_ref[0], green_ref[1] = inverse_of(base[0], base[1])


def rest_kernel(layer_count, where_ref, *refs):
    refs = list(refs)
    take = lambda count: [refs.pop(0) for _ in range(count)]
    base_refs = take(layer_count)
    (masked_ref,) = take(1)
    same_refs, other_refs = take(layer_count - 1), take(layer_count - 1)
    (green_in,) = take(1)
    out_refs = take(layer_count)
    bases, coups, greens, in_sems, out_sems = refs
    layer, core = where_ref[0], where_ref[1]
    other = 1 - core

    def inputs(l, k):
        if k == 0:
            pairs = [(masked_ref, coups.at[l])]
        else:
            pairs = [
                (same_refs[k - 1], coups.at[l, core]),
                (other_refs[k - 1], coups.at[l, other]),
            ]
        pairs.append((base_refs[k], bases.at[l]))
        return [pltpu.make_async_copy(s, d, in_sems.at[l, i]) for i, (s, d) in enumerate(pairs)]

    for l in range(1, layer_count):
        for k in range(layer_count):
            @pl.when(jnp.bitwise_xor(layer, l) == k)
            def _(l=l, k=k):
                for copy in inputs(l, k):
                    copy.start()
    greens[0] = green_in[...]

    def output(l, k):
        return pltpu.make_async_copy(greens.at[l], out_refs[k], out_sems.at[k])

    def put(l):
        for k in range(layer_count):
            @pl.when(jnp.bitwise_xor(layer, l) == k)
            def _(k=k):
                output(l, k).start()

    put(0)
    for l in range(1, layer_count):
        for k in range(layer_count):
            @pl.when(jnp.bitwise_xor(layer, l) == k)
            def _(l=l, k=k):
                for copy in inputs(l, k):
                    copy.wait()

    def step(l, carry):
        cs = split_pair((coups[l, 0], coups[l, 1]))
        moved = product(cs, split_pair((greens[l - 1, 0], greens[l - 1, 1])))
        contact_r, contact_i = product_adjoint(split_pair(moved), cs)
        greens[l, 0], greens[l, 1] = inverse_of(
            bases[l, 0] - contact_r, bases[l, 1] - contact_i
        )
        put(l)
        return carry

    lax.fori_loop(1, layer_count, step, 0)
    for k in range(layer_count):
        output(0, k).wait()


def mix_kernel(has_acc, weight_ref, *refs):
    refs = list(refs)
    out_ref = refs.pop()
    acc_ref = refs.pop(0) if has_acc else None
    outputs, _, rows, _ = out_ref.shape[1:]
    step_rows = 8

    def body(i, carry):
        part = i // (rows // step_rows)
        here = pl.ds(pl.multiple_of((i % (rows // step_rows)) * step_rows, step_rows), step_rows)
        if has_acc:
            total = [acc_ref[0, f, part, here, :] for f in range(outputs)]
        else:
            total = [None] * outputs
        for j, ref in enumerate(refs):
            x = ref[part, here, :]
            for f in range(outputs):
                term = weight_ref[f, j] * x
                total[f] = term if total[f] is None else total[f] + term
        for f in range(outputs):
            out_ref[0, f, part, here, :] = total[f]
        return carry

    lax.fori_loop(0, 2 * (rows // step_rows), body, 0)


def mix(weights, acc, blocks, outputs):
    _, n, _ = blocks[0].shape
    rows = 64 if n % 64 == 0 else n
    small = pl.BlockSpec((2, rows, n), lambda i: (0, i, 0))
    large = pl.BlockSpec((1, outputs, 2, rows, n), lambda i: (0, 0, 0, i, 0))
    head = [] if acc is None else [acc]
    return pl.pallas_call(
        functools.partial(mix_kernel, acc is not None),
        grid=(n // rows,),
        in_specs=[pl.BlockSpec(memory_space=pltpu.SMEM)]
        + [large] * len(head)
        + [small] * len(blocks),
        out_specs=large,
        out_shape=jax.ShapeDtypeStruct((1, outputs, 2, n, n), F32),
        name="mix_more" if head else "mix_first",
    )(weights, *head, *blocks)


def weights_for(kernel_weights, kernel_offsets, rows, columns):
    matches = columns[None, None, :] == rows[None, :, None] + kernel_offsets[:, None, None]
    return jnp.sum(jnp.where(matches, kernel_weights[:, None, None], F32(0.0)), axis=0)


def local(
    onsite, broadening, hamiltonian, coupling, coupling_mask, prior_sigma,
    kernel_weights, kernel_offsets,
):
    layer_count = lax.axis_size("layer")
    group_count = lax.axis_size("energy")
    per_device = prior_sigma.shape[1]
    n = prior_sigma.shape[-1]
    grid_size = per_device * group_count
    span = 2 * per_device
    assert per_device == layer_count and layer_count & (layer_count - 1) == 0
    assert group_count % 2 == 0 and span > REACH
    layer = lax.axis_index("layer")
    group = lax.axis_index("energy")
    core, pair = group % 2, group // 2
    where = jnp.stack([layer, core]).astype(jnp.int32)
    block = jax.ShapeDtypeStruct((2, n, n), F32)
    smem = pl.BlockSpec(memory_space=pltpu.SMEM)
    hbm = pl.BlockSpec(memory_space=HBM)
    vmem = pl.BlockSpec(memory_space=VMEM)

    everyone = [(l, g) for l in range(layer_count) for g in range(group_count)]

    def move(x, target, wanted=lambda l, g: True):
        pairs = []
        for l, g in everyone:
            if not wanted(l, g):
                continue
            tl, tg = target(l, g)
            if 0 <= tg < group_count:
                pairs.append((l * group_count + g, tl * group_count + tg))
        return lax.ppermute(x, AXES, pairs)

    def to_layer(x, k):
        return move(x, lambda l, g: (l ^ k, g))

    own = group * per_device + jnp.arange(per_device, dtype=jnp.int32)
    levels = -1.0 + 2.0 * (own.astype(F32) + 0.5) / grid_size
    prepared = pl.pallas_call(
        prep_kernel,
        in_specs=[smem, smem] + [vmem] * 6,
        out_specs=[vmem] * (layer_count + 2),
        out_shape=[block] * (layer_count + 1) + [jax.ShapeDtypeStruct((n, n), F32)],
        name="prep",
    )(where, levels, onsite, broadening, hamiltonian, coupling, coupling_mask, prior_sigma)
    bases, masked, half = list(prepared[:layer_count]), prepared[-2], prepared[-1]
    ks = range(1, layer_count)
    bases = bases[:1] + [to_layer(bases[k], k) for k in ks]
    same = [to_layer(half, k) for k in ks]
    other = [move(x, lambda l, g: (l, g ^ 1)) for x in same]
    green = pl.pallas_call(
        first_kernel,
        in_specs=[smem] + [hbm] * layer_count,
        out_specs=vmem,
        out_shape=block,
        scratch_shapes=[VMEM((2, n, n), F32), pltpu.SemaphoreType.DMA],
        name="solve_first",
    )(where, *bases)
    greens = pl.pallas_call(
        functools.partial(rest_kernel, layer_count),
        in_specs=[smem] + [hbm] * (layer_count + 1 + 2 * len(ks)) + [vmem],
        out_specs=[hbm] * layer_count,
        out_shape=[block] * layer_count,
        scratch_shapes=[
            VMEM((layer_count, 2, n, n), F32),
            VMEM((layer_count, 2, n, n), F32),
            VMEM((layer_count, 2, n, n), F32),
            pltpu.SemaphoreType.DMA((layer_count, 3)),
            pltpu.SemaphoreType.DMA((layer_count,)),
        ],
        name="solve_rest",
    )(where, *bases, masked, *same, *other, green)

    mine = [greens[0]] + [to_layer(greens[k], k) for k in ks]

    def energy_in_pair(l, g, k):
        return per_device * (g % 2) + (l ^ k)

    up, down, theirs, cross = [], [], [], []
    for k in range(layer_count):
        up.append(
            move(
                mine[k],
                lambda l, g: (l, g + 2),
                lambda l, g: span - energy_in_pair(l, g, k) <= REACH,
            )
        )
        down.append(
            move(
                mine[k],
                lambda l, g: (l, g - 2),
                lambda l, g: energy_in_pair(l, g, k) + 1 <= REACH,
            )
        )
        theirs.append(move(mine[k], lambda l, g: (l, g ^ 1)))
        cross.append(
            (
                move(up[k], lambda l, g: (l, g - 1), lambda l, g: g % 2 == 1),
                move(down[k], lambda l, g: (l, g + 1), lambda l, g: g % 2 == 0),
            )
        )

    def energy(shift, c, k):
        return span * (pair + shift) + per_device * c + jnp.bitwise_xor(layer, k)

    def mixed(acc, entries):
        columns = jnp.stack([e for _, e in entries])
        w = weights_for(kernel_weights, kernel_offsets, own, columns)
        return mix(w, acc, [x for x, _ in entries], per_device)

    def far(k):
        return [
            (up[k], energy(-1, core, k)),
            (down[k], energy(1, core, k)),
            (cross[k][0], energy(-1, 1 - core, k)),
            (cross[k][1], energy(1, 1 - core, k)),
        ]

    near = []
    for k in range(layer_count):
        near += [(mine[k], energy(0, core, k)), (theirs[k], energy(0, 1 - core, k))]
    acc = mixed(None, near)
    acc = mixed(acc, [entry for k in range(layer_count - 1) for entry in far(k)])
    return mixed(acc, far(layer_count - 1))


def solution(mesh):
    placed = (
        P("layer", None),
        P("layer", None),
        P("layer", None, None, None),
        P("layer", None, None, None),
        P("layer", None, None),
        P("layer", "energy", None, None, None),
        P(),
        P(),
    )
    return jax.shard_map(
        local,
        mesh=mesh,
        in_specs=placed,
        out_specs=P("layer", "energy", None, None, None),
        check_vma=False,
    )
```

time: 358 us -> 163 us (0.46); the launches traced: 353 us -> 162 us
  blocking collectives: 90.2 us -> 0 us
  matrix products: 59.9 us -> 0 us
  waiting for transfers between devices: 114 us -> 61.4 us
  starting transfers between devices: 10.1 us -> 53.8 us
  Pallas kernels: 0 us -> 40.1 us
  local copies, waits for them, and re-layouts: 41.3 us -> 2.96 us
  other arithmetic: 22.2 us -> 3.37 us
  between operations: 15.2 us -> 0.46 us
    all_gather x3 -> x0, waiting for transfers between devices: 62.6 us -> none  [the longest x1 32.1 us: local(): lax.all_gather(hamiltonian, 'layer', axis=0, tiled=True)]
    ppermute x0 -> x32, waiting for transfers between devices: none -> 61.4 us  [move(): return lax.ppermute(x, AXES, pairs)]
    dot_general x129 -> x0, matrix products: 59.9 us -> none  [the longest x128 56.9 us: matmul_high(): return jnp.matmul(first_op, second_op, precision=exact_mode)]
    ppermute x0 -> x32, starting transfers between devices: none -> 53.8 us  [move(): return lax.ppermute(x, AXES, pairs)]
    all_to_all x1 -> x0, blocking collectives: 51.5 us -> none  [local(): lax.all_to_all(blended, 'energy', split_axis=0, concat_axis=2, tiled=True)]
    all_to_all x2 -> x0, waiting for transfers between devices: 49.8 us -> none  [the longest x1 49.8 us: local(): lax.all_to_all(joined, ('layer', 'energy'), split_axis=2, concat_axis=0,...]
    pallas_call x0 -> x6, Pallas kernels: none -> 40.1 us  [the longest x3 17.1 us: mix(): pl.pallas_call(functools.partial(mix_kernel, acc is not None), grid=(n //...]
    all_gather x2 -> x0, blocking collectives: 38.8 us -> none  [the longest x1 30.2 us: local(): lax.all_gather(onsite, 'layer', axis=0, tiled=True)]
  transfers between devices with their start and end apart: 5 -> 32, of which waited for: 3 -> 8; matrix products, arithmetic and copies ran while one was open for 6% -> 1% of each run, Pallas kernels for 0% -> 10%
where the time goes in v1:
time: 163 us; the launch traced here: 162 us
  waiting for transfers between devices  61.4 us (38%)
  starting transfers between devices  53.8 us (33%)
  Pallas kernels  40.1 us (25%)
  other arithmetic  3.37 us (2%)
  local copies, waits for them, and re-layouts  2.96 us (2%)
    ppermute x32, waiting for transfers between devices, move(): return lax.ppermute(x, AXES, pairs)  61.4 us
    ppermute x32, starting transfers between devices, move(): return lax.ppermute(x, AXES, pairs)  53.8 us
    pallas_call x3, Pallas kernels, mix(): pl.pallas_call(functools.partial(mix_kernel, acc is not None), grid=(n //...  17.1 us
    pallas_call x1, Pallas kernels, local(): pl.pallas_call(functools.partial(rest_kernel, layer_count), in_specs=[sme...  13.9 us
    pallas_call x1, Pallas kernels, local(): pl.pallas_call(first_kernel, in_specs=[smem] + [hbm] * layer_count, out_s...  4.74 us
    pallas_call x1, Pallas kernels, local(): pl.pallas_call(prep_kernel, in_specs=[smem, smem] + [vmem] * 6, out_specs...  4.37 us
  transfers between devices with their start and end apart: 32, of which 8 were waited for; matrix products, arithmetic and copies ran while one was open for 1% of the time, Pallas kernels for 10%

profile of v1, /device:TPU:0, one launch (start us, length us, event | category | flops | bytes accessed | tf_op | source)
XLA Modules:
  0.0 162.1 jit_solution(11310330989512259573)
XLA Ops:
  1.1 4.4 %prep.1 = (f32[2,256,256]{2,1,0:T(8,128)}, f32[2,256,256]{2,1,0:T(8,128)}, f32[2,256,256]{2,1,0:T(8,128)}, f32[2,256,256]{2,1,0:T(8,128)}, f32[2,256,256]{2,1,0:T(8,128)}, /*index=5*/f32[256,256]{1,0:T(8,128)}) custom-call(s32[2]{0:T(128)} %pad_add_fusion.1.where_ref, f32[4]{0:T(128)} %multiply_add_fusion.levels_ref, f32[1,256]{1,0:T(1,128)} %onsite_ref.1, ...), custom_call_target="tpu_custom_call" | custom-call | tf_op jit(solution)/shard_map/prep/pallas_call | solution.py:281
  5.5 3.0 %collective-permute-start.3 = (f32[256,256]{1,0:T(8,128)}, f32[256,256]{1,0:T(8,128)S(1)}, u32[]{:S(2)}, u32[]{:S(2)}) collective-permute-start(f32[256,256]{1,0:T(8,128)} %get-tuple-element.20), channel_id=1, source_target_pairs={{0,8},{1,9},{2,10},{3,11},{4,12},{5,13},{6,14},{7,15},{8,0},{9,1},... | collective-permute-start | bytes 786440 | tf_op jit(solution)/shard_map/ppermute | solution.py:274
  8.5 2.0 %collective-permute-start.1 = (f32[2,256,256]{2,1,0:T(8,128)}, f32[2,256,256]{2,1,0:T(8,128)S(1)}, u32[]{:S(2)}, u32[]{:S(2)}) collective-permute-start(f32[2,256,256]{2,1,0:T(8,128)} %get-tuple-element.17), channel_id=1, source_target_pairs={{0,16},{1,17},{2,18},{3,19},{4,20},{5,21},{6,22},{7,23},{8,24},{9,... | collective-permute-start | bytes 1572872 | tf_op jit(solution)/shard_map/ppermute | solution.py:274
  10.5 1.4 collective-permute-start.2
  12.0 1.5 collective-permute-start.4
  13.5 2.4 %collective-permute-done.3.refs_5_ = f32[256,256]{1,0:T(8,128)S(1)} collective-permute-done((f32[256,256]{1,0:T(8,128)}, f32[256,256]{1,0:T(8,128)S(1)}, u32[]{:S(2)}, u32[]{:S(2)}) %collective-permute-start.3) | collective-permute-done | bytes 262176 | tf_op jit(solution)/shard_map/ppermute | solution.py:274
  15.8 3.0 %collective-permute-start.5 = (f32[256,256]{1,0:T(8,128)}, f32[256,256]{1,0:T(8,128)S(1)}, u32[]{:S(2)}, u32[]{:S(2)}) collective-permute-start(f32[256,256]{1,0:T(8,128)} %get-tuple-element.20), channel_id=1, source_target_pairs={{0,24},{1,25},{2,26},{3,27},{4,28},{5,29},{6,30},{7,31},{8,16},{9,... | collective-permute-start | bytes 786440 | tf_op jit(solution)/shard_map/ppermute | solution.py:274
  18.8 25.8 %collective-permute-done.4.refs_6_ = f32[256,256]{1,0:T(8,128)S(1)} collective-permute-done((f32[256,256]{1,0:T(8,128)}, f32[256,256]{1,0:T(8,128)S(1)}, u32[]{:S(2)}, u32[]{:S(2)}) %collective-permute-start.4) | collective-permute-done | bytes 262176 | tf_op jit(solution)/shard_map/ppermute | solution.py:274
  46.3 4.7 %solve_first.1.refs_11_ = f32[2,256,256]{2,1,0:T(8,128)} custom-call(s32[2]{0:T(128)} %pad_add_fusion.1.where_ref, f32[2,256,256]{2,1,0:T(8,128)} %get-tuple-element.15.refs_0_, f32[2,256,256]{2,1,0:T(8,128)} %copy-done, f32[2,256,256]{2,1,0:T(8,128)} %copy-done.1, f32[2,256,256]{2,1,0:T(8,128)} %copy-done.2), custom_call_target="tpu_custom_call" | custom-call | tf_op jit(solution)/shard_map/solve_first/pallas_call | solution.py:293
  51.9 13.9 %solve_rest.1 = (f32[2,256,256]{2,1,0:T(8,128)}, f32[2,256,256]{2,1,0:T(8,128)}, f32[2,256,256]{2,1,0:T(8,128)}, f32[2,256,256]{2,1,0:T(8,128)}) custom-call(s32[2]{0:T(128)} %pad_add_fusion.1.where_ref, f32[2,256,256]{2,1,0:T(8,128)} %get-tuple-element.15.refs_0_, f32[2,256,256]{2,1,0:T(8,128)} %copy-done, f32[2,256,256]{2,1,0:T(8,128)} %copy-done.1, ...), custom_call_target="tpu_custom_call" | custom-call | tf_op jit(solution)/shard_map/solve_rest/pallas_call | solution.py:301
  66.2 1.7 %collective-permute-start.10 = (f32[2,256,256]{2,1,0:T(8,128)}, f32[2,256,256]{2,1,0:T(8,128)S(1)}, u32[]{:S(2)}, u32[]{:S(2)}) collective-permute-start(f32[2,256,256]{2,1,0:T(8,128)} %get-tuple-element.22), channel_id=1, source_target_pairs={{0,8},{1,9},{2,10},{3,11},{4,12},{5,13},{6,14},{7,15},{8,0},{9,1},... | collective-permute-start | bytes 1572872 | tf_op jit(solution)/shard_map/ppermute | solution.py:274
  67.9 1.5 collective-permute-start.12
  70.4 1.3 collective-permute-start.17
  71.7 9.5 %collective-permute-done.10.refs_2_ = f32[2,256,256]{2,1,0:T(8,128)S(1)} collective-permute-done((f32[2,256,256]{2,1,0:T(8,128)}, f32[2,256,256]{2,1,0:T(8,128)S(1)}, u32[]{:S(2)}, u32[]{:S(2)}) %collective-permute-start.10) | collective-permute-done | bytes 524320 | tf_op jit(solution)/shard_map/ppermute | solution.py:274
  81.2 11.9 %collective-permute-done.12.refs_4_ = f32[2,256,256]{2,1,0:T(8,128)S(1)} collective-permute-done((f32[2,256,256]{2,1,0:T(8,128)}, f32[2,256,256]{2,1,0:T(8,128)S(1)}, u32[]{:S(2)}, u32[]{:S(2)}) %collective-permute-start.12) | collective-permute-done | bytes 524320 | tf_op jit(solution)/shard_map/ppermute | solution.py:274
  94.9 3.1 %collective-permute-start.19 = (f32[2,256,256]{2,1,0:T(8,128)S(1)}, f32[2,256,256]{2,1,0:T(8,128)S(1)}, u32[]{:S(2)}, u32[]{:S(2)}) collective-permute-start(f32[2,256,256]{2,1,0:T(8,128)S(1)} %collective-permute-done.17.refs_2_), channel_id=1, source_target_pairs={{0,1},{2,3},{4,5},{6,7},{8,9},{10,11},{12,13},{14,15},{16,17},{18,... | collective-permute-start | bytes 1572872 | tf_op jit(solution)/shard_map/ppermute | solution.py:274
  98.1 4.3 %collective-permute-start.20 = (f32[2,256,256]{2,1,0:T(8,128)S(1)}, f32[2,256,256]{2,1,0:T(8,128)}, u32[]{:S(2)}, u32[]{:S(2)}) collective-permute-start(f32[2,256,256]{2,1,0:T(8,128)S(1)} %collective-permute-done.10.refs_2_), channel_id=1, source_target_pairs={{0,2},{1,3},{2,4},{3,5},{4,6},{5,7},{9,11},{11,13},{13,15},{16,18}... | collective-permute-start | bytes 1572872 | tf_op jit(solution)/shard_map/ppermute | solution.py:274
  102.4 1.3 collective-permute-start.21
  103.7 5.4 %collective-permute-start.24 = (f32[2,256,256]{2,1,0:T(8,128)S(1)}, f32[2,256,256]{2,1,0:T(8,128)}, u32[]{:S(2)}, u32[]{:S(2)}) collective-permute-start(f32[2,256,256]{2,1,0:T(8,128)S(1)} %collective-permute-done.12.refs_4_), channel_id=1, source_target_pairs={{0,2},{1,3},{2,4},{3,5},{4,6},{5,7},{8,10},{9,11},{10,12},{11,13},... | collective-permute-start | bytes 1572872 | tf_op jit(solution)/shard_map/ppermute | solution.py:274
  109.0 1.3 collective-permute-start.25
  110.4 5.4 %collective-permute-start.28 = (f32[2,256,256]{2,1,0:T(8,128)S(1)}, f32[2,256,256]{2,1,0:T(8,128)}, u32[]{:S(2)}, u32[]{:S(2)}) collective-permute-start(f32[2,256,256]{2,1,0:T(8,128)S(1)} %collective-permute-done.14.refs_6_), channel_id=1, source_target_pairs={{0,2},{1,3},{2,4},{3,5},{4,6},{5,7},{8,10},{9,11},{10,12},{11,13},... | collective-permute-start | bytes 1572872 | tf_op jit(solution)/shard_map/ppermute | solution.py:274
  115.7 1.3 collective-permute-start.29
  117.0 2.0 %collective-permute-done.21.refs_6_ = f32[2,256,256]{2,1,0:T(8,128)S(1)} collective-permute-done((f32[2,256,256]{2,1,0:T(8,128)S(1)}, f32[2,256,256]{2,1,0:T(8,128)S(1)}, u32[]{:S(2)}, u32[]{:S(2)}) %collective-permute-start.21) | collective-permute-done | bytes 524320 | tf_op jit(solution)/shard_map/ppermute | solution.py:274
  121.5 3.6 %collective-permute-done.24.refs_9_ = f32[2,256,256]{2,1,0:T(8,128)} collective-permute-done((f32[2,256,256]{2,1,0:T(8,128)S(1)}, f32[2,256,256]{2,1,0:T(8,128)}, u32[]{:S(2)}, u32[]{:S(2)}) %collective-permute-start.24) | collective-permute-done | bytes 524320 | tf_op jit(solution)/shard_map/ppermute | solution.py:274
  125.1 2.1 %collective-permute-start.23 = (f32[2,256,256]{2,1,0:T(8,128)}, f32[2,256,256]{2,1,0:T(8,128)}, u32[]{:S(2)}, u32[]{:S(2)}) collective-permute-start(f32[2,256,256]{2,1,0:T(8,128)} %copy-done.14), channel_id=1, source_target_pairs={{0,1},{2,3},{4,5},{6,7},{8,9},{10,11},{12,13},{14,15},{16,17},{18,... | collective-permute-start | bytes 1572872 | tf_op jit(solution)/shard_map/ppermute | solution.py:274
  127.2 1.3 collective-permute-done.25.refs_10_
  129.8 4.9 %collective-permute-done.28.refs_1_ = f32[2,256,256]{2,1,0:T(8,128)} collective-permute-done((f32[2,256,256]{2,1,0:T(8,128)S(1)}, f32[2,256,256]{2,1,0:T(8,128)}, u32[]{:S(2)}, u32[]{:S(2)}) %collective-permute-start.28) | collective-permute-done | bytes 524320 | tf_op jit(solution)/shard_map/ppermute | solution.py:274
  134.7 2.1 %collective-permute-start.27 = (f32[2,256,256]{2,1,0:T(8,128)}, f32[2,256,256]{2,1,0:T(8,128)}, u32[]{:S(2)}, u32[]{:S(2)}) collective-permute-start(f32[2,256,256]{2,1,0:T(8,128)} %collective-permute-done.25.refs_10_), channel_id=1, source_target_pairs={{0,1},{2,3},{4,5},{6,7},{8,9},{10,11},{12,13},{14,15},{16,17},{18,... | collective-permute-start | bytes 1572872 | tf_op jit(solution)/shard_map/ppermute | solution.py:274
  138.1 4.6 %collective-permute-start.31 = (f32[2,256,256]{2,1,0:T(8,128)}, f32[2,256,256]{2,1,0:T(8,128)}, u32[]{:S(2)}, u32[]{:S(2)}) collective-permute-start(f32[2,256,256]{2,1,0:T(8,128)} %collective-permute-done.29.refs_2_), channel_id=1, source_target_pairs={{0,1},{2,3},{4,5},{6,7},{8,9},{10,11},{12,13},{14,15},{16,17},{18,... | collective-permute-start | bytes 1572872 | tf_op jit(solution)/shard_map/ppermute | solution.py:274
  144.9 5.5 %mix_first.1.refs_0_ = f32[1,4,2,256,256]{4,3,2,1,0:T(8,128)} custom-call(f32[4,8]{1,0:T(4,128)} %select_reduce_fusion.weight_ref, f32[2,256,256]{2,1,0:T(8,128)} %get-tuple-element.21.refs_0_, f32[2,256,256]{2,1,0:T(8,128)} %copy-done.4, f32[2,256,256]{2,1,0:T(8,128)} %copy-done.5, f32[2,256,256]{2,1,0:T(8,128)} %copy-done.9, f32[2,256,256]{2,1,0:T(8,128)} %copy-done.7, ...), custom_call_target="tpu_custom_call" | custom-call | tf_op jit(solution)/shard_map/mix_first/pallas_call | solution.py:226
  150.5 6.7 %mix_more.2.refs_0_ = f32[1,4,2,256,256]{4,3,2,1,0:T(8,128)} custom-call(f32[4,12]{1,0:T(4,128)} %select_reduce_fusion.1.weight_ref, f32[1,4,2,256,256]{4,3,2,1,0:T(8,128)} %mix_first.1.refs_0_, f32[2,256,256]{2,1,0:T(8,128)} %copy-done.3, f32[2,256,256]{2,1,0:T(8,128)} %copy-done.6, f32[2,256,256]{2,1,0:T(8,128)} %copy-done.11, f32[2,256,256]{2,1,0:T(8,128)} %copy-done.12, ...), custom_call_target="tpu_custom_call" | custom-call | tf_op jit(solution)/shard_map/mix_more/pallas_call | solution.py:226
  157.2 4.9 %mix_more.3 = f32[1,4,2,256,256]{4,3,2,1,0:T(8,128)} custom-call(f32[4,4]{1,0:T(4,128)} %select_reduce_fusion.2.weight_ref, f32[1,4,2,256,256]{4,3,2,1,0:T(8,128)} %mix_more.2.refs_0_, f32[2,256,256]{2,1,0:T(8,128)} %collective-permute-done.28.refs_1_, f32[2,256,256]{2,1,0:T(8,128)} %collective-permute-done.29.refs_2_, ...), custom_call_target="tpu_custom_call" | custom-call | tf_op jit(solution)/shard_map/mix_more/pallas_call | solution.py:226
  (94 shorter events, 14.0 us)
Async XLA Ops:
  5.5 10.3 %collective-permute-start.3 = (f32[256,256]{1,0:T(8,128)}, f32[256,256]{1,0:T(8,128)S(1)}, u32[]{:S(2)}, u32[]{:S(2)}) collective-permute-start(f32[256,256]{1,0:T(8,128)} %get-tuple-element.20), channel_id=1, source_target_pairs={{0,8},{1,9},{2,10},{3,11},{4,12},{5,13},{6,14},{7,15},{8,0},{9,1},... | collective-permute-start | bytes 786440 | tf_op jit(solution)/shard_map/ppermute | solution.py:274
  8.5 36.7 %collective-permute-start = (f32[2,256,256]{2,1,0:T(8,128)}, f32[2,256,256]{2,1,0:T(8,128)S(1)}, u32[]{:S(2)}, u32[]{:S(2)}) collective-permute-start(f32[2,256,256]{2,1,0:T(8,128)} %get-tuple-element.16), channel_id=1, source_target_pairs={{0,8},{1,9},{2,10},{3,11},{4,12},{5,13},{6,14},{7,15},{8,0},{9,1},... | collective-permute-start | bytes 1572872 | tf_op jit(solution)/shard_map/ppermute | solution.py:274
  8.5 36.7 %collective-permute-start.1 = (f32[2,256,256]{2,1,0:T(8,128)}, f32[2,256,256]{2,1,0:T(8,128)S(1)}, u32[]{:S(2)}, u32[]{:S(2)}) collective-permute-start(f32[2,256,256]{2,1,0:T(8,128)} %get-tuple-element.17), channel_id=1, source_target_pairs={{0,16},{1,17},{2,18},{3,19},{4,20},{5,21},{6,22},{7,23},{8,24},{9,... | collective-permute-start | bytes 1572872 | tf_op jit(solution)/shard_map/ppermute | solution.py:274
  10.5 34.7 %collective-permute-start.2 = (f32[2,256,256]{2,1,0:T(8,128)}, f32[2,256,256]{2,1,0:T(8,128)S(1)}, u32[]{:S(2)}, u32[]{:S(2)}) collective-permute-start(f32[2,256,256]{2,1,0:T(8,128)} %get-tuple-element.18), channel_id=1, source_target_pairs={{0,24},{1,25},{2,26},{3,27},{4,28},{5,29},{6,30},{7,31},{8,16},{9,... | collective-permute-start | bytes 1572872 | tf_op jit(solution)/shard_map/ppermute | solution.py:274
  12.0 32.6 %collective-permute-start.4 = (f32[256,256]{1,0:T(8,128)}, f32[256,256]{1,0:T(8,128)S(1)}, u32[]{:S(2)}, u32[]{:S(2)}) collective-permute-start(f32[256,256]{1,0:T(8,128)} %get-tuple-element.20), channel_id=1, source_target_pairs={{0,16},{1,17},{2,18},{3,19},{4,20},{5,21},{6,22},{7,23},{8,24},{9,... | collective-permute-start | bytes 786440 | tf_op jit(solution)/shard_map/ppermute | solution.py:274
  15.8 28.8 %collective-permute-start.5 = (f32[256,256]{1,0:T(8,128)}, f32[256,256]{1,0:T(8,128)S(1)}, u32[]{:S(2)}, u32[]{:S(2)}) collective-permute-start(f32[256,256]{1,0:T(8,128)} %get-tuple-element.20), channel_id=1, source_target_pairs={{0,24},{1,25},{2,26},{3,27},{4,28},{5,29},{6,30},{7,31},{8,16},{9,... | collective-permute-start | bytes 786440 | tf_op jit(solution)/shard_map/ppermute | solution.py:274
  44.6 6.4 %collective-permute-start.6 = (f32[256,256]{1,0:T(8,128)S(1)}, f32[256,256]{1,0:T(8,128)S(1)}, u32[]{:S(2)}, u32[]{:S(2)}) collective-permute-start(f32[256,256]{1,0:T(8,128)S(1)} %collective-permute-done.3.refs_5_), channel_id=1, source_target_pairs={{0,1},{1,0},{2,3},{3,2},{4,5},{5,4},{6,7},{7,6},{8,9},{9,8},{10,11... | collective-permute-start | bytes 786440 | tf_op jit(solution)/shard_map/ppermute | solution.py:274
  44.6 6.4 %collective-permute-start.7 = (f32[256,256]{1,0:T(8,128)S(1)}, f32[256,256]{1,0:T(8,128)S(1)}, u32[]{:S(2)}, u32[]{:S(2)}) collective-permute-start(f32[256,256]{1,0:T(8,128)S(1)} %collective-permute-done.4.refs_6_), channel_id=1, source_target_pairs={{0,1},{1,0},{2,3},{3,2},{4,5},{5,4},{6,7},{7,6},{8,9},{9,8},{10,11... | collective-permute-start | bytes 786440 | tf_op jit(solution)/shard_map/ppermute | solution.py:274
  45.1 6.0 %collective-permute-start.8 = (f32[256,256]{1,0:T(8,128)S(1)}, f32[256,256]{1,0:T(8,128)S(1)}, u32[]{:S(2)}, u32[]{:S(2)}) collective-permute-start(f32[256,256]{1,0:T(8,128)S(1)} %collective-permute-done.5.refs_7_), channel_id=1, source_target_pairs={{0,1},{1,0},{2,3},{3,2},{4,5},{5,4},{6,7},{7,6},{8,9},{9,8},{10,11... | collective-permute-start | bytes 786440 | tf_op jit(solution)/shard_map/ppermute | solution.py:274
  65.8 4.6 %collective-permute-start.9 = (f32[2,256,256]{2,1,0:T(8,128)}, f32[2,256,256]{2,1,0:T(8,128)S(1)}, u32[]{:S(2)}, u32[]{:S(2)}) collective-permute-start(f32[2,256,256]{2,1,0:T(8,128)} %get-tuple-element.21.refs_0_), channel_id=1, source_target_pairs={{0,1},{1,0},{2,3},{3,2},{4,5},{5,4},{6,7},{7,6},{8,9},{9,8},{10,11... | collective-permute-start | bytes 1572872 | tf_op jit(solution)/shard_map/ppermute | solution.py:274
  66.2 15.0 %collective-permute-start.10 = (f32[2,256,256]{2,1,0:T(8,128)}, f32[2,256,256]{2,1,0:T(8,128)S(1)}, u32[]{:S(2)}, u32[]{:S(2)}) collective-permute-start(f32[2,256,256]{2,1,0:T(8,128)} %get-tuple-element.22), channel_id=1, source_target_pairs={{0,8},{1,9},{2,10},{3,11},{4,12},{5,13},{6,14},{7,15},{8,0},{9,1},... | collective-permute-start | bytes 1572872 | tf_op jit(solution)/shard_map/ppermute | solution.py:274
  67.9 25.2 %collective-permute-start.12 = (f32[2,256,256]{2,1,0:T(8,128)}, f32[2,256,256]{2,1,0:T(8,128)S(1)}, u32[]{:S(2)}, u32[]{:S(2)}) collective-permute-start(f32[2,256,256]{2,1,0:T(8,128)} %get-tuple-element.23), channel_id=1, source_target_pairs={{0,16},{1,17},{2,18},{3,19},{4,20},{5,21},{6,22},{7,23},{8,24},{9,... | collective-permute-start | bytes 1572872 | tf_op jit(solution)/shard_map/ppermute | solution.py:274
  69.4 23.7 %collective-permute-start.14 = (f32[2,256,256]{2,1,0:T(8,128)}, f32[2,256,256]{2,1,0:T(8,128)S(1)}, u32[]{:S(2)}, u32[]{:S(2)}) collective-permute-start(f32[2,256,256]{2,1,0:T(8,128)} %get-tuple-element.24), channel_id=1, source_target_pairs={{0,24},{1,25},{2,26},{3,27},{4,28},{5,29},{6,30},{7,31},{8,16},{9,... | collective-permute-start | bytes 1572872 | tf_op jit(solution)/shard_map/ppermute | solution.py:274
  69.7 23.9 %collective-permute-start.16 = (f32[2,256,256]{2,1,0:T(8,128)}, f32[2,256,256]{2,1,0:T(8,128)S(1)}, u32[]{:S(2)}, u32[]{:S(2)}) collective-permute-start(f32[2,256,256]{2,1,0:T(8,128)} %get-tuple-element.21.refs_0_), channel_id=1, source_target_pairs={{1,3},{3,5},{5,7},{8,10},{9,11},{10,12},{11,13},{12,14},{13,15},{1... | collective-permute-start | bytes 1572872 | tf_op jit(solution)/shard_map/ppermute | solution.py:274
  70.4 24.5 %collective-permute-start.17 = (f32[2,256,256]{2,1,0:T(8,128)}, f32[2,256,256]{2,1,0:T(8,128)S(1)}, u32[]{:S(2)}, u32[]{:S(2)}) collective-permute-start(f32[2,256,256]{2,1,0:T(8,128)} %get-tuple-element.21.refs_0_), channel_id=1, source_target_pairs={{2,0},{3,1},{4,2},{5,3},{6,4},{7,5},{10,8},{11,9},{12,10},{13,11},... | collective-permute-start | bytes 1572872 | tf_op jit(solution)/shard_map/ppermute | solution.py:274
  81.2 16.8 %collective-permute-start.11 = (f32[2,256,256]{2,1,0:T(8,128)S(1)}, f32[2,256,256]{2,1,0:T(8,128)S(1)}, u32[]{:S(2)}, u32[]{:S(2)}) collective-permute-start(f32[2,256,256]{2,1,0:T(8,128)S(1)} %collective-permute-done.10.refs_2_), channel_id=1, source_target_pairs={{0,1},{1,0},{2,3},{3,2},{4,5},{5,4},{6,7},{7,6},{8,9},{9,8},{10,11... | collective-permute-start | bytes 1572872 | tf_op jit(solution)/shard_map/ppermute | solution.py:274
  93.1 9.2 %collective-permute-start.13 = (f32[2,256,256]{2,1,0:T(8,128)S(1)}, f32[2,256,256]{2,1,0:T(8,128)S(1)}, u32[]{:S(2)}, u32[]{:S(2)}) collective-permute-start(f32[2,256,256]{2,1,0:T(8,128)S(1)} %collective-permute-done.12.refs_4_), channel_id=1, source_target_pairs={{0,1},{1,0},{2,3},{3,2},{4,5},{5,4},{6,7},{7,6},{8,9},{9,8},{10,11... | collective-permute-start | bytes 1572872 | tf_op jit(solution)/shard_map/ppermute | solution.py:274
  93.1 10.5 %collective-permute-start.15 = (f32[2,256,256]{2,1,0:T(8,128)S(1)}, f32[2,256,256]{2,1,0:T(8,128)S(1)}, u32[]{:S(2)}, u32[]{:S(2)}) collective-permute-start(f32[2,256,256]{2,1,0:T(8,128)S(1)} %collective-permute-done.14.refs_6_), channel_id=1, source_target_pairs={{0,1},{1,0},{2,3},{3,2},{4,5},{5,4},{6,7},{7,6},{8,9},{9,8},{10,11... | collective-permute-start | bytes 1572872 | tf_op jit(solution)/shard_map/ppermute | solution.py:274
  93.6 15.4 %collective-permute-start.18 = (f32[2,256,256]{2,1,0:T(8,128)S(1)}, f32[2,256,256]{2,1,0:T(8,128)S(1)}, u32[]{:S(2)}, u32[]{:S(2)}) collective-permute-start(f32[2,256,256]{2,1,0:T(8,128)S(1)} %collective-permute-done.16.refs_1_), channel_id=1, source_target_pairs={{1,0},{3,2},{5,4},{7,6},{9,8},{11,10},{13,12},{15,14},{17,16},{19,... | collective-permute-start | bytes 1572872 | tf_op jit(solution)/shard_map/ppermute | solution.py:274
  94.9 15.4 %collective-permute-start.19 = (f32[2,256,256]{2,1,0:T(8,128)S(1)}, f32[2,256,256]{2,1,0:T(8,128)S(1)}, u32[]{:S(2)}, u32[]{:S(2)}) collective-permute-start(f32[2,256,256]{2,1,0:T(8,128)S(1)} %collective-permute-done.17.refs_2_), channel_id=1, source_target_pairs={{0,1},{2,3},{4,5},{6,7},{8,9},{10,11},{12,13},{14,15},{16,17},{18,... | collective-permute-start | bytes 1572872 | tf_op jit(solution)/shard_map/ppermute | solution.py:274
  98.1 17.7 %collective-permute-start.20 = (f32[2,256,256]{2,1,0:T(8,128)S(1)}, f32[2,256,256]{2,1,0:T(8,128)}, u32[]{:S(2)}, u32[]{:S(2)}) collective-permute-start(f32[2,256,256]{2,1,0:T(8,128)S(1)} %collective-permute-done.10.refs_2_), channel_id=1, source_target_pairs={{0,2},{1,3},{2,4},{3,5},{4,6},{5,7},{9,11},{11,13},{13,15},{16,18}... | collective-permute-start | bytes 1572872 | tf_op jit(solution)/shard_map/ppermute | solution.py:274
  102.4 16.7 %collective-permute-start.21 = (f32[2,256,256]{2,1,0:T(8,128)S(1)}, f32[2,256,256]{2,1,0:T(8,128)S(1)}, u32[]{:S(2)}, u32[]{:S(2)}) collective-permute-start(f32[2,256,256]{2,1,0:T(8,128)S(1)} %collective-permute-done.10.refs_2_), channel_id=1, source_target_pairs={{2,0},{3,1},{4,2},{5,3},{6,4},{7,5},{10,8},{11,9},{12,10},{13,11},... | collective-permute-start | bytes 1572872 | tf_op jit(solution)/shard_map/ppermute | solution.py:274
  103.7 21.4 %collective-permute-start.24 = (f32[2,256,256]{2,1,0:T(8,128)S(1)}, f32[2,256,256]{2,1,0:T(8,128)}, u32[]{:S(2)}, u32[]{:S(2)}) collective-permute-start(f32[2,256,256]{2,1,0:T(8,128)S(1)} %collective-permute-done.12.refs_4_), channel_id=1, source_target_pairs={{0,2},{1,3},{2,4},{3,5},{4,6},{5,7},{8,10},{9,11},{10,12},{11,13},... | collective-permute-start | bytes 1572872 | tf_op jit(solution)/shard_map/ppermute | solution.py:274
  109.0 19.4 %collective-permute-start.25 = (f32[2,256,256]{2,1,0:T(8,128)S(1)}, f32[2,256,256]{2,1,0:T(8,128)}, u32[]{:S(2)}, u32[]{:S(2)}) collective-permute-start(f32[2,256,256]{2,1,0:T(8,128)S(1)} %collective-permute-done.12.refs_4_), channel_id=1, source_target_pairs={{2,0},{3,1},{4,2},{5,3},{6,4},{7,5},{10,8},{12,10},{14,12},{18,16}... | collective-permute-start | bytes 1572872 | tf_op jit(solution)/shard_map/ppermute | solution.py:274
  110.4 24.4 %collective-permute-start.28 = (f32[2,256,256]{2,1,0:T(8,128)S(1)}, f32[2,256,256]{2,1,0:T(8,128)}, u32[]{:S(2)}, u32[]{:S(2)}) collective-permute-start(f32[2,256,256]{2,1,0:T(8,128)S(1)} %collective-permute-done.14.refs_6_), channel_id=1, source_target_pairs={{0,2},{1,3},{2,4},{3,5},{4,6},{5,7},{8,10},{9,11},{10,12},{11,13},... | collective-permute-start | bytes 1572872 | tf_op jit(solution)/shard_map/ppermute | solution.py:274
  115.7 21.1 %collective-permute-start.29 = (f32[2,256,256]{2,1,0:T(8,128)S(1)}, f32[2,256,256]{2,1,0:T(8,128)}, u32[]{:S(2)}, u32[]{:S(2)}) collective-permute-start(f32[2,256,256]{2,1,0:T(8,128)S(1)} %collective-permute-done.14.refs_6_), channel_id=1, source_target_pairs={{2,0},{4,2},{6,4},{10,8},{11,9},{12,10},{13,11},{14,12},{15,13},{1... | collective-permute-start | bytes 1572872 | tf_op jit(solution)/shard_map/ppermute | solution.py:274
  119.9 18.2 %collective-permute-start.22 = (f32[2,256,256]{2,1,0:T(8,128)}, f32[2,256,256]{2,1,0:T(8,128)}, u32[]{:S(2)}, u32[]{:S(2)}) collective-permute-start(f32[2,256,256]{2,1,0:T(8,128)} %collective-permute-done.20.refs_5_), channel_id=1, source_target_pairs={{1,0},{3,2},{5,4},{7,6},{9,8},{11,10},{13,12},{15,14},{17,16},{19,... | collective-permute-start | bytes 1572872 | tf_op jit(solution)/shard_map/ppermute | solution.py:274
  125.1 25.3 %collective-permute-start.23 = (f32[2,256,256]{2,1,0:T(8,128)}, f32[2,256,256]{2,1,0:T(8,128)}, u32[]{:S(2)}, u32[]{:S(2)}) collective-permute-start(f32[2,256,256]{2,1,0:T(8,128)} %copy-done.14), channel_id=1, source_target_pairs={{0,1},{2,3},{4,5},{6,7},{8,9},{10,11},{12,13},{14,15},{16,17},{18,... | collective-permute-start | bytes 1572872 | tf_op jit(solution)/shard_map/ppermute | solution.py:274
  128.5 21.9 %collective-permute-start.26 = (f32[2,256,256]{2,1,0:T(8,128)}, f32[2,256,256]{2,1,0:T(8,128)}, u32[]{:S(2)}, u32[]{:S(2)}) collective-permute-start(f32[2,256,256]{2,1,0:T(8,128)} %collective-permute-done.24.refs_9_), channel_id=1, source_target_pairs={{1,0},{3,2},{5,4},{7,6},{9,8},{11,10},{13,12},{15,14},{17,16},{19,... | collective-permute-start | bytes 1572872 | tf_op jit(solution)/shard_map/ppermute | solution.py:274
  134.7 15.7 %collective-permute-start.27 = (f32[2,256,256]{2,1,0:T(8,128)}, f32[2,256,256]{2,1,0:T(8,128)}, u32[]{:S(2)}, u32[]{:S(2)}) collective-permute-start(f32[2,256,256]{2,1,0:T(8,128)} %collective-permute-done.25.refs_10_), channel_id=1, source_target_pairs={{0,1},{2,3},{4,5},{6,7},{8,9},{10,11},{12,13},{14,15},{16,17},{18,... | collective-permute-start | bytes 1572872 | tf_op jit(solution)/shard_map/ppermute | solution.py:274
  136.8 20.4 %collective-permute-start.30 = (f32[2,256,256]{2,1,0:T(8,128)}, f32[2,256,256]{2,1,0:T(8,128)}, u32[]{:S(2)}, u32[]{:S(2)}) collective-permute-start(f32[2,256,256]{2,1,0:T(8,128)} %collective-permute-done.28.refs_1_), channel_id=1, source_target_pairs={{1,0},{3,2},{5,4},{7,6},{9,8},{11,10},{13,12},{15,14},{17,16},{19,... | collective-permute-start | bytes 1572872 | tf_op jit(solution)/shard_map/ppermute | solution.py:274
  138.1 19.1 %collective-permute-start.31 = (f32[2,256,256]{2,1,0:T(8,128)}, f32[2,256,256]{2,1,0:T(8,128)}, u32[]{:S(2)}, u32[]{:S(2)}) collective-permute-start(f32[2,256,256]{2,1,0:T(8,128)} %collective-permute-done.29.refs_2_), channel_id=1, source_target_pairs={{0,1},{2,3},{4,5},{6,7},{8,9},{10,11},{12,13},{14,15},{16,17},{18,... | collective-permute-start | bytes 1572872 | tf_op jit(solution)/shard_map/ppermute | solution.py:274
  (23 other events, 661.8 us)

commit v2 on v0

v2 whole, which is shorter than its diff:
```python
import functools

import jax
import jax.numpy as jnp
from jax import lax
from jax.experimental import pallas as pl
from jax.experimental.pallas import tpu as pltpu
from jax.sharding import PartitionSpec as P


NS_ITERS = 3
REACH = 7

AXES = ("layer", "energy")
F32 = jnp.float32
BF16 = jnp.bfloat16
HBM = pltpu.HBM
VMEM = pltpu.VMEM


def split(x):
    high = x.astype(BF16)
    low = (x - high.astype(F32)).astype(BF16)
    return high, low


def dot(a, b, transposed):
    dims = (((1,), (1 if transposed else 0,)), ((), ()))
    return lax.dot_general(a, b, dims, preferred_element_type=F32)


def dot3(a, b, transposed=False):
    return (
        dot(a[0], b[0], transposed) + dot(a[0], b[1], transposed) + dot(a[1], b[0], transposed)
    )


def negated(a):
    return (-a[0], -a[1])


def product(a, b):
    real = dot3(a[0], b[0]) + dot3(negated(a[1]), b[1])
    imag = dot3(a[0], b[1]) + dot3(a[1], b[0])
    return real, imag


def product_adjoint(a, c):
    real = dot3(a[0], c[0], True) + dot3(a[1], c[1], True)
    imag = dot3(a[1], c[0], True) + dot3(negated(a[0]), c[1], True)
    return real, imag


def split_pair(pair):
    return split(pair[0]), split(pair[1])


def eye_mask(n):
    return lax.broadcasted_iota(jnp.int32, (n, n), 0) == lax.broadcasted_iota(
        jnp.int32, (n, n), 1
    )


def inverse_of(real, imag):
    n = real.shape[0]
    eye = eye_mask(n)
    zero = jnp.zeros_like(real)
    diag_real = jnp.where(eye, real, zero)
    diag_imag = jnp.where(eye, imag, zero)

    def reciprocal(axis):
        dr = jnp.sum(diag_real, axis=axis, keepdims=True)
        di = jnp.sum(diag_imag, axis=axis, keepdims=True)
        modulus = dr * dr + di * di
        return dr / modulus, -di / modulus

    row_r, row_i = reciprocal(0)
    col_r, col_i = reciprocal(1)
    e_r = jnp.where(eye, zero, real * -row_r + imag * row_i)
    e_i = jnp.where(eye, zero, real * -row_i - imag * row_r)
    unit = jnp.where(eye, 1.0, 0.0).astype(F32)
    f_r, f_i = unit + e_r, e_i
    for _ in range(NS_ITERS - 1):
        es = split_pair((e_r, e_i))
        e_r, e_i = product(es, es)
        es = split_pair((e_r, e_i))
        g_r, g_i = product(split_pair((f_r, f_i)), es)
        f_r, f_i = f_r + g_r, f_i + g_i
    return col_r * f_r - col_i * f_i, col_r * f_i + col_i * f_r


def prep_kernel(
    coup_hbm, mask_hbm, ham_hbm, onsite_hbm, broad_hbm, prior_hbm, masked_ref, quarter_ref, *refs
):
    base_refs = refs[:-7]
    coup_ref, mask_ref, ham_ref, onsite_ref, broad_ref, prior_ref, sems = refs[-7:]
    sources = (coup_hbm, mask_hbm, ham_hbm, onsite_hbm, broad_hbm, prior_hbm)
    targets = (coup_ref, mask_ref, ham_ref, onsite_ref, broad_ref, prior_ref)
    copies = [
        pltpu.make_async_copy(source, target, sems.at[i])
        for i, (source, target) in enumerate(zip(sources, targets))
    ]
    for copy in copies:
        copy.start()
    per_device = prior_ref.shape[1]
    layer = lax.axis_index("layer")
    group = lax.axis_index("energy")
    plane, half = group % 2, (group // 2) % 2
    rows = quarter_ref.shape[0]
    for copy in copies[:2]:
        copy.wait()
    mask = mask_ref[0].astype(F32)
    c_r, c_i = coup_ref[0, 0] * mask, coup_ref[0, 1] * mask
    masked_ref[0], masked_ref[1] = c_r, c_i
    here = pl.ds(pl.multiple_of(half * rows, rows), rows)
    quarter_ref[...] = masked_ref[plane, here, :]
    cs = split_pair((c_r, c_i))
    q_r, q_i = product_adjoint(cs, cs)
    for copy in copies[2:5]:
        copy.wait()
    first = group * per_device
    grid_size = per_device * lax.axis_size("energy")
    n = ham_ref.shape[-1]
    h_r, h_i = ham_ref[0, 0], ham_ref[0, 1]
    eye = eye_mask(n)
    own = jnp.where(layer == 0, 0.5, 0.0).astype(F32)
    fixed_r = -0.5 * (h_r + h_r.T) - own * q_i + jnp.where(eye, -onsite_ref[...], 0.0)
    fixed_i = -0.5 * (h_i - h_i.T) + own * q_r + jnp.where(eye, broad_ref[...], 0.0)
    copies[5].wait()
    for k, base_ref in enumerate(base_refs):
        mine = jnp.bitwise_xor(layer, k)
        level = -1.0 + 2.0 * ((first + mine).astype(F32) + 0.5) / grid_size
        base_ref[0] = fixed_r - prior_ref[0, mine, 0] + jnp.where(eye, level, 0.0)
        base_ref[1] = fixed_i - prior_ref[0, mine, 1]


def stack_kernel(*refs):
    out_ref = refs[-1]
    for k, ref in enumerate(refs[:-1]):
        out_ref[k] = ref[...]


def join_kernel(near_ref, far_ref, out_ref):
    half = (lax.axis_index("energy") // 2) % 2
    rows = near_ref.shape[1]
    for side, ref in ((half, near_ref), (1 - half, far_ref)):
        out_ref[:, pl.ds(pl.multiple_of(side * rows, rows), rows), :] = ref[...]


def solve_kernel(layer_count, *refs):
    base_refs = refs[:layer_count]
    masked_ref, same_ref, other_ref = refs[layer_count : layer_count + 3]
    out_refs = refs[layer_count + 3 : 2 * layer_count + 3]
    system, coup, green = refs[2 * layer_count + 3 :]
    layer = lax.axis_index("layer")
    core = lax.axis_index("energy") % 2

    def step(l, carry):
        source = jnp.bitwise_xor(layer, l)
        for k in range(layer_count):
            @pl.when(source == k)
            def _(k=k):
                system[...] = base_refs[k][...]
                if k == 0:
                    coup[...] = masked_ref[...]
                else:
                    coup[core] = same_ref[k - 1]
                    coup[1 - core] = other_ref[k - 1]

        @pl.when(l > 0)
        def _():
            cs = split_pair((coup[0], coup[1]))
            moved = product(cs, split_pair((green[0], green[1])))
            contact_r, contact_i = product_adjoint(split_pair(moved), cs)
            system[0] -= contact_r
            system[1] -= contact_i

        g_r, g_i = inverse_of(system[0], system[1])
        green[0], green[1] = g_r, g_i
        for k in range(layer_count):
            @pl.when(source == k)
            def _(k=k):
                out_refs[k][0], out_refs[k][1] = g_r, g_i
        return carry

    lax.fori_loop(0, layer_count, step, 0)


STEP_ROWS = 16


def weight_kernel(value_ref, offset_ref, out_ref):
    layer = lax.axis_index("layer")
    group = lax.axis_index("energy")
    layer_count = lax.axis_size("layer")
    per_device = layer_count
    span = 2 * per_device
    core = group % 2
    shape = out_ref.shape
    row = lax.broadcasted_iota(jnp.int32, shape, 0)
    lane = lax.broadcasted_iota(jnp.int32, shape, 1)
    kind = lane // layer_count
    away = 2 * core - 1
    shift = jnp.where(kind == INNER, -away, jnp.where(kind == CROSSED, away, 0))
    shift = jnp.where(kind == OUTER, away, shift)
    far_core = jnp.where((kind == THEIRS) | (kind == CROSSED), 1 - core, core)
    source = jnp.bitwise_xor(lane % layer_count, layer)
    gap = span * shift + per_device * far_core + source - (per_device * core + row)
    total = jnp.zeros(shape, F32)
    for tap in range(value_ref.shape[0]):
        total += jnp.where(gap == offset_ref[tap], value_ref[tap], 0.0)
    out_ref[...] = total


MINE, THEIRS, INNER, CROSSED, OUTER = range(5)


def mix_rows(weight_ref, slots, acc, refs, outputs, part, start):
    here = pl.ds(pl.multiple_of(start, STEP_ROWS), STEP_ROWS)
    total = [None] * outputs if acc is None else [acc[0, f, part, here, :] for f in range(outputs)]
    for slot, ref in zip(slots, refs):
        x = ref[part, here, :]
        for f in range(outputs):
            term = weight_ref[f, slot] * x
            total[f] = term if total[f] is None else total[f] + term
    return here, total


def mix_kernel(slots, has_acc, weight_ref, *refs):
    refs = list(refs)
    out_ref = refs.pop()
    acc_ref = refs.pop(0) if has_acc else None
    outputs, parts, rows, _ = out_ref.shape[1:]
    for part in range(parts):
        def body(i, carry, part=part):
            here, total = mix_rows(
                weight_ref, slots, acc_ref, refs, outputs, part, i * STEP_ROWS
            )
            for f in range(outputs):
                out_ref[0, f, part, here, :] = total[f]
            return carry

        lax.fori_loop(0, rows // STEP_ROWS, body, 0, unroll=2)


def last_kernel(slots, weight_ref, *refs):
    acc_ref, blocks, out_ref, buffer, sems = refs[0], refs[1:-3], refs[-3], refs[-2], refs[-1]
    outputs, parts, rows, _ = out_ref.shape[1:]
    pieces = 2
    size = rows // pieces
    copies = []
    for part in range(parts):
        for piece in range(pieces):
            def body(i, carry, part=part, base=piece * size):
                here, total = mix_rows(
                    weight_ref, slots, acc_ref, blocks, outputs, part, base + i * STEP_ROWS
                )
                for f in range(outputs):
                    buffer[0, f, part, here, :] = total[f]
                return carry

            lax.fori_loop(0, size // STEP_ROWS, body, 0, unroll=2)
            here = (slice(None), slice(None), part, pl.ds(piece * size, size))
            copy = pltpu.make_async_copy(buffer.at[here], out_ref.at[here], sems.at[part, piece])
            copy.start()
            copies.append(copy)
    for copy in copies:
        copy.wait()


SMEM_SPEC = pl.BlockSpec(memory_space=pltpu.SMEM)
VMEM_SPEC = pl.BlockSpec(memory_space=VMEM)
HBM_SPEC = pl.BlockSpec(memory_space=HBM)


def run(kernel, arrays, out_shape, head=(), scratch=(), space=VMEM, **more):
    arrays = [pltpu.with_memory_space_constraint(x, space) for x in arrays]
    return pl.pallas_call(
        kernel,
        in_specs=[SMEM_SPEC] * len(head) + [pl.BlockSpec(memory_space=space)] * len(arrays),
        out_shape=out_shape,
        scratch_shapes=list(scratch),
        compiler_params=pltpu.CompilerParams(vmem_limit_bytes=24 * 2**20),
        **({"out_specs": jax.tree.map(lambda _: VMEM_SPEC, out_shape)} | more),
    )(*head, *arrays)


def sweep(
    onsite, broadening, hamiltonian, coupling, coupling_mask, prior_sigma,
    kernel_weights, kernel_offsets,
):
    layer_count = lax.axis_size("layer")
    group_count = lax.axis_size("energy")
    per_device = prior_sigma.shape[1]
    n = prior_sigma.shape[-1]
    span = 2 * per_device
    assert per_device == layer_count and layer_count & (layer_count - 1) == 0
    assert group_count % 4 == 0 and span > REACH
    ks = range(1, layer_count)

    everyone = [(l, g) for l in range(layer_count) for g in range(group_count)]

    def move(x, target, wanted=lambda l, g: True):
        pairs = []
        for l, g in everyone:
            tl, tg = target(l, g)
            if wanted(l, g) and 0 <= tg < group_count:
                pairs.append((l * group_count + g, tl * group_count + tg))
        return lax.ppermute(x, AXES, pairs)

    def to_layer(x, k):
        return move(x, lambda l, g: (l ^ k, g))

    def swapped(x):
        return move(x, lambda l, g: (l, g ^ 1))

    block = VMEM((2, n, n), F32)
    inputs = [coupling, coupling_mask, hamiltonian, onsite, broadening, prior_sigma]
    masked, quarter, *bases = run(
        prep_kernel, inputs, [block, VMEM((n // 2, n), F32)] + [block] * layer_count,
        scratch=[VMEM(x.shape, x.dtype) for x in inputs]
        + [pltpu.SemaphoreType.DMA((len(inputs),))],
        space=HBM,
    )
    quarters = [to_layer(quarter, k) for k in ks]
    bases = [bases[0]] + [to_layer(bases[k], k) for k in ks]
    weights = run(
        weight_kernel, [], VMEM((8 * -(-per_device // 8), 128), F32),
        [kernel_weights, kernel_offsets],
    )
    near = run(stack_kernel, quarters, VMEM((len(ks), n // 2, n), F32))
    far = move(near, lambda l, g: (l, g ^ 2))
    same = run(join_kernel, [near, far], VMEM((len(ks), n, n), F32))
    other = swapped(same)
    greens = run(
        functools.partial(solve_kernel, layer_count),
        [*bases, masked, same, other], [block] * layer_count, scratch=[block] * 3,
    )

    mine = [greens[0]] + [to_layer(greens[k], k) for k in ks]

    def reached(l, g, k, step):
        spot = per_device * (g % 2) + (l ^ k)
        return (span - spot if step > 0 else spot + 1) <= REACH

    inner, outer, theirs, crossed = [], [], [], []
    for k in range(layer_count):
        def beyond(sign, k=k):
            step = lambda g: sign * (4 * (g % 2) - 2)
            return move(
                mine[k], lambda l, g: (l, g + step(g)),
                lambda l, g: reached(l, g, k, step(g)),
            )

        inner.append(beyond(1))
        outer.append(beyond(-1))
        theirs.append(swapped(mine[k]))
        crossed.append(swapped(inner[k]))

    shape = (1, per_device, 2, n, n)
    kinds = {MINE: mine, THEIRS: theirs, INNER: inner, CROSSED: crossed, OUTER: outer}

    def mixed(acc, entries, name):
        slots = tuple(kind * layer_count + k for kind, k in entries)
        blocks = [kinds[kind][k] for kind, k in entries]
        if name == "mix_last":
            return run(
                functools.partial(last_kernel, slots), [acc] + blocks,
                jax.ShapeDtypeStruct(shape, F32), [weights],
                [VMEM(shape, F32), pltpu.SemaphoreType.DMA((2, 2))], out_specs=HBM_SPEC,
            )
        kernel = functools.partial(mix_kernel, slots, acc is not None)
        return run(kernel, ([] if acc is None else [acc]) + blocks, VMEM(shape, F32), [weights])

    final = layer_count - 1
    acc = mixed(None, [(MINE, 0)], "mix_own")
    for k in ks[:-1]:
        acc = mixed(acc, [(MINE, k), (THEIRS, k - 1)], f"mix_next{k}")
    acc = mixed(acc, [(MINE, final), (THEIRS, final - 1), (THEIRS, final)], "mix_near")
    outside = (INNER, CROSSED, OUTER)
    acc = mixed(acc, [(kind, k) for kind in outside for k in range(final)], "mix_far")
    return mixed(acc, [(kind, final) for kind in outside], "mix_last")


def solution(mesh):
    placed = (
        P("layer", None),
        P("layer", None),
        P("layer", None, None, None),
        P("layer", None, None, None),
        P("layer", None, None),
        P("layer", "energy", None, None, None),
        P(),
        P(),
    )
    return jax.shard_map(
        sweep,
        mesh=mesh,
        in_specs=placed,
        out_specs=P("layer", "energy", None, None, None),
        check_vma=False,
    )
```

time: 358 us -> 132 us (0.37); the launches traced: 353 us -> 132 us
  blocking collectives: 90.2 us -> 0 us
  matrix products: 59.9 us -> 0 us
  waiting for transfers between devices: 114 us -> 71.3 us
  local copies, waits for them, and re-layouts: 41.3 us -> 0.01 us
  starting transfers between devices: 10.1 us -> 36.2 us
  Pallas kernels: 0 us -> 24 us
  other arithmetic: 22.2 us -> 0 us
  between operations: 15.2 us -> 0.25 us
    ppermute x0 -> x27, waiting for transfers between devices: none -> 71.3 us  [move(): return lax.ppermute(x, AXES, pairs)]
    all_gather x3 -> x0, waiting for transfers between devices: 62.6 us -> none  [the longest x1 32.1 us: local(): lax.all_gather(hamiltonian, 'layer', axis=0, tiled=True)]
    dot_general x129 -> x0, matrix products: 59.9 us -> none  [the longest x128 56.9 us: matmul_high(): return jnp.matmul(first_op, second_op, precision=exact_mode)]
    all_to_all x1 -> x0, blocking collectives: 51.5 us -> none  [local(): lax.all_to_all(blended, 'energy', split_axis=0, concat_axis=2, tiled=True)]
    all_to_all x2 -> x0, waiting for transfers between devices: 49.8 us -> none  [the longest x1 49.8 us: local(): lax.all_to_all(joined, ('layer', 'energy'), split_axis=2, concat_axis=0,...]
    all_gather x2 -> x0, blocking collectives: 38.8 us -> none  [the longest x1 30.2 us: local(): lax.all_gather(onsite, 'layer', axis=0, tiled=True)]
    ppermute x0 -> x27, starting transfers between devices: none -> 36.2 us  [move(): return lax.ppermute(x, AXES, pairs)]
    pallas_call x0 -> x11, Pallas kernels: none -> 24 us  [run(): pl.pallas_call(kernel, in_specs=[SMEM_SPEC] * len(head) + [pl.BlockSpec(m...]
  transfers between devices with their start and end apart: 5 -> 27, of which waited for: 3 -> 9; matrix products, arithmetic and copies ran while one was open for 6% -> 0% of each run, Pallas kernels for 0% -> 5%
where the time goes in v2:
time: 132 us
  waiting for transfers between devices  71.3 us (54%)
  starting transfers between devices  36.2 us (27%)
  Pallas kernels  24 us (18%)
    ppermute x27, waiting for transfers between devices, move(): return lax.ppermute(x, AXES, pairs)  71.3 us
    ppermute x27, starting transfers between devices, move(): return lax.ppermute(x, AXES, pairs)  36.2 us
    pallas_call x11, Pallas kernels, run(): pl.pallas_call(kernel, in_specs=[SMEM_SPEC] * len(head) + [pl.BlockSpec(m...  24 us
  transfers between devices with their start and end apart: 27, of which 9 were waited for; matrix products, arithmetic and copies ran while one was open for 0% of the time, Pallas kernels for 5%

profile of v2, /device:TPU:0, one launch (start us, length us, event | category | flops | bytes accessed | tf_op | source)
XLA Modules:
  0.0 131.8 jit_solution(18393855296861951684)
XLA Ops:
  0.0 2.3 %shard_map.83 = (f32[2,256,256]{2,1,0:T(8,128)S(1)}, f32[128,256]{1,0:T(8,128)S(1)}, f32[2,256,256]{2,1,0:T(8,128)S(1)}, f32[2,256,256]{2,1,0:T(8,128)S(1)}, f32...) custom-call(f32[1,2,256,256]{3,2,1,0:T(8,128)} %coup_hbm.1, s32[1,256,256]{2,1,0:T(8,128)} %mask_hbm.1, ...), custom_call_target="tpu_custom_call" | custom-call | tf_op jit(solution)/shard_map/pallas_call | solution.py:278
  2.3 3.0 %collective-permute-start.3 = (f32[128,256]{1,0:T(8,128)S(1)}, f32[128,256]{1,0:T(8,128)S(1)}, u32[]{:S(2)}, u32[]{:S(2)}) collective-permute-start(f32[128,256]{1,0:T(8,128)S(1)} %get-tuple-element.20), channel_id=1, source_target_pairs={{0,8},{1,9},{2,10},{3,11},{4,12},{5,13},{6,14},{7,15},{8,0},{9,1},... | collective-permute-start | bytes 393224 | tf_op jit(solution)/shard_map/ppermute | solution.py:309
  5.3 1.5 %collective-permute-start.4 = (f32[128,256]{1,0:T(8,128)S(1)}, f32[128,256]{1,0:T(8,128)S(1)}, u32[]{:S(2)}, u32[]{:S(2)}) collective-permute-start(f32[128,256]{1,0:T(8,128)S(1)} %get-tuple-element.20), channel_id=1, source_target_pairs={{0,16},{1,17},{2,18},{3,19},{4,20},{5,21},{6,22},{7,23},{8,24},{9,... | collective-permute-start | bytes 393224 | tf_op jit(solution)/shard_map/ppermute | solution.py:309
  6.9 2.3 %collective-permute-done.3.refs_0_ = f32[128,256]{1,0:T(8,128)S(1)} collective-permute-done((f32[128,256]{1,0:T(8,128)S(1)}, f32[128,256]{1,0:T(8,128)S(1)}, u32[]{:S(2)}, u32[]{:S(2)}) %collective-permute-start.3) | collective-permute-done | bytes 131104 | tf_op jit(solution)/shard_map/ppermute | solution.py:309
  9.2 3.9 %collective-permute-done.4.refs_1_ = f32[128,256]{1,0:T(8,128)S(1)} collective-permute-done((f32[128,256]{1,0:T(8,128)S(1)}, f32[128,256]{1,0:T(8,128)S(1)}, u32[]{:S(2)}, u32[]{:S(2)}) %collective-permute-start.4) | collective-permute-done | bytes 131104 | tf_op jit(solution)/shard_map/ppermute | solution.py:309
  13.1 1.6 %collective-permute-start.6 = (f32[3,128,256]{2,1,0:T(8,128)S(1)}, f32[3,128,256]{2,1,0:T(8,128)S(1)}, u32[]{:S(2)}, u32[]{:S(2)}) collective-permute-start(f32[3,128,256]{2,1,0:T(8,128)S(1)} %shard_map.84.near_ref), channel_id=1, source_target_pairs={{0,2},{1,3},{2,0},{3,1},{4,6},{5,7},{6,4},{7,5},{8,10},{9,11},{10,... | collective-permute-start | bytes 1179656 | tf_op jit(solution)/shard_map/ppermute | solution.py:309
  14.8 8.1 %collective-permute-done.6.far_ref = f32[3,128,256]{2,1,0:T(8,128)S(1)} collective-permute-done((f32[3,128,256]{2,1,0:T(8,128)S(1)}, f32[3,128,256]{2,1,0:T(8,128)S(1)}, u32[]{:S(2)}, u32[]{:S(2)}) %collective-permute-start.6) | collective-permute-done | bytes 393248 | tf_op jit(solution)/shard_map/ppermute | solution.py:309
  23.0 1.7 %collective-permute-start = (f32[2,256,256]{2,1,0:T(8,128)S(1)}, f32[2,256,256]{2,1,0:T(8,128)S(1)}, u32[]{:S(2)}, u32[]{:S(2)}) collective-permute-start(f32[2,256,256]{2,1,0:T(8,128)S(1)} %get-tuple-element.16), channel_id=1, source_target_pairs={{0,8},{1,9},{2,10},{3,11},{4,12},{5,13},{6,14},{7,15},{8,0},{9,1},... | collective-permute-start | bytes 1572872 | tf_op jit(solution)/shard_map/ppermute | solution.py:309
  25.2 1.4 %collective-permute-start.2 = (f32[2,256,256]{2,1,0:T(8,128)S(1)}, f32[2,256,256]{2,1,0:T(8,128)S(1)}, u32[]{:S(2)}, u32[]{:S(2)}) collective-permute-start(f32[2,256,256]{2,1,0:T(8,128)S(1)} %get-tuple-element.18), channel_id=1, source_target_pairs={{0,24},{1,25},{2,26},{3,27},{4,28},{5,29},{6,30},{7,31},{8,16},{9,... | collective-permute-start | bytes 1572872 | tf_op jit(solution)/shard_map/ppermute | solution.py:309
  26.5 11.3 %collective-permute-done.refs_1_ = f32[2,256,256]{2,1,0:T(8,128)S(1)} collective-permute-done((f32[2,256,256]{2,1,0:T(8,128)S(1)}, f32[2,256,256]{2,1,0:T(8,128)S(1)}, u32[]{:S(2)}, u32[]{:S(2)}) %collective-permute-start) | collective-permute-done | bytes 524320 | tf_op jit(solution)/shard_map/ppermute | solution.py:309
  37.9 12.0 %collective-permute-done.1.refs_2_ = f32[2,256,256]{2,1,0:T(8,128)S(1)} collective-permute-done((f32[2,256,256]{2,1,0:T(8,128)S(1)}, f32[2,256,256]{2,1,0:T(8,128)S(1)}, u32[]{:S(2)}, u32[]{:S(2)}) %collective-permute-start.1) | collective-permute-done | bytes 524320 | tf_op jit(solution)/shard_map/ppermute | solution.py:309
  49.9 12.7 %shard_map.86 = (f32[2,256,256]{2,1,0:T(8,128)S(1)}, f32[2,256,256]{2,1,0:T(8,128)S(1)}, f32[2,256,256]{2,1,0:T(8,128)S(1)}, f32[2,256,256]{2,1,0:T(8,128)S(1)}) custom-call(f32[2,256,256]{2,1,0:T(8,128)S(1)} %get-tuple-element.15.refs_0_, f32[2,256,256]{2,1,0:T(8,128)S(1)} %collective-permute-done.refs_1_, ...), custom_call_target="tpu_custom_call" | custom-call | tf_op jit(solution)/shard_map/pallas_call | solution.py:278
  63.1 1.8 %collective-permute-start.10 = (f32[2,256,256]{2,1,0:T(8,128)S(1)}, f32[2,256,256]{2,1,0:T(8,128)S(1)}, u32[]{:S(2)}, u32[]{:S(2)}) collective-permute-start(f32[2,256,256]{2,1,0:T(8,128)S(1)} %get-tuple-element.23), channel_id=1, source_target_pairs={{0,16},{1,17},{2,18},{3,19},{4,20},{5,21},{6,22},{7,23},{8,24},{9,... | collective-permute-start | bytes 1572872 | tf_op jit(solution)/shard_map/ppermute | solution.py:309
  64.9 1.3 collective-permute-start.12
  66.2 1.3 collective-permute-start.15
  67.5 10.0 %collective-permute-done.8.refs_1_ = f32[2,256,256]{2,1,0:T(8,128)S(1)} collective-permute-done((f32[2,256,256]{2,1,0:T(8,128)S(1)}, f32[2,256,256]{2,1,0:T(8,128)S(1)}, u32[]{:S(2)}, u32[]{:S(2)}) %collective-permute-start.8) | collective-permute-done | bytes 524320 | tf_op jit(solution)/shard_map/ppermute | solution.py:309
  78.3 10.4 %collective-permute-done.10.refs_1_ = f32[2,256,256]{2,1,0:T(8,128)S(1)} collective-permute-done((f32[2,256,256]{2,1,0:T(8,128)S(1)}, f32[2,256,256]{2,1,0:T(8,128)S(1)}, u32[]{:S(2)}, u32[]{:S(2)}) %collective-permute-start.10) | collective-permute-done | bytes 524320 | tf_op jit(solution)/shard_map/ppermute | solution.py:309
  89.2 1.3 collective-permute-start.16
  90.5 1.3 collective-permute-start.17
  91.8 3.9 %collective-permute-start.18 = (f32[2,256,256]{2,1,0:T(8,128)S(1)}, f32[2,256,256]{2,1,0:T(8,128)S(1)}, u32[]{:S(2)}, u32[]{:S(2)}) collective-permute-start(f32[2,256,256]{2,1,0:T(8,128)S(1)} %collective-permute-done.15.refs_1_), channel_id=1, source_target_pairs={{0,1},{1,0},{2,3},{3,2},{4,5},{5,4},{6,7},{7,6},{8,9},{9,8},{10,11... | collective-permute-start | bytes 1572872 | tf_op jit(solution)/shard_map/ppermute | solution.py:309
  95.7 3.5 %collective-permute-start.22 = (f32[2,256,256]{2,1,0:T(8,128)S(1)}, f32[2,256,256]{2,1,0:T(8,128)S(1)}, u32[]{:S(2)}, u32[]{:S(2)}) collective-permute-start(f32[2,256,256]{2,1,0:T(8,128)S(1)} %collective-permute-done.8.refs_1_), channel_id=1, source_target_pairs={{0,2},{2,4},{3,1},{4,6},{5,3},{7,5},{11,9},{13,11},{15,13},{16,18}... | collective-permute-start | bytes 1572872 | tf_op jit(solution)/shard_map/ppermute | solution.py:309
  99.2 1.3 collective-permute-start.24
  100.5 4.6 %collective-permute-start.23 = (f32[2,256,256]{2,1,0:T(8,128)S(1)}, f32[2,256,256]{2,1,0:T(8,128)S(1)}, u32[]{:S(2)}, u32[]{:S(2)}) collective-permute-start(f32[2,256,256]{2,1,0:T(8,128)S(1)} %collective-permute-done.10.refs_1_), channel_id=1, source_target_pairs={{0,2},{2,4},{3,1},{4,6},{5,3},{7,5},{8,10},{10,12},{12,14},{19,17}... | collective-permute-start | bytes 1572872 | tf_op jit(solution)/shard_map/ppermute | solution.py:309
  105.1 6.4 %collective-permute-done.17.refs_3_ = f32[2,256,256]{2,1,0:T(8,128)S(1)} collective-permute-done((f32[2,256,256]{2,1,0:T(8,128)S(1)}, f32[2,256,256]{2,1,0:T(8,128)S(1)}, u32[]{:S(2)}, u32[]{:S(2)}) %collective-permute-start.17) | collective-permute-done | bytes 524320 | tf_op jit(solution)/shard_map/ppermute | solution.py:309
  112.0 3.9 %collective-permute-start.26 = (f32[2,256,256]{2,1,0:T(8,128)S(1)}, f32[2,256,256]{2,1,0:T(8,128)S(1)}, u32[]{:S(2)}, u32[]{:S(2)}) collective-permute-start(f32[2,256,256]{2,1,0:T(8,128)S(1)} %collective-permute-done.12.refs_1_), channel_id=1, source_target_pairs={{0,2},{2,4},{4,6},{8,10},{10,12},{11,9},{12,14},{13,11},{15,13},{1... | collective-permute-start | bytes 1572872 | tf_op jit(solution)/shard_map/ppermute | solution.py:309
  115.9 6.8 %collective-permute-done.24.refs_1_ = f32[2,256,256]{2,1,0:T(8,128)S(1)} collective-permute-done((f32[2,256,256]{2,1,0:T(8,128)S(1)}, f32[2,256,256]{2,1,0:T(8,128)S(1)}, u32[]{:S(2)}, u32[]{:S(2)}) %collective-permute-start.24) | collective-permute-done | bytes 524320 | tf_op jit(solution)/shard_map/ppermute | solution.py:309
  123.3 0.8 shard_map.87.refs_0_
  124.2 1.0 shard_map.88.refs_0_
  125.2 1.0 shard_map.89.refs_0_
  126.3 1.2 shard_map.90.refs_0_
  127.5 2.1 %shard_map.91.refs_0_ = f32[1,4,2,256,256]{4,3,2,1,0:T(8,128)S(1)} custom-call(f32[8,128]{1,0:T(8,128)S(1)} %shard_map.82.weight_ref, f32[1,4,2,256,256]{4,3,2,1,0:T(8,128)S(1)} %shard_map.90.refs_0_, f32[2,256,256]{2,1,0:T(8,128)S(1)} %collective-permute-done.15.refs_1_, f32[2,256,256]{2,1,0:T(8,128)S(1)} %collective-permute-done.16.refs_2_, ...), custom_call_target="tpu_custom_call" | custom-call | tf_op jit(solution)/shard_map/pallas_call | solution.py:278
  129.7 2.1 %shard_map.92 = f32[1,4,2,256,256]{4,3,2,1,0:T(8,128)} custom-call(f32[8,128]{1,0:T(8,128)S(1)} %shard_map.82.weight_ref, f32[1,4,2,256,256]{4,3,2,1,0:T(8,128)S(1)} %shard_map.91.refs_0_, f32[2,256,256]{2,1,0:T(8,128)S(1)} %collective-permute-done.24.refs_1_, f32[2,256,256]{2,1,0:T(8,128)S(1)} %collective-permute-done.25.refs_2_, ...), custom_call_target="tpu_custom_call" | custom-call | tf_op jit(solution)/shard_map/pallas_call | solution.py:278
  (37 shorter events, 3.6 us)
Async XLA Ops:
  2.3 6.9 %collective-permute-start.3 = (f32[128,256]{1,0:T(8,128)S(1)}, f32[128,256]{1,0:T(8,128)S(1)}, u32[]{:S(2)}, u32[]{:S(2)}) collective-permute-start(f32[128,256]{1,0:T(8,128)S(1)} %get-tuple-element.20), channel_id=1, source_target_pairs={{0,8},{1,9},{2,10},{3,11},{4,12},{5,13},{6,14},{7,15},{8,0},{9,1},... | collective-permute-start | bytes 393224 | tf_op jit(solution)/shard_map/ppermute | solution.py:309
  5.3 7.8 %collective-permute-start.4 = (f32[128,256]{1,0:T(8,128)S(1)}, f32[128,256]{1,0:T(8,128)S(1)}, u32[]{:S(2)}, u32[]{:S(2)}) collective-permute-start(f32[128,256]{1,0:T(8,128)S(1)} %get-tuple-element.20), channel_id=1, source_target_pairs={{0,16},{1,17},{2,18},{3,19},{4,20},{5,21},{6,22},{7,23},{8,24},{9,... | collective-permute-start | bytes 393224 | tf_op jit(solution)/shard_map/ppermute | solution.py:309
  6.8 6.3 %collective-permute-start.5 = (f32[128,256]{1,0:T(8,128)S(1)}, f32[128,256]{1,0:T(8,128)S(1)}, u32[]{:S(2)}, u32[]{:S(2)}) collective-permute-start(f32[128,256]{1,0:T(8,128)S(1)} %get-tuple-element.20), channel_id=1, source_target_pairs={{0,24},{1,25},{2,26},{3,27},{4,28},{5,29},{6,30},{7,31},{8,16},{9,... | collective-permute-start | bytes 393224 | tf_op jit(solution)/shard_map/ppermute | solution.py:309
  13.1 9.7 %collective-permute-start.6 = (f32[3,128,256]{2,1,0:T(8,128)S(1)}, f32[3,128,256]{2,1,0:T(8,128)S(1)}, u32[]{:S(2)}, u32[]{:S(2)}) collective-permute-start(f32[3,128,256]{2,1,0:T(8,128)S(1)} %shard_map.84.near_ref), channel_id=1, source_target_pairs={{0,2},{1,3},{2,0},{3,1},{4,6},{5,7},{6,4},{7,5},{8,10},{9,11},{10,... | collective-permute-start | bytes 1179656 | tf_op jit(solution)/shard_map/ppermute | solution.py:309
  22.9 27.0 %collective-permute-start.7 = (f32[3,256,256]{2,1,0:T(8,128)S(1)}, f32[3,256,256]{2,1,0:T(8,128)S(1)}, u32[]{:S(2)}, u32[]{:S(2)}) collective-permute-start(f32[3,256,256]{2,1,0:T(8,128)S(1)} %shard_map.85.refs_5_), channel_id=1, source_target_pairs={{0,1},{1,0},{2,3},{3,2},{4,5},{5,4},{6,7},{7,6},{8,9},{9,8},{10,11... | collective-permute-start | bytes 2359304 | tf_op jit(solution)/shard_map/ppermute | solution.py:309
  23.0 14.9 %collective-permute-start = (f32[2,256,256]{2,1,0:T(8,128)S(1)}, f32[2,256,256]{2,1,0:T(8,128)S(1)}, u32[]{:S(2)}, u32[]{:S(2)}) collective-permute-start(f32[2,256,256]{2,1,0:T(8,128)S(1)} %get-tuple-element.16), channel_id=1, source_target_pairs={{0,8},{1,9},{2,10},{3,11},{4,12},{5,13},{6,14},{7,15},{8,0},{9,1},... | collective-permute-start | bytes 1572872 | tf_op jit(solution)/shard_map/ppermute | solution.py:309
  24.7 25.2 %collective-permute-start.1 = (f32[2,256,256]{2,1,0:T(8,128)S(1)}, f32[2,256,256]{2,1,0:T(8,128)S(1)}, u32[]{:S(2)}, u32[]{:S(2)}) collective-permute-start(f32[2,256,256]{2,1,0:T(8,128)S(1)} %get-tuple-element.17), channel_id=1, source_target_pairs={{0,16},{1,17},{2,18},{3,19},{4,20},{5,21},{6,22},{7,23},{8,24},{9,... | collective-permute-start | bytes 1572872 | tf_op jit(solution)/shard_map/ppermute | solution.py:309
  25.2 24.7 %collective-permute-start.2 = (f32[2,256,256]{2,1,0:T(8,128)S(1)}, f32[2,256,256]{2,1,0:T(8,128)S(1)}, u32[]{:S(2)}, u32[]{:S(2)}) collective-permute-start(f32[2,256,256]{2,1,0:T(8,128)S(1)} %get-tuple-element.18), channel_id=1, source_target_pairs={{0,24},{1,25},{2,26},{3,27},{4,28},{5,29},{6,30},{7,31},{8,16},{9,... | collective-permute-start | bytes 1572872 | tf_op jit(solution)/shard_map/ppermute | solution.py:309
  49.9 72.9 %copy-start = (f32[8]{0:T(128)S(1)}, f32[8]{0:T(128)}, u32[]{:S(2)}) copy-start(f32[8]{0:T(128)} %value_ref.1) | copy-start | bytes 100
  49.9 72.9 %copy-start.1 = (s32[8]{0:T(128)S(1)}, s32[8]{0:T(128)}, u32[]{:S(2)}) copy-start(s32[8]{0:T(128)} %offset_ref.1) | copy-start | bytes 100
  62.6 14.9 %collective-permute-start.8 = (f32[2,256,256]{2,1,0:T(8,128)S(1)}, f32[2,256,256]{2,1,0:T(8,128)S(1)}, u32[]{:S(2)}, u32[]{:S(2)}) collective-permute-start(f32[2,256,256]{2,1,0:T(8,128)S(1)} %get-tuple-element.22), channel_id=1, source_target_pairs={{0,8},{1,9},{2,10},{3,11},{4,12},{5,13},{6,14},{7,15},{8,0},{9,1},... | collective-permute-start | bytes 1572872 | tf_op jit(solution)/shard_map/ppermute | solution.py:309
  63.1 15.1 %collective-permute-start.9 = (f32[2,256,256]{2,1,0:T(8,128)S(1)}, f32[2,256,256]{2,1,0:T(8,128)S(1)}, u32[]{:S(2)}, u32[]{:S(2)}) collective-permute-start(f32[2,256,256]{2,1,0:T(8,128)S(1)} %get-tuple-element.21.refs_0_), channel_id=1, source_target_pairs={{0,1},{1,0},{2,3},{3,2},{4,5},{5,4},{6,7},{7,6},{8,9},{9,8},{10,11... | collective-permute-start | bytes 1572872 | tf_op jit(solution)/shard_map/ppermute | solution.py:309
  63.1 25.6 %collective-permute-start.10 = (f32[2,256,256]{2,1,0:T(8,128)S(1)}, f32[2,256,256]{2,1,0:T(8,128)S(1)}, u32[]{:S(2)}, u32[]{:S(2)}) collective-permute-start(f32[2,256,256]{2,1,0:T(8,128)S(1)} %get-tuple-element.23), channel_id=1, source_target_pairs={{0,16},{1,17},{2,18},{3,19},{4,20},{5,21},{6,22},{7,23},{8,24},{9,... | collective-permute-start | bytes 1572872 | tf_op jit(solution)/shard_map/ppermute | solution.py:309
  64.9 23.8 %collective-permute-start.12 = (f32[2,256,256]{2,1,0:T(8,128)S(1)}, f32[2,256,256]{2,1,0:T(8,128)S(1)}, u32[]{:S(2)}, u32[]{:S(2)}) collective-permute-start(f32[2,256,256]{2,1,0:T(8,128)S(1)} %get-tuple-element.24), channel_id=1, source_target_pairs={{0,24},{1,25},{2,26},{3,27},{4,28},{5,29},{6,30},{7,31},{8,16},{9,... | collective-permute-start | bytes 1572872 | tf_op jit(solution)/shard_map/ppermute | solution.py:309
  66.2 23.0 %collective-permute-start.15 = (f32[2,256,256]{2,1,0:T(8,128)S(1)}, f32[2,256,256]{2,1,0:T(8,128)S(1)}, u32[]{:S(2)}, u32[]{:S(2)}) collective-permute-start(f32[2,256,256]{2,1,0:T(8,128)S(1)} %get-tuple-element.21.refs_0_), channel_id=1, source_target_pairs={{1,3},{2,0},{3,5},{4,2},{5,7},{6,4},{9,11},{10,8},{11,13},{12,10},... | collective-permute-start | bytes 1572872 | tf_op jit(solution)/shard_map/ppermute | solution.py:309
  77.5 13.0 %collective-permute-start.21 = (f32[2,256,256]{2,1,0:T(8,128)S(1)}, f32[2,256,256]{2,1,0:T(8,128)S(1)}, u32[]{:S(2)}, u32[]{:S(2)}) collective-permute-start(f32[2,256,256]{2,1,0:T(8,128)S(1)} %get-tuple-element.21.refs_0_), channel_id=1, source_target_pairs={{3,1},{5,3},{7,5},{8,10},{10,12},{11,9},{12,14},{13,11},{15,13},{1... | collective-permute-start | bytes 1572872 | tf_op jit(solution)/shard_map/ppermute | solution.py:309
  78.2 13.6 %collective-permute-start.11 = (f32[2,256,256]{2,1,0:T(8,128)S(1)}, f32[2,256,256]{2,1,0:T(8,128)S(1)}, u32[]{:S(2)}, u32[]{:S(2)}) collective-permute-start(f32[2,256,256]{2,1,0:T(8,128)S(1)} %collective-permute-done.8.refs_1_), channel_id=1, source_target_pairs={{0,1},{1,0},{2,3},{3,2},{4,5},{5,4},{6,7},{7,6},{8,9},{9,8},{10,11... | collective-permute-start | bytes 1572872 | tf_op jit(solution)/shard_map/ppermute | solution.py:309
  88.7 7.1 %collective-permute-start.13 = (f32[2,256,256]{2,1,0:T(8,128)S(1)}, f32[2,256,256]{2,1,0:T(8,128)S(1)}, u32[]{:S(2)}, u32[]{:S(2)}) collective-permute-start(f32[2,256,256]{2,1,0:T(8,128)S(1)} %collective-permute-done.10.refs_1_), channel_id=1, source_target_pairs={{0,1},{1,0},{2,3},{3,2},{4,5},{5,4},{6,7},{7,6},{8,9},{9,8},{10,11... | collective-permute-start | bytes 1572872 | tf_op jit(solution)/shard_map/ppermute | solution.py:309
  88.7 10.5 %collective-permute-start.14 = (f32[2,256,256]{2,1,0:T(8,128)S(1)}, f32[2,256,256]{2,1,0:T(8,128)S(1)}, u32[]{:S(2)}, u32[]{:S(2)}) collective-permute-start(f32[2,256,256]{2,1,0:T(8,128)S(1)} %collective-permute-done.12.refs_1_), channel_id=1, source_target_pairs={{0,1},{1,0},{2,3},{3,2},{4,5},{5,4},{6,7},{7,6},{8,9},{9,8},{10,11... | collective-permute-start | bytes 1572872 | tf_op jit(solution)/shard_map/ppermute | solution.py:309
  89.2 11.3 %collective-permute-start.16 = (f32[2,256,256]{2,1,0:T(8,128)S(1)}, f32[2,256,256]{2,1,0:T(8,128)S(1)}, u32[]{:S(2)}, u32[]{:S(2)}) collective-permute-start(f32[2,256,256]{2,1,0:T(8,128)S(1)} %collective-permute-done.8.refs_1_), channel_id=1, source_target_pairs={{1,3},{2,0},{3,5},{4,2},{5,7},{6,4},{9,11},{10,8},{11,13},{12,10},... | collective-permute-start | bytes 1572872 | tf_op jit(solution)/shard_map/ppermute | solution.py:309
  90.5 21.0 %collective-permute-start.17 = (f32[2,256,256]{2,1,0:T(8,128)S(1)}, f32[2,256,256]{2,1,0:T(8,128)S(1)}, u32[]{:S(2)}, u32[]{:S(2)}) collective-permute-start(f32[2,256,256]{2,1,0:T(8,128)S(1)} %collective-permute-done.10.refs_1_), channel_id=1, source_target_pairs={{1,3},{2,0},{3,5},{4,2},{5,7},{6,4},{9,11},{10,8},{11,13},{12,10},... | collective-permute-start | bytes 1572872 | tf_op jit(solution)/shard_map/ppermute | solution.py:309
  91.8 19.7 %collective-permute-start.18 = (f32[2,256,256]{2,1,0:T(8,128)S(1)}, f32[2,256,256]{2,1,0:T(8,128)S(1)}, u32[]{:S(2)}, u32[]{:S(2)}) collective-permute-start(f32[2,256,256]{2,1,0:T(8,128)S(1)} %collective-permute-done.15.refs_1_), channel_id=1, source_target_pairs={{0,1},{1,0},{2,3},{3,2},{4,5},{5,4},{6,7},{7,6},{8,9},{9,8},{10,11... | collective-permute-start | bytes 1572872 | tf_op jit(solution)/shard_map/ppermute | solution.py:309
  95.7 16.3 %collective-permute-start.22 = (f32[2,256,256]{2,1,0:T(8,128)S(1)}, f32[2,256,256]{2,1,0:T(8,128)S(1)}, u32[]{:S(2)}, u32[]{:S(2)}) collective-permute-start(f32[2,256,256]{2,1,0:T(8,128)S(1)} %collective-permute-done.8.refs_1_), channel_id=1, source_target_pairs={{0,2},{2,4},{3,1},{4,6},{5,3},{7,5},{11,9},{13,11},{15,13},{16,18}... | collective-permute-start | bytes 1572872 | tf_op jit(solution)/shard_map/ppermute | solution.py:309
  99.2 23.5 %collective-permute-start.24 = (f32[2,256,256]{2,1,0:T(8,128)S(1)}, f32[2,256,256]{2,1,0:T(8,128)S(1)}, u32[]{:S(2)}, u32[]{:S(2)}) collective-permute-start(f32[2,256,256]{2,1,0:T(8,128)S(1)} %collective-permute-done.12.refs_1_), channel_id=1, source_target_pairs={{1,3},{2,0},{3,5},{4,2},{5,7},{6,4},{9,11},{10,8},{11,13},{12,10},... | collective-permute-start | bytes 1572872 | tf_op jit(solution)/shard_map/ppermute | solution.py:309
  100.5 26.9 %collective-permute-start.23 = (f32[2,256,256]{2,1,0:T(8,128)S(1)}, f32[2,256,256]{2,1,0:T(8,128)S(1)}, u32[]{:S(2)}, u32[]{:S(2)}) collective-permute-start(f32[2,256,256]{2,1,0:T(8,128)S(1)} %collective-permute-done.10.refs_1_), channel_id=1, source_target_pairs={{0,2},{2,4},{3,1},{4,6},{5,3},{7,5},{8,10},{10,12},{12,14},{19,17}... | collective-permute-start | bytes 1572872 | tf_op jit(solution)/shard_map/ppermute | solution.py:309
  111.5 16.0 %collective-permute-start.19 = (f32[2,256,256]{2,1,0:T(8,128)S(1)}, f32[2,256,256]{2,1,0:T(8,128)S(1)}, u32[]{:S(2)}, u32[]{:S(2)}) collective-permute-start(f32[2,256,256]{2,1,0:T(8,128)S(1)} %collective-permute-done.16.refs_2_), channel_id=1, source_target_pairs={{0,1},{1,0},{2,3},{3,2},{4,5},{5,4},{6,7},{7,6},{8,9},{9,8},{10,11... | collective-permute-start | bytes 1572872 | tf_op jit(solution)/shard_map/ppermute | solution.py:309
  111.5 16.0 %collective-permute-start.20 = (f32[2,256,256]{2,1,0:T(8,128)S(1)}, f32[2,256,256]{2,1,0:T(8,128)S(1)}, u32[]{:S(2)}, u32[]{:S(2)}) collective-permute-start(f32[2,256,256]{2,1,0:T(8,128)S(1)} %collective-permute-done.17.refs_3_), channel_id=1, source_target_pairs={{0,1},{1,0},{2,3},{3,2},{4,5},{5,4},{6,7},{7,6},{8,9},{9,8},{10,11... | collective-permute-start | bytes 1572872 | tf_op jit(solution)/shard_map/ppermute | solution.py:309
  112.0 17.6 %collective-permute-start.26 = (f32[2,256,256]{2,1,0:T(8,128)S(1)}, f32[2,256,256]{2,1,0:T(8,128)S(1)}, u32[]{:S(2)}, u32[]{:S(2)}) collective-permute-start(f32[2,256,256]{2,1,0:T(8,128)S(1)} %collective-permute-done.12.refs_1_), channel_id=1, source_target_pairs={{0,2},{2,4},{4,6},{8,10},{10,12},{11,9},{12,14},{13,11},{15,13},{1... | collective-permute-start | bytes 1572872 | tf_op jit(solution)/shard_map/ppermute | solution.py:309
  122.7 6.9 %collective-permute-start.25 = (f32[2,256,256]{2,1,0:T(8,128)S(1)}, f32[2,256,256]{2,1,0:T(8,128)S(1)}, u32[]{:S(2)}, u32[]{:S(2)}) collective-permute-start(f32[2,256,256]{2,1,0:T(8,128)S(1)} %collective-permute-done.24.refs_1_), channel_id=1, source_target_pairs={{0,1},{1,0},{2,3},{3,2},{4,5},{5,4},{6,7},{7,6},{8,9},{9,8},{10,11... | collective-permute-start | bytes 1572872 | tf_op jit(solution)/shard_map/ppermute | solution.py:309

commit v3 on v2

--- a/solution.py
+++ b/solution.py
@@ -30,29 +30,25 @@
 
 
 def dot3(a, b, transposed=False):
-    return (
-        dot(a[0], b[0], transposed) + dot(a[0], b[1], transposed) + dot(a[1], b[0], transposed)
-    )
-
-
-def negated(a):
-    return (-a[0], -a[1])
+    left = jnp.concatenate([a[0], a[0], a[1]], axis=1)
+    right = jnp.concatenate([b[0], b[1], b[0]], axis=1 if transposed else 0)
+    return dot(left, right, transposed)
 
 
 def product(a, b):
-    real = dot3(a[0], b[0]) + dot3(negated(a[1]), b[1])
-    imag = dot3(a[0], b[1]) + dot3(a[1], b[0])
-    return real, imag
+    rr = dot3(a[0], b[0])
+    ii = dot3(a[1], b[1])
+    return rr - ii, dot3(a[2], b[2]) - rr - ii
 
 
 def product_adjoint(a, c):
-    real = dot3(a[0], c[0], True) + dot3(a[1], c[1], True)
-    imag = dot3(a[1], c[0], True) + dot3(negated(a[0]), c[1], True)
-    return real, imag
+    rr = dot3(a[0], c[0], True)
+    ii = dot3(a[1], c[1], True)
+    return rr + ii, dot3(a[2], c[3], True) - rr + ii
 
 
 def split_pair(pair):
-    return split(pair[0]), split(pair[1])
+    return split(pair[0]), split(pair[1]), split(pair[0] + pair[1]), split(pair[0] - pair[1])
 
 
 def eye_mask(n):
@@ -148,24 +144,34 @@
 
 
 def solve_kernel(layer_count, *refs):
-    base_refs = refs[:layer_count]
-    masked_ref, same_ref, other_ref = refs[layer_count : layer_count + 3]
-    out_refs = refs[layer_count + 3 : 2 * layer_count + 3]
-    system, coup, green = refs[2 * layer_count + 3 :]
+    refs = list(refs)
+    take = lambda count: [refs.pop(0) for _ in range(count)]
+    (own_base,) = take(1)
+    base_refs = [take(layer_count - 1) for _ in range(2)]
+    masked_ref, same_ref, other_ref = take(3)
+    out_refs = take(layer_count)
+    system, coup, green = refs
     layer = lax.axis_index("layer")
     core = lax.axis_index("energy") % 2
 
     def step(l, carry):
         source = jnp.bitwise_xor(layer, l)
-        for k in range(layer_count):
+
+        @pl.when(source == 0)
+        def _():
+            system[...] = own_base[...]
+            coup[...] = masked_ref[...]
+
+        for k in range(1, layer_count):
             @pl.when(source == k)
             def _(k=k):
-                system[...] = base_refs[k][...]
-                if k == 0:
-                    coup[...] = masked_ref[...]
-                else:
-                    coup[core] = same_ref[k - 1]
-                    coup[1 - core] = other_ref[k - 1]
+                coup[core] = same_ref[k - 1]
+                coup[1 - core] = other_ref[k - 1]
+
+            for c in range(2):
+                @pl.when((source == k) & (core == c))
+                def _(k=k, c=c):
+                    system[...] = base_refs[c][k - 1][...]
 
         @pl.when(l > 0)
         def _():
@@ -189,77 +195,90 @@
 STEP_ROWS = 16
 
 
+MINE, INNER, OUTER, CROSSED = range(4)
+
+
 def weight_kernel(value_ref, offset_ref, out_ref):
     layer = lax.axis_index("layer")
-    group = lax.axis_index("energy")
+    core = lax.axis_index("energy") % 2
     layer_count = lax.axis_size("layer")
     per_device = layer_count
-    span = 2 * per_device
-    core = group % 2
     shape = out_ref.shape
     row = lax.broadcasted_iota(jnp.int32, shape, 0)
     lane = lax.broadcasted_iota(jnp.int32, shape, 1)
     kind = lane // layer_count
     away = 2 * core - 1
-    shift = jnp.where(kind == INNER, -away, jnp.where(kind == CROSSED, away, 0))
-    shift = jnp.where(kind == OUTER, away, shift)
-    far_core = jnp.where((kind == THEIRS) | (kind == CROSSED), 1 - core, core)
+    shift = jnp.where(kind == INNER, -away, jnp.where(kind == MINE, 0, away))
+    far_core = jnp.where(kind == CROSSED, 1 - core, core)
     source = jnp.bitwise_xor(lane % layer_count, layer)
-    gap = span * shift + per_device * far_core + source - (per_device * core + row)
+    target = jnp.where(row < per_device, per_device * core, -per_device * core) + row
+    gap = 2 * per_device * shift + per_device * far_core + source - target
     total = jnp.zeros(shape, F32)
     for tap in range(value_ref.shape[0]):
         total += jnp.where(gap == offset_ref[tap], value_ref[tap], 0.0)
     out_ref[...] = total
 
 
-MINE, THEIRS, INNER, CROSSED, OUTER = range(5)
-
-
-def mix_rows(weight_ref, slots, acc, refs, outputs, part, start):
-    here = pl.ds(pl.multiple_of(start, STEP_ROWS), STEP_ROWS)
-    total = [None] * outputs if acc is None else [acc[0, f, part, here, :] for f in range(outputs)]
+STEP_ROWS = 8
+
+
+def add_blocks(total, weight_ref, slots, refs, part, here, first_row):
+    total = list(total)
     for slot, ref in zip(slots, refs):
         x = ref[part, here, :]
-        for f in range(outputs):
-            term = weight_ref[f, slot] * x
+        for f in range(len(total)):
+            term = weight_ref[first_row + f, slot] * x
             total[f] = term if total[f] is None else total[f] + term
-    return here, total
-
-
-def mix_kernel(slots, has_acc, weight_ref, *refs):
+    return total
+
+
+def tick_kernel(in_ref, out_ref):
+    out_ref[...] = in_ref[...]
+
+
+def mix_kernel(both, single, has_acc, weight_ref, *refs):
     refs = list(refs)
-    out_ref = refs.pop()
-    acc_ref = refs.pop(0) if has_acc else None
-    outputs, parts, rows, _ = out_ref.shape[1:]
+    own_ref, partner_ref = refs[-2:]
+    accs = refs[:2] if has_acc else None
+    blocks = refs[2 if has_acc else 0 : -2]
+    outputs, parts, rows, _ = own_ref.shape
     for part in range(parts):
         def body(i, carry, part=part):
-            here, total = mix_rows(
-                weight_ref, slots, acc_ref, refs, outputs, part, i * STEP_ROWS
-            )
-            for f in range(outputs):
-                out_ref[0, f, part, here, :] = total[f]
+            here = pl.ds(pl.multiple_of(i * STEP_ROWS, STEP_ROWS), STEP_ROWS)
+            for side, (target, slots) in enumerate(
+                ((own_ref, both + single), (partner_ref, both))
+            ):
+                total = [accs[side][f, part, here, :] if has_acc else None for f in range(outputs)]
+                total = add_blocks(
+                    total, weight_ref, slots, blocks[: len(slots)], part, here, side * outputs
+                )
+                for f in range(outputs):
+                    target[f, part, here, :] = total[f]
             return carry
 
         lax.fori_loop(0, rows // STEP_ROWS, body, 0, unroll=2)
 
 
-def last_kernel(slots, weight_ref, *refs):
-    acc_ref, blocks, out_ref, buffer, sems = refs[0], refs[1:-3], refs[-3], refs[-2], refs[-1]
-    outputs, parts, rows, _ = out_ref.shape[1:]
-    pieces = 2
+def last_kernel(slots, weight_ref, own_ref, partner_ref, *refs):
+    blocks, out_ref, buffer, sems = refs[:-3], refs[-3], refs[-2], refs[-1]
+    outputs, parts, rows, _ = own_ref.shape
+    pieces = sems.shape[1]
     size = rows // pieces
     copies = []
     for part in range(parts):
         for piece in range(pieces):
             def body(i, carry, part=part, base=piece * size):
-                here, total = mix_rows(
-                    weight_ref, slots, acc_ref, blocks, outputs, part, base + i * STEP_ROWS
-                )
+                here = pl.ds(pl.multiple_of(base + i * STEP_ROWS, STEP_ROWS), STEP_ROWS)
+                total = [
+                    own_ref[f, part, here, :] + partner_ref[f, part, here, :]
+                    for f in range(outputs)
+                ]
+                total = add_blocks(total, weight_ref, slots, blocks, part, here, 0)
                 for f in range(outputs):
                     buffer[0, f, part, here, :] = total[f]
                 return carry
 
-            lax.fori_loop(0, size // STEP_ROWS, body, 0, unroll=2)
+            lax.fori_loop(0, size // STEP_ROWS, body, 0, unroll=4)
             here = (slice(None), slice(None), part, pl.ds(piece * size, size))
             copy = pltpu.make_async_copy(buffer.at[here], out_ref.at[here], sems.at[part, piece])
             copy.start()
@@ -323,18 +342,23 @@
         space=HBM,
     )
     quarters = [to_layer(quarter, k) for k in ks]
-    bases = [bases[0]] + [to_layer(bases[k], k) for k in ks]
+    moved = [
+        [move(bases[k], lambda l, g: (l ^ k, g), lambda l, g: g % 2 == c) for k in ks]
+        for c in range(2)
+    ]
     weights = run(
-        weight_kernel, [], VMEM((8 * -(-per_device // 8), 128), F32),
+        weight_kernel, [], VMEM((8 * -(-span // 8), 128), F32),
         [kernel_weights, kernel_offsets],
     )
+    for _ in range(layer_count - 1):
+        weights = run(tick_kernel, [weights], VMEM(weights.shape, F32))
     near = run(stack_kernel, quarters, VMEM((len(ks), n // 2, n), F32))
     far = move(near, lambda l, g: (l, g ^ 2))
     same = run(join_kernel, [near, far], VMEM((len(ks), n, n), F32))
     other = swapped(same)
     greens = run(
         functools.partial(solve_kernel, layer_count),
-        [*bases, masked, same, other], [block] * layer_count, scratch=[block] * 3,
+        [bases[0], *moved[0], *moved[1], masked, same, other], [block] * layer_count, scratch=[block] * 3,
     )
 
     mine = [greens[0]] + [to_layer(greens[k], k) for k in ks]
@@ -343,7 +367,7 @@
         spot = per_device * (g % 2) + (l ^ k)
         return (span - spot if step > 0 else spot + 1) <= REACH
 
-    inner, outer, theirs, crossed = [], [], [], []
+    inner, outer = [], []
     for k in range(layer_count):
         def beyond(sign, k=k):
             step = lambda g: sign * (4 * (g % 2) - 2)
@@ -354,32 +378,37 @@
 
         inner.append(beyond(1))
         outer.append(beyond(-1))
-        theirs.append(swapped(mine[k]))
-        crossed.append(swapped(inner[k]))
-
+    final = layer_count - 1
+    crossed = swapped(inner[final])
+    kinds = {MINE: mine, INNER: inner, OUTER: outer, CROSSED: {final: crossed}}
+    sums = VMEM((per_device, 2, n, n), F32)
+
+    def slots_of(entries):
+        return tuple(kind * layer_count + k for kind, k in entries)
+
+    def mixed(accs, both, single=()):
+        kernel = functools.partial(
+            mix_kernel, slots_of(both), slots_of(single), accs is not None
+        )
+        blocks = [kinds[kind][k] for kind, k in (*both, *single)]
+        return run(kernel, [*(accs or ()), *blocks], [sums, sums], [weights])
+
+    every = range(layer_count)
+    early = range(final - 1)
+    sides = mixed(
+        None, [(MINE, k) for k in every] + [(INNER, k) for k in early],
+        [(OUTER, k) for k in early],
+    )
+    own, partner = mixed(sides, [(INNER, final - 1)], [(OUTER, final - 1)])
+    given = swapped(partner)
+    ending = [(INNER, final), (OUTER, final), (CROSSED, final)]
     shape = (1, per_device, 2, n, n)
-    kinds = {MINE: mine, THEIRS: theirs, INNER: inner, CROSSED: crossed, OUTER: outer}
-
-    def mixed(acc, entries, name):
-        slots = tuple(kind * layer_count + k for kind, k in entries)
-        blocks = [kinds[kind][k] for kind, k in entries]
-        if name == "mix_last":
-            return run(
-                functools.partial(last_kernel, slots), [acc] + blocks,
-                jax.ShapeDtypeStruct(shape, F32), [weights],
-                [VMEM(shape, F32), pltpu.SemaphoreType.DMA((2, 2))], out_specs=HBM_SPEC,
-            )
-        kernel = functools.partial(mix_kernel, slots, acc is not None)
-        return run(kernel, ([] if acc is None else [acc]) + blocks, VMEM(shape, F32), [weights])
-
-    final = layer_count - 1
-    acc = mixed(None, [(MINE, 0)], "mix_own")
-    for k in ks[:-1]:
-        acc = mixed(acc, [(MINE, k), (THEIRS, k - 1)], f"mix_next{k}")
-    acc = mixed(acc, [(MINE, final), (THEIRS, final - 1), (THEIRS, final)], "mix_near")
-    outside = (INNER, CROSSED, OUTER)
-    acc = mixed(acc, [(kind, k) for kind in outside for k in range(final)], "mix_far")
-    return mixed(acc, [(kind, final) for kind in outside], "mix_last")
+    return run(
+        functools.partial(last_kernel, slots_of(ending)),
+        [own, given] + [kinds[kind][k] for kind, k in ending],
+        jax.ShapeDtypeStruct(shape, F32), [weights],
+        [VMEM(shape, F32), pltpu.SemaphoreType.DMA((2, 2))], out_specs=HBM_SPEC,
+    )
 
 
 def solution(mesh):

time: 132 us -> 115 us (0.87)
  waiting for transfers between devices: 71.3 us -> 45.8 us
  starting transfers between devices: 36.2 us -> 47.8 us
  Pallas kernels: 24 us -> 19.7 us
    ppermute x27 -> x24, waiting for transfers between devices: 71.3 us -> 45.8 us  [move(): return lax.ppermute(x, AXES, pairs)]
    ppermute x27 -> x24, starting transfers between devices: 36.2 us -> 47.8 us  [move(): return lax.ppermute(x, AXES, pairs)]
    pallas_call x11, Pallas kernels: 24 us -> 19.7 us  [run(): pl.pallas_call(kernel, in_specs=[SMEM_SPEC] * len(head) + [pl.BlockSpec(m...]
  transfers between devices with their start and end apart: 27 -> 24, of which waited for: 9 -> 12; matrix products, arithmetic and copies ran while one was open for 0% -> 0% of each run, Pallas kernels for 5% -> 3%
where the time goes in v3:
time: 115 us; the launch traced here: 114 us
  starting transfers between devices  47.8 us (42%)
  waiting for transfers between devices  45.8 us (40%)
  Pallas kernels  19.7 us (17%)
    ppermute x24, starting transfers between devices, move(): return lax.ppermute(x, AXES, pairs)  47.8 us
    ppermute x24, waiting for transfers between devices, move(): return lax.ppermute(x, AXES, pairs)  45.8 us
    pallas_call x11, Pallas kernels, run(): pl.pallas_call(kernel, in_specs=[SMEM_SPEC] * len(head) + [pl.BlockSpec(m...  19.7 us
  transfers between devices with their start and end apart: 24, of which 12 were waited for; matrix products, arithmetic and copies ran while one was open for 0% of the time, Pallas kernels for 3%

profile of v3, /device:TPU:0, one launch (start us, length us, event | category | flops | bytes accessed | tf_op | source)
XLA Modules:
  0.0 113.6 jit_solution(17470800279295116436)
XLA Ops:
  0.0 2.3 %shard_map.86 = (f32[2,256,256]{2,1,0:T(8,128)S(1)}, f32[128,256]{1,0:T(8,128)S(1)}, f32[2,256,256]{2,1,0:T(8,128)S(1)}, f32[2,256,256]{2,1,0:T(8,128)S(1)}, f32...) custom-call(f32[1,2,256,256]{3,2,1,0:T(8,128)} %coup_hbm.1, s32[1,256,256]{2,1,0:T(8,128)} %mask_hbm.1, ...), custom_call_target="tpu_custom_call" | custom-call | tf_op jit(solution)/shard_map/pallas_call | solution.py:297
  2.3 3.0 %collective-permute-start.6 = (f32[128,256]{1,0:T(8,128)S(1)}, f32[128,256]{1,0:T(8,128)S(1)}, u32[]{:S(2)}, u32[]{:S(2)}) collective-permute-start(f32[128,256]{1,0:T(8,128)S(1)} %get-tuple-element.24), channel_id=1, source_target_pairs={{0,8},{1,9},{2,10},{3,11},{4,12},{5,13},{6,14},{7,15},{8,0},{9,1},... | collective-permute-start | bytes 393224 | tf_op jit(solution)/shard_map/ppermute | solution.py:328
  5.3 1.5 %collective-permute-start.7 = (f32[128,256]{1,0:T(8,128)S(1)}, f32[128,256]{1,0:T(8,128)S(1)}, u32[]{:S(2)}, u32[]{:S(2)}) collective-permute-start(f32[128,256]{1,0:T(8,128)S(1)} %get-tuple-element.24), channel_id=1, source_target_pairs={{0,16},{1,17},{2,18},{3,19},{4,20},{5,21},{6,22},{7,23},{8,24},{9,... | collective-permute-start | bytes 393224 | tf_op jit(solution)/shard_map/ppermute | solution.py:328
  6.9 2.3 %collective-permute-done.6.refs_0_ = f32[128,256]{1,0:T(8,128)S(1)} collective-permute-done((f32[128,256]{1,0:T(8,128)S(1)}, f32[128,256]{1,0:T(8,128)S(1)}, u32[]{:S(2)}, u32[]{:S(2)}) %collective-permute-start.6) | collective-permute-done | bytes 131104 | tf_op jit(solution)/shard_map/ppermute | solution.py:328
  9.2 3.9 %collective-permute-done.7.refs_1_ = f32[128,256]{1,0:T(8,128)S(1)} collective-permute-done((f32[128,256]{1,0:T(8,128)S(1)}, f32[128,256]{1,0:T(8,128)S(1)}, u32[]{:S(2)}, u32[]{:S(2)}) %collective-permute-start.7) | collective-permute-done | bytes 131104 | tf_op jit(solution)/shard_map/ppermute | solution.py:328
  13.1 1.6 %collective-permute-start.9 = (f32[3,128,256]{2,1,0:T(8,128)S(1)}, f32[3,128,256]{2,1,0:T(8,128)S(1)}, u32[]{:S(2)}, u32[]{:S(2)}) collective-permute-start(f32[3,128,256]{2,1,0:T(8,128)S(1)} %shard_map.87.near_ref), channel_id=1, source_target_pairs={{0,2},{1,3},{2,0},{3,1},{4,6},{5,7},{6,4},{7,5},{8,10},{9,11},{10,... | collective-permute-start | bytes 1179656 | tf_op jit(solution)/shard_map/ppermute | solution.py:328
  14.8 3.1 %collective-permute-start = (f32[2,256,256]{2,1,0:T(8,128)S(1)}, f32[2,256,256]{2,1,0:T(8,128)S(1)}, u32[]{:S(2)}, u32[]{:S(2)}) collective-permute-start(f32[2,256,256]{2,1,0:T(8,128)S(1)} %get-tuple-element.20), channel_id=1, source_target_pairs={{0,8},{2,10},{4,12},{6,14},{8,0},{10,2},{12,4},{14,6},{16,24},{18,... | collective-permute-start | bytes 1572872 | tf_op jit(solution)/shard_map/ppermute | solution.py:328
  17.9 2.7 %collective-permute-start.1 = (f32[2,256,256]{2,1,0:T(8,128)S(1)}, f32[2,256,256]{2,1,0:T(8,128)S(1)}, u32[]{:S(2)}, u32[]{:S(2)}) collective-permute-start(f32[2,256,256]{2,1,0:T(8,128)S(1)} %get-tuple-element.21), channel_id=1, source_target_pairs={{0,16},{2,18},{4,20},{6,22},{8,24},{10,26},{12,28},{14,30},{16,0},... | collective-permute-start | bytes 1572872 | tf_op jit(solution)/shard_map/ppermute | solution.py:328
  20.6 2.2 %collective-permute-done.9.far_ref = f32[3,128,256]{2,1,0:T(8,128)S(1)} collective-permute-done((f32[3,128,256]{2,1,0:T(8,128)S(1)}, f32[3,128,256]{2,1,0:T(8,128)S(1)}, u32[]{:S(2)}, u32[]{:S(2)}) %collective-permute-start.9) | collective-permute-done | bytes 393248 | tf_op jit(solution)/shard_map/ppermute | solution.py:328
  23.7 3.4 %collective-permute-start.2 = (f32[2,256,256]{2,1,0:T(8,128)S(1)}, f32[2,256,256]{2,1,0:T(8,128)S(1)}, u32[]{:S(2)}, u32[]{:S(2)}) collective-permute-start(f32[2,256,256]{2,1,0:T(8,128)S(1)} %get-tuple-element.22), channel_id=1, source_target_pairs={{0,24},{2,26},{4,28},{6,30},{8,16},{10,18},{12,20},{14,22},{16,8},... | collective-permute-start | bytes 1572872 | tf_op jit(solution)/shard_map/ppermute | solution.py:328
  29.7 11.7 %collective-permute-done.2.refs_3_ = f32[2,256,256]{2,1,0:T(8,128)S(1)} collective-permute-done((f32[2,256,256]{2,1,0:T(8,128)S(1)}, f32[2,256,256]{2,1,0:T(8,128)S(1)}, u32[]{:S(2)}, u32[]{:S(2)}) %collective-permute-start.2) | collective-permute-done | bytes 524320 | tf_op jit(solution)/shard_map/ppermute | solution.py:328
  41.4 10.4 %shard_map.89 = (f32[2,256,256]{2,1,0:T(8,128)S(1)}, f32[2,256,256]{2,1,0:T(8,128)S(1)}, f32[2,256,256]{2,1,0:T(8,128)S(1)}, f32[2,256,256]{2,1,0:T(8,128)S(1)}) custom-call(f32[2,256,256]{2,1,0:T(8,128)S(1)} %get-tuple-element.19.refs_0_, f32[2,256,256]{2,1,0:T(8,128)S(1)} %collective-permute-done.refs_1_, ...), custom_call_target="tpu_custom_call" | custom-call | tf_op jit(solution)/shard_map/pallas_call | solution.py:297
  51.8 1.7 %collective-permute-start.11 = (f32[2,256,256]{2,1,0:T(8,128)S(1)}, f32[2,256,256]{2,1,0:T(8,128)S(1)}, u32[]{:S(2)}, u32[]{:S(2)}) collective-permute-start(f32[2,256,256]{2,1,0:T(8,128)S(1)} %get-tuple-element.26), channel_id=1, source_target_pairs={{0,8},{1,9},{2,10},{3,11},{4,12},{5,13},{6,14},{7,15},{8,0},{9,1},... | collective-permute-start | bytes 1572872 | tf_op jit(solution)/shard_map/ppermute | solution.py:328
  54.0 1.4 %collective-permute-start.13 = (f32[2,256,256]{2,1,0:T(8,128)S(1)}, f32[2,256,256]{2,1,0:T(8,128)S(1)}, u32[]{:S(2)}, u32[]{:S(2)}) collective-permute-start(f32[2,256,256]{2,1,0:T(8,128)S(1)} %get-tuple-element.28), channel_id=1, source_target_pairs={{0,24},{1,25},{2,26},{3,27},{4,28},{5,29},{6,30},{7,31},{8,16},{9,... | collective-permute-start | bytes 1572872 | tf_op jit(solution)/shard_map/ppermute | solution.py:328
  55.4 1.3 %collective-permute-start.14 = (f32[2,256,256]{2,1,0:T(8,128)S(1)}, f32[2,256,256]{2,1,0:T(8,128)S(1)}, u32[]{:S(2)}, u32[]{:S(2)}) collective-permute-start(f32[2,256,256]{2,1,0:T(8,128)S(1)} %get-tuple-element.25.refs_0_), channel_id=1, source_target_pairs={{1,3},{2,0},{3,5},{4,2},{5,7},{6,4},{9,11},{10,8},{11,13},{12,10},... | collective-permute-start | bytes 1572872 | tf_op jit(solution)/shard_map/ppermute | solution.py:328
  57.4 4.0 %collective-permute-done.11.refs_1_ = f32[2,256,256]{2,1,0:T(8,128)S(1)} collective-permute-done((f32[2,256,256]{2,1,0:T(8,128)S(1)}, f32[2,256,256]{2,1,0:T(8,128)S(1)}, u32[]{:S(2)}, u32[]{:S(2)}) %collective-permute-start.11) | collective-permute-done | bytes 524320 | tf_op jit(solution)/shard_map/ppermute | solution.py:328
  61.4 1.3 %collective-permute-start.15 = (f32[2,256,256]{2,1,0:T(8,128)S(1)}, f32[2,256,256]{2,1,0:T(8,128)S(1)}, u32[]{:S(2)}, u32[]{:S(2)}) collective-permute-start(f32[2,256,256]{2,1,0:T(8,128)S(1)} %collective-permute-done.11.refs_1_), channel_id=1, source_target_pairs={{1,3},{2,0},{3,5},{4,2},{5,7},{6,4},{9,11},{10,8},{11,13},{12,10},... | collective-permute-start | bytes 1572872 | tf_op jit(solution)/shard_map/ppermute | solution.py:328
  62.7 1.8 %collective-permute-done.12.refs_2_ = f32[2,256,256]{2,1,0:T(8,128)S(1)} collective-permute-done((f32[2,256,256]{2,1,0:T(8,128)S(1)}, f32[2,256,256]{2,1,0:T(8,128)S(1)}, u32[]{:S(2)}, u32[]{:S(2)}) %collective-permute-start.12) | collective-permute-done | bytes 524320 | tf_op jit(solution)/shard_map/ppermute | solution.py:328
  64.5 5.5 %collective-permute-start.17 = (f32[2,256,256]{2,1,0:T(8,128)S(1)}, f32[2,256,256]{2,1,0:T(8,128)S(1)}, u32[]{:S(2)}, u32[]{:S(2)}) collective-permute-start(f32[2,256,256]{2,1,0:T(8,128)S(1)} %collective-permute-done.11.refs_1_), channel_id=1, source_target_pairs={{0,2},{2,4},{3,1},{4,6},{5,3},{7,5},{11,9},{13,11},{15,13},{16,18}... | collective-permute-start | bytes 1572872 | tf_op jit(solution)/shard_map/ppermute | solution.py:328
  70.0 4.5 %collective-permute-done.13.refs_3_ = f32[2,256,256]{2,1,0:T(8,128)S(1)} collective-permute-done((f32[2,256,256]{2,1,0:T(8,128)S(1)}, f32[2,256,256]{2,1,0:T(8,128)S(1)}, u32[]{:S(2)}, u32[]{:S(2)}) %collective-permute-start.13) | collective-permute-done | bytes 524320 | tf_op jit(solution)/shard_map/ppermute | solution.py:328
  74.5 1.3 %collective-permute-start.18 = (f32[2,256,256]{2,1,0:T(8,128)S(1)}, f32[2,256,256]{2,1,0:T(8,128)S(1)}, u32[]{:S(2)}, u32[]{:S(2)}) collective-permute-start(f32[2,256,256]{2,1,0:T(8,128)S(1)} %collective-permute-done.12.refs_2_), channel_id=1, source_target_pairs={{1,3},{2,0},{3,5},{4,2},{5,7},{6,4},{9,11},{10,8},{11,13},{12,10},... | collective-permute-start | bytes 1572872 | tf_op jit(solution)/shard_map/ppermute | solution.py:328
  75.8 4.6 %collective-permute-start.19 = (f32[2,256,256]{2,1,0:T(8,128)S(1)}, f32[2,256,256]{2,1,0:T(8,128)S(1)}, u32[]{:S(2)}, u32[]{:S(2)}) collective-permute-start(f32[2,256,256]{2,1,0:T(8,128)S(1)} %collective-permute-done.12.refs_2_), channel_id=1, source_target_pairs={{0,2},{2,4},{3,1},{4,6},{5,3},{7,5},{8,10},{10,12},{12,14},{19,17}... | collective-permute-start | bytes 1572872 | tf_op jit(solution)/shard_map/ppermute | solution.py:328
  81.1 2.9 %shard_map.90 = (f32[4,2,256,256]{3,2,1,0:T(8,128)S(1)}, f32[4,2,256,256]{3,2,1,0:T(8,128)S(1)}) custom-call(f32[8,128]{1,0:T(8,128)S(1)} %shard_map.85.weight_ref, f32[2,256,256]{2,1,0:T(8,128)S(1)} %get-tuple-element.25.refs_0_, f32[2,256,256]{2,1,0:T(8,128)S(1)} %collective-permute-done.11.refs_1_, f32[2,256,256]{2,1,0:T(8,128)S(1)} %collective-permute-done.12.refs_2_, ...), custom_call_target="tpu_custom_call" | custom-call | tf_op jit(solution)/shard_map/pallas_call | solution.py:297
  84.0 3.3 %collective-permute-done.18.refs_2_ = f32[2,256,256]{2,1,0:T(8,128)S(1)} collective-permute-done((f32[2,256,256]{2,1,0:T(8,128)S(1)}, f32[2,256,256]{2,1,0:T(8,128)S(1)}, u32[]{:S(2)}, u32[]{:S(2)}) %collective-permute-start.18) | collective-permute-done | bytes 524320 | tf_op jit(solution)/shard_map/ppermute | solution.py:328
  87.3 3.4 %collective-permute-done.19.refs_3_ = f32[2,256,256]{2,1,0:T(8,128)S(1)} collective-permute-done((f32[2,256,256]{2,1,0:T(8,128)S(1)}, f32[2,256,256]{2,1,0:T(8,128)S(1)}, u32[]{:S(2)}, u32[]{:S(2)}) %collective-permute-start.19) | collective-permute-done | bytes 524320 | tf_op jit(solution)/shard_map/ppermute | solution.py:328
  90.6 1.4 %shard_map.91 = (f32[4,2,256,256]{3,2,1,0:T(8,128)S(1)}, f32[4,2,256,256]{3,2,1,0:T(8,128)S(1)}) custom-call(f32[8,128]{1,0:T(8,128)S(1)} %shard_map.85.weight_ref, f32[4,2,256,256]{3,2,1,0:T(8,128)S(1)} %get-tuple-element.29.refs_0_, f32[4,2,256,256]{3,2,1,0:T(8,128)S(1)} %get-tuple-element.30.refs_1_, f32[2,256,256]{2,1,0:T(8,128)S(1)} %collective-permute-done.18.refs_2_, ...), custom_call_target="tpu_custom_call" | custom-call | tf_op jit(solution)/shard_map/pallas_call | solution.py:297
  92.0 6.1 %collective-permute-start.20 = (f32[4,2,256,256]{3,2,1,0:T(8,128)S(1)}, f32[4,2,256,256]{3,2,1,0:T(8,128)S(1)}, u32[]{:S(2)}, u32[]{:S(2)}) collective-permute-start(f32[4,2,256,256]{3,2,1,0:T(8,128)S(1)} %get-tuple-element.32), channel_id=1, source_target_pairs={{0,1},{1,0},{2,3},{3,2},{4,5},{5,4},{6,7},{7,6},{8,9},{9,8},{10,11... | collective-permute-start | bytes 6291464 | tf_op jit(solution)/shard_map/ppermute | solution.py:328
  98.1 1.3 %collective-permute-start.21 = (f32[2,256,256]{2,1,0:T(8,128)S(1)}, f32[2,256,256]{2,1,0:T(8,128)S(1)}, u32[]{:S(2)}, u32[]{:S(2)}) collective-permute-start(f32[2,256,256]{2,1,0:T(8,128)S(1)} %collective-permute-done.13.refs_3_), channel_id=1, source_target_pairs={{1,3},{2,0},{3,5},{4,2},{5,7},{6,4},{9,11},{10,8},{11,13},{12,10},... | collective-permute-start | bytes 1572872 | tf_op jit(solution)/shard_map/ppermute | solution.py:328
  99.4 4.6 %collective-permute-start.22 = (f32[2,256,256]{2,1,0:T(8,128)S(1)}, f32[2,256,256]{2,1,0:T(8,128)S(1)}, u32[]{:S(2)}, u32[]{:S(2)}) collective-permute-start(f32[2,256,256]{2,1,0:T(8,128)S(1)} %collective-permute-done.13.refs_3_), channel_id=1, source_target_pairs={{0,2},{2,4},{4,6},{8,10},{10,12},{11,9},{12,14},{13,11},{15,13},{1... | collective-permute-start | bytes 1572872 | tf_op jit(solution)/shard_map/ppermute | solution.py:328
  104.0 5.2 %collective-permute-done.21.refs_0_ = f32[2,256,256]{2,1,0:T(8,128)S(1)} collective-permute-done((f32[2,256,256]{2,1,0:T(8,128)S(1)}, f32[2,256,256]{2,1,0:T(8,128)S(1)}, u32[]{:S(2)}, u32[]{:S(2)}) %collective-permute-start.21) | collective-permute-done | bytes 524320 | tf_op jit(solution)/shard_map/ppermute | solution.py:328
  109.2 2.3 %collective-permute-done.22.refs_1_ = f32[2,256,256]{2,1,0:T(8,128)S(1)} collective-permute-done((f32[2,256,256]{2,1,0:T(8,128)S(1)}, f32[2,256,256]{2,1,0:T(8,128)S(1)}, u32[]{:S(2)}, u32[]{:S(2)}) %collective-permute-start.22) | collective-permute-done | bytes 524320 | tf_op jit(solution)/shard_map/ppermute | solution.py:328
  111.4 2.1 %shard_map.92 = f32[1,4,2,256,256]{4,3,2,1,0:T(8,128)} custom-call(f32[8,128]{1,0:T(8,128)S(1)} %shard_map.85.weight_ref, f32[4,2,256,256]{3,2,1,0:T(8,128)S(1)} %get-tuple-element.31.own_ref, f32[4,2,256,256]{3,2,1,0:T(8,128)S(1)} %collective-permute-done.20.partner_ref, f32[2,256,256]{2,1,0:T(8,128)S(1)} %collective-permute-done.21.refs_0_, ...), custom_call_target="tpu_custom_call" | custom-call | tf_op jit(solution)/shard_map/pallas_call | solution.py:297
  (31 shorter events, 5.2 us)
Async XLA Ops:
  2.3 6.9 %collective-permute-start.6 = (f32[128,256]{1,0:T(8,128)S(1)}, f32[128,256]{1,0:T(8,128)S(1)}, u32[]{:S(2)}, u32[]{:S(2)}) collective-permute-start(f32[128,256]{1,0:T(8,128)S(1)} %get-tuple-element.24), channel_id=1, source_target_pairs={{0,8},{1,9},{2,10},{3,11},{4,12},{5,13},{6,14},{7,15},{8,0},{9,1},... | collective-permute-start | bytes 393224 | tf_op jit(solution)/shard_map/ppermute | solution.py:328
  5.3 7.8 %collective-permute-start.7 = (f32[128,256]{1,0:T(8,128)S(1)}, f32[128,256]{1,0:T(8,128)S(1)}, u32[]{:S(2)}, u32[]{:S(2)}) collective-permute-start(f32[128,256]{1,0:T(8,128)S(1)} %get-tuple-element.24), channel_id=1, source_target_pairs={{0,16},{1,17},{2,18},{3,19},{4,20},{5,21},{6,22},{7,23},{8,24},{9,... | collective-permute-start | bytes 393224 | tf_op jit(solution)/shard_map/ppermute | solution.py:328
  6.8 6.3 %collective-permute-start.8 = (f32[128,256]{1,0:T(8,128)S(1)}, f32[128,256]{1,0:T(8,128)S(1)}, u32[]{:S(2)}, u32[]{:S(2)}) collective-permute-start(f32[128,256]{1,0:T(8,128)S(1)} %get-tuple-element.24), channel_id=1, source_target_pairs={{0,24},{1,25},{2,26},{3,27},{4,28},{5,29},{6,30},{7,31},{8,16},{9,... | collective-permute-start | bytes 393224 | tf_op jit(solution)/shard_map/ppermute | solution.py:328
  13.1 9.7 %collective-permute-start.9 = (f32[3,128,256]{2,1,0:T(8,128)S(1)}, f32[3,128,256]{2,1,0:T(8,128)S(1)}, u32[]{:S(2)}, u32[]{:S(2)}) collective-permute-start(f32[3,128,256]{2,1,0:T(8,128)S(1)} %shard_map.87.near_ref), channel_id=1, source_target_pairs={{0,2},{1,3},{2,0},{3,1},{4,6},{5,7},{6,4},{7,5},{8,10},{9,11},{10,... | collective-permute-start | bytes 1179656 | tf_op jit(solution)/shard_map/ppermute | solution.py:328
  14.8 12.4 %collective-permute-start = (f32[2,256,256]{2,1,0:T(8,128)S(1)}, f32[2,256,256]{2,1,0:T(8,128)S(1)}, u32[]{:S(2)}, u32[]{:S(2)}) collective-permute-start(f32[2,256,256]{2,1,0:T(8,128)S(1)} %get-tuple-element.20), channel_id=1, source_target_pairs={{0,8},{2,10},{4,12},{6,14},{8,0},{10,2},{12,4},{14,6},{16,24},{18,... | collective-permute-start | bytes 1572872 | tf_op jit(solution)/shard_map/ppermute | solution.py:328
  17.9 11.1 %collective-permute-start.1 = (f32[2,256,256]{2,1,0:T(8,128)S(1)}, f32[2,256,256]{2,1,0:T(8,128)S(1)}, u32[]{:S(2)}, u32[]{:S(2)}) collective-permute-start(f32[2,256,256]{2,1,0:T(8,128)S(1)} %get-tuple-element.21), channel_id=1, source_target_pairs={{0,16},{2,18},{4,20},{6,22},{8,24},{10,26},{12,28},{14,30},{16,0},... | collective-permute-start | bytes 1572872 | tf_op jit(solution)/shard_map/ppermute | solution.py:328
  22.9 18.5 %collective-permute-start.10 = (f32[3,256,256]{2,1,0:T(8,128)S(1)}, f32[3,256,256]{2,1,0:T(8,128)S(1)}, u32[]{:S(2)}, u32[]{:S(2)}) collective-permute-start(f32[3,256,256]{2,1,0:T(8,128)S(1)} %shard_map.88.refs_8_), channel_id=1, source_target_pairs={{0,1},{1,0},{2,3},{3,2},{4,5},{5,4},{6,7},{7,6},{8,9},{9,8},{10,11... | collective-permute-start | bytes 2359304 | tf_op jit(solution)/shard_map/ppermute | solution.py:328
  23.0 18.4 %collective-permute-start.3 = (f32[2,256,256]{2,1,0:T(8,128)S(1)}, f32[2,256,256]{2,1,0:T(8,128)S(1)}, u32[]{:S(2)}, u32[]{:S(2)}) collective-permute-start(f32[2,256,256]{2,1,0:T(8,128)S(1)} %get-tuple-element.20), channel_id=1, source_target_pairs={{1,9},{3,11},{5,13},{7,15},{9,1},{11,3},{13,5},{15,7},{17,25},{19,... | collective-permute-start | bytes 1572872 | tf_op jit(solution)/shard_map/ppermute | solution.py:328
  23.7 17.7 %collective-permute-start.2 = (f32[2,256,256]{2,1,0:T(8,128)S(1)}, f32[2,256,256]{2,1,0:T(8,128)S(1)}, u32[]{:S(2)}, u32[]{:S(2)}) collective-permute-start(f32[2,256,256]{2,1,0:T(8,128)S(1)} %get-tuple-element.22), channel_id=1, source_target_pairs={{0,24},{2,26},{4,28},{6,30},{8,16},{10,18},{12,20},{14,22},{16,8},... | collective-permute-start | bytes 1572872 | tf_op jit(solution)/shard_map/ppermute | solution.py:328
  27.2 14.2 %collective-permute-start.4 = (f32[2,256,256]{2,1,0:T(8,128)S(1)}, f32[2,256,256]{2,1,0:T(8,128)S(1)}, u32[]{:S(2)}, u32[]{:S(2)}) collective-permute-start(f32[2,256,256]{2,1,0:T(8,128)S(1)} %get-tuple-element.21), channel_id=1, source_target_pairs={{1,17},{3,19},{5,21},{7,23},{9,25},{11,27},{13,29},{15,31},{17,1},... | collective-permute-start | bytes 1572872 | tf_op jit(solution)/shard_map/ppermute | solution.py:328
  29.0 12.4 %collective-permute-start.5 = (f32[2,256,256]{2,1,0:T(8,128)S(1)}, f32[2,256,256]{2,1,0:T(8,128)S(1)}, u32[]{:S(2)}, u32[]{:S(2)}) collective-permute-start(f32[2,256,256]{2,1,0:T(8,128)S(1)} %get-tuple-element.22), channel_id=1, source_target_pairs={{1,25},{3,27},{5,29},{7,31},{9,17},{11,19},{13,21},{15,23},{17,9},... | collective-permute-start | bytes 1572872 | tf_op jit(solution)/shard_map/ppermute | solution.py:328
  41.4 39.0 %copy-start = (f32[8]{0:T(128)S(1)}, f32[8]{0:T(128)}, u32[]{:S(2)}) copy-start(f32[8]{0:T(128)} %value_ref.1) | copy-start | bytes 100
  41.4 39.0 %copy-start.1 = (s32[8]{0:T(128)S(1)}, s32[8]{0:T(128)}, u32[]{:S(2)}) copy-start(s32[8]{0:T(128)} %offset_ref.1) | copy-start | bytes 100
  51.8 9.6 %collective-permute-start.11 = (f32[2,256,256]{2,1,0:T(8,128)S(1)}, f32[2,256,256]{2,1,0:T(8,128)S(1)}, u32[]{:S(2)}, u32[]{:S(2)}) collective-permute-start(f32[2,256,256]{2,1,0:T(8,128)S(1)} %get-tuple-element.26), channel_id=1, source_target_pairs={{0,8},{1,9},{2,10},{3,11},{4,12},{5,13},{6,14},{7,15},{8,0},{9,1},... | collective-permute-start | bytes 1572872 | tf_op jit(solution)/shard_map/ppermute | solution.py:328
  53.5 11.0 %collective-permute-start.12 = (f32[2,256,256]{2,1,0:T(8,128)S(1)}, f32[2,256,256]{2,1,0:T(8,128)S(1)}, u32[]{:S(2)}, u32[]{:S(2)}) collective-permute-start(f32[2,256,256]{2,1,0:T(8,128)S(1)} %get-tuple-element.27), channel_id=1, source_target_pairs={{0,16},{1,17},{2,18},{3,19},{4,20},{5,21},{6,22},{7,23},{8,24},{9,... | collective-permute-start | bytes 1572872 | tf_op jit(solution)/shard_map/ppermute | solution.py:328
  54.0 20.6 %collective-permute-start.13 = (f32[2,256,256]{2,1,0:T(8,128)S(1)}, f32[2,256,256]{2,1,0:T(8,128)S(1)}, u32[]{:S(2)}, u32[]{:S(2)}) collective-permute-start(f32[2,256,256]{2,1,0:T(8,128)S(1)} %get-tuple-element.28), channel_id=1, source_target_pairs={{0,24},{1,25},{2,26},{3,27},{4,28},{5,29},{6,30},{7,31},{8,16},{9,... | collective-permute-start | bytes 1572872 | tf_op jit(solution)/shard_map/ppermute | solution.py:328
  55.4 20.5 %collective-permute-start.14 = (f32[2,256,256]{2,1,0:T(8,128)S(1)}, f32[2,256,256]{2,1,0:T(8,128)S(1)}, u32[]{:S(2)}, u32[]{:S(2)}) collective-permute-start(f32[2,256,256]{2,1,0:T(8,128)S(1)} %get-tuple-element.25.refs_0_), channel_id=1, source_target_pairs={{1,3},{2,0},{3,5},{4,2},{5,7},{6,4},{9,11},{10,8},{11,13},{12,10},... | collective-permute-start | bytes 1572872 | tf_op jit(solution)/shard_map/ppermute | solution.py:328
  56.7 24.4 %collective-permute-start.16 = (f32[2,256,256]{2,1,0:T(8,128)S(1)}, f32[2,256,256]{2,1,0:T(8,128)S(1)}, u32[]{:S(2)}, u32[]{:S(2)}) collective-permute-start(f32[2,256,256]{2,1,0:T(8,128)S(1)} %get-tuple-element.25.refs_0_), channel_id=1, source_target_pairs={{3,1},{5,3},{7,5},{8,10},{10,12},{11,9},{12,14},{13,11},{15,13},{1... | collective-permute-start | bytes 1572872 | tf_op jit(solution)/shard_map/ppermute | solution.py:328
  61.4 19.7 %collective-permute-start.15 = (f32[2,256,256]{2,1,0:T(8,128)S(1)}, f32[2,256,256]{2,1,0:T(8,128)S(1)}, u32[]{:S(2)}, u32[]{:S(2)}) collective-permute-start(f32[2,256,256]{2,1,0:T(8,128)S(1)} %collective-permute-done.11.refs_1_), channel_id=1, source_target_pairs={{1,3},{2,0},{3,5},{4,2},{5,7},{6,4},{9,11},{10,8},{11,13},{12,10},... | collective-permute-start | bytes 1572872 | tf_op jit(solution)/shard_map/ppermute | solution.py:328
  64.5 16.6 %collective-permute-start.17 = (f32[2,256,256]{2,1,0:T(8,128)S(1)}, f32[2,256,256]{2,1,0:T(8,128)S(1)}, u32[]{:S(2)}, u32[]{:S(2)}) collective-permute-start(f32[2,256,256]{2,1,0:T(8,128)S(1)} %collective-permute-done.11.refs_1_), channel_id=1, source_target_pairs={{0,2},{2,4},{3,1},{4,6},{5,3},{7,5},{11,9},{13,11},{15,13},{16,18}... | collective-permute-start | bytes 1572872 | tf_op jit(solution)/shard_map/ppermute | solution.py:328
  74.5 12.7 %collective-permute-start.18 = (f32[2,256,256]{2,1,0:T(8,128)S(1)}, f32[2,256,256]{2,1,0:T(8,128)S(1)}, u32[]{:S(2)}, u32[]{:S(2)}) collective-permute-start(f32[2,256,256]{2,1,0:T(8,128)S(1)} %collective-permute-done.12.refs_2_), channel_id=1, source_target_pairs={{1,3},{2,0},{3,5},{4,2},{5,7},{6,4},{9,11},{10,8},{11,13},{12,10},... | collective-permute-start | bytes 1572872 | tf_op jit(solution)/shard_map/ppermute | solution.py:328
  75.8 14.8 %collective-permute-start.19 = (f32[2,256,256]{2,1,0:T(8,128)S(1)}, f32[2,256,256]{2,1,0:T(8,128)S(1)}, u32[]{:S(2)}, u32[]{:S(2)}) collective-permute-start(f32[2,256,256]{2,1,0:T(8,128)S(1)} %collective-permute-done.12.refs_2_), channel_id=1, source_target_pairs={{0,2},{2,4},{3,1},{4,6},{5,3},{7,5},{8,10},{10,12},{12,14},{19,17}... | collective-permute-start | bytes 1572872 | tf_op jit(solution)/shard_map/ppermute | solution.py:328
  92.0 19.5 %collective-permute-start.20 = (f32[4,2,256,256]{3,2,1,0:T(8,128)S(1)}, f32[4,2,256,256]{3,2,1,0:T(8,128)S(1)}, u32[]{:S(2)}, u32[]{:S(2)}) collective-permute-start(f32[4,2,256,256]{3,2,1,0:T(8,128)S(1)} %get-tuple-element.32), channel_id=1, source_target_pairs={{0,1},{1,0},{2,3},{3,2},{4,5},{5,4},{6,7},{7,6},{8,9},{9,8},{10,11... | collective-permute-start | bytes 6291464 | tf_op jit(solution)/shard_map/ppermute | solution.py:328
  98.1 11.1 %collective-permute-start.21 = (f32[2,256,256]{2,1,0:T(8,128)S(1)}, f32[2,256,256]{2,1,0:T(8,128)S(1)}, u32[]{:S(2)}, u32[]{:S(2)}) collective-permute-start(f32[2,256,256]{2,1,0:T(8,128)S(1)} %collective-permute-done.13.refs_3_), channel_id=1, source_target_pairs={{1,3},{2,0},{3,5},{4,2},{5,7},{6,4},{9,11},{10,8},{11,13},{12,10},... | collective-permute-start | bytes 1572872 | tf_op jit(solution)/shard_map/ppermute | solution.py:328
  99.4 12.0 %collective-permute-start.22 = (f32[2,256,256]{2,1,0:T(8,128)S(1)}, f32[2,256,256]{2,1,0:T(8,128)S(1)}, u32[]{:S(2)}, u32[]{:S(2)}) collective-permute-start(f32[2,256,256]{2,1,0:T(8,128)S(1)} %collective-permute-done.13.refs_3_), channel_id=1, source_target_pairs={{0,2},{2,4},{4,6},{8,10},{10,12},{11,9},{12,14},{13,11},{15,13},{1... | collective-permute-start | bytes 1572872 | tf_op jit(solution)/shard_map/ppermute | solution.py:328
  109.2 2.3 %collective-permute-start.23 = (f32[2,256,256]{2,1,0:T(8,128)S(1)}, f32[2,256,256]{2,1,0:T(8,128)S(1)}, u32[]{:S(2)}, u32[]{:S(2)}) collective-permute-start(f32[2,256,256]{2,1,0:T(8,128)S(1)} %collective-permute-done.21.refs_0_), channel_id=1, source_target_pairs={{0,1},{1,0},{2,3},{3,2},{4,5},{5,4},{6,7},{7,6},{8,9},{9,8},{10,11... | collective-permute-start | bytes 1572872 | tf_op jit(solution)/shard_map/ppermute | solution.py:328

commit v4 on v3

--- a/solution.py
+++ b/solution.py
@@ -83,6 +83,10 @@
         g_r, g_i = product(split_pair((f_r, f_i)), es)
         f_r, f_i = f_r + g_r, f_i + g_i
     return col_r * f_r - col_i * f_i, col_r * f_i + col_i * f_r
+
+
+def turn(layer_count):
+    return layer_count // 2
 
 
 def prep_kernel(
@@ -124,7 +128,7 @@
     fixed_i = -0.5 * (h_i - h_i.T) + own * q_r + jnp.where(eye, broad_ref[...], 0.0)
     copies[5].wait()
     for k, base_ref in enumerate(base_refs):
-        mine = jnp.bitwise_xor(layer, k)
+        mine = jnp.bitwise_xor(layer, k ^ turn(len(base_refs)))
         level = -1.0 + 2.0 * ((first + mine).astype(F32) + 0.5) / grid_size
         base_ref[0] = fixed_r - prior_ref[0, mine, 0] + jnp.where(eye, level, 0.0)
         base_ref[1] = fixed_i - prior_ref[0, mine, 1]
@@ -189,7 +193,7 @@
                 out_refs[k][0], out_refs[k][1] = g_r, g_i
         return carry
 
-    lax.fori_loop(0, layer_count, step, 0)
+    lax.fori_loop(0, layer_count, step, 0, unroll=True)
 
 
 STEP_ROWS = 16
@@ -210,7 +214,7 @@
     away = 2 * core - 1
     shift = jnp.where(kind == INNER, -away, jnp.where(kind == MINE, 0, away))
     far_core = jnp.where(kind == CROSSED, 1 - core, core)
-    source = jnp.bitwise_xor(lane % layer_count, layer)
+    source = jnp.bitwise_xor((lane % layer_count) ^ turn(layer_count), layer)
     target = jnp.where(row < per_device, per_device * core, -per_device * core) + row
     gap = 2 * per_device * shift + per_device * far_core + source - target
     total = jnp.zeros(shape, F32)
@@ -364,7 +368,7 @@
     mine = [greens[0]] + [to_layer(greens[k], k) for k in ks]
 
     def reached(l, g, k, step):
-        spot = per_device * (g % 2) + (l ^ k)
+        spot = per_device * (g % 2) + (l ^ k ^ turn(layer_count))
         return (span - spot if step > 0 else spot + 1) <= REACH
 
     inner, outer = [], []
@@ -407,7 +411,7 @@
         functools.partial(last_kernel, slots_of(ending)),
         [own, given] + [kinds[kind][k] for kind, k in ending],
         jax.ShapeDtypeStruct(shape, F32), [weights],
-        [VMEM(shape, F32), pltpu.SemaphoreType.DMA((2, 2))], out_specs=HBM_SPEC,
+        [VMEM(shape, F32), pltpu.SemaphoreType.DMA((2, 4))], out_specs=HBM_SPEC,
     )
 
 

time: 115 us -> 116 us (level)
  the two profiles are of different devices: /device:TPU:0 before, /device:TPU:19 now
where the time goes in v4:
time: 116 us
  waiting for transfers between devices  51.5 us (44%)
  starting transfers between devices  44.1 us (38%)
  Pallas kernels  19.8 us (17%)
    ppermute x24, waiting for transfers between devices, move(): return lax.ppermute(x, AXES, pairs)  51.5 us
    ppermute x24, starting transfers between devices, move(): return lax.ppermute(x, AXES, pairs)  44.1 us
    pallas_call x11, Pallas kernels, run(): pl.pallas_call(kernel, in_specs=[SMEM_SPEC] * len(head) + [pl.BlockSpec(m...  19.8 us
  transfers between devices with their start and end apart: 24, of which 12 were waited for; matrix products, arithmetic and copies ran while one was open for 0% of the time, Pallas kernels for 3%

profile of v4, /device:TPU:19, one launch (start us, length us, event | category | flops | bytes accessed | tf_op | source)
XLA Modules:
  0.0 115.8 jit_solution(9823220480657490585)
XLA Ops:
  0.0 2.3 %shard_map.86 = (f32[2,256,256]{2,1,0:T(8,128)S(1)}, f32[128,256]{1,0:T(8,128)S(1)}, f32[2,256,256]{2,1,0:T(8,128)S(1)}, f32[2,256,256]{2,1,0:T(8,128)S(1)}, f32...) custom-call(f32[1,2,256,256]{3,2,1,0:T(8,128)} %coup_hbm.1, s32[1,256,256]{2,1,0:T(8,128)} %mask_hbm.1, ...), custom_call_target="tpu_custom_call" | custom-call | tf_op jit(solution)/shard_map/pallas_call | solution.py:301
  2.6 1.2 %collective-permute-start.7 = (f32[128,256]{1,0:T(8,128)S(1)}, f32[128,256]{1,0:T(8,128)S(1)}, u32[]{:S(2)}, u32[]{:S(2)}) collective-permute-start(f32[128,256]{1,0:T(8,128)S(1)} %get-tuple-element.24), channel_id=1, source_target_pairs={{0,16},{1,17},{2,18},{3,19},{4,20},{5,21},{6,22},{7,23},{8,24},{9,... | collective-permute-start | bytes 393224 | tf_op jit(solution)/shard_map/ppermute | solution.py:332
  3.9 1.2 collective-permute-start.8
  5.0 1.7 %collective-permute-done.6.refs_0_ = f32[128,256]{1,0:T(8,128)S(1)} collective-permute-done((f32[128,256]{1,0:T(8,128)S(1)}, f32[128,256]{1,0:T(8,128)S(1)}, u32[]{:S(2)}, u32[]{:S(2)}) %collective-permute-start.6) | collective-permute-done | bytes 131104 | tf_op jit(solution)/shard_map/ppermute | solution.py:332
  6.7 3.8 %collective-permute-done.8.refs_2_ = f32[128,256]{1,0:T(8,128)S(1)} collective-permute-done((f32[128,256]{1,0:T(8,128)S(1)}, f32[128,256]{1,0:T(8,128)S(1)}, u32[]{:S(2)}, u32[]{:S(2)}) %collective-permute-start.8) | collective-permute-done | bytes 131104 | tf_op jit(solution)/shard_map/ppermute | solution.py:332
  10.5 1.4 %collective-permute-start.9 = (f32[3,128,256]{2,1,0:T(8,128)S(1)}, f32[3,128,256]{2,1,0:T(8,128)S(1)}, u32[]{:S(2)}, u32[]{:S(2)}) collective-permute-start(f32[3,128,256]{2,1,0:T(8,128)S(1)} %shard_map.87.near_ref), channel_id=1, source_target_pairs={{0,2},{1,3},{2,0},{3,1},{4,6},{5,7},{6,4},{7,5},{8,10},{9,11},{10,... | collective-permute-start | bytes 1179656 | tf_op jit(solution)/shard_map/ppermute | solution.py:332
  13.3 6.5 %collective-permute-done.9.far_ref = f32[3,128,256]{2,1,0:T(8,128)S(1)} collective-permute-done((f32[3,128,256]{2,1,0:T(8,128)S(1)}, f32[3,128,256]{2,1,0:T(8,128)S(1)}, u32[]{:S(2)}, u32[]{:S(2)}) %collective-permute-start.9) | collective-permute-done | bytes 393248 | tf_op jit(solution)/shard_map/ppermute | solution.py:332
  19.8 2.5 %collective-permute-start.10 = (f32[3,256,256]{2,1,0:T(8,128)S(1)}, f32[3,256,256]{2,1,0:T(8,128)S(1)}, u32[]{:S(2)}, u32[]{:S(2)}) collective-permute-start(f32[3,256,256]{2,1,0:T(8,128)S(1)} %shard_map.88.refs_8_), channel_id=1, source_target_pairs={{0,1},{1,0},{2,3},{3,2},{4,5},{5,4},{6,7},{7,6},{8,9},{9,8},{10,11... | collective-permute-start | bytes 2359304 | tf_op jit(solution)/shard_map/ppermute | solution.py:332
  22.3 2.0 %collective-permute-start.3 = (f32[2,256,256]{2,1,0:T(8,128)S(1)}, f32[2,256,256]{2,1,0:T(8,128)S(1)}, u32[]{:S(2)}, u32[]{:S(2)}) collective-permute-start(f32[2,256,256]{2,1,0:T(8,128)S(1)} %get-tuple-element.20), channel_id=1, source_target_pairs={{1,9},{3,11},{5,13},{7,15},{9,1},{11,3},{13,5},{15,7},{17,25},{19,... | collective-permute-start | bytes 1572872 | tf_op jit(solution)/shard_map/ppermute | solution.py:332
  25.1 2.1 %collective-permute-start.4 = (f32[2,256,256]{2,1,0:T(8,128)S(1)}, f32[2,256,256]{2,1,0:T(8,128)S(1)}, u32[]{:S(2)}, u32[]{:S(2)}) collective-permute-start(f32[2,256,256]{2,1,0:T(8,128)S(1)} %get-tuple-element.21), channel_id=1, source_target_pairs={{1,17},{3,19},{5,21},{7,23},{9,25},{11,27},{13,29},{15,31},{17,1},... | collective-permute-start | bytes 1572872 | tf_op jit(solution)/shard_map/ppermute | solution.py:332
  27.2 4.2 %collective-permute-start.5 = (f32[2,256,256]{2,1,0:T(8,128)S(1)}, f32[2,256,256]{2,1,0:T(8,128)S(1)}, u32[]{:S(2)}, u32[]{:S(2)}) collective-permute-start(f32[2,256,256]{2,1,0:T(8,128)S(1)} %get-tuple-element.22), channel_id=1, source_target_pairs={{1,25},{3,27},{5,29},{7,31},{9,17},{11,19},{13,21},{15,23},{17,9},... | collective-permute-start | bytes 1572872 | tf_op jit(solution)/shard_map/ppermute | solution.py:332
  31.4 5.6 %collective-permute-done.3.refs_4_ = f32[2,256,256]{2,1,0:T(8,128)S(1)} collective-permute-done((f32[2,256,256]{2,1,0:T(8,128)S(1)}, f32[2,256,256]{2,1,0:T(8,128)S(1)}, u32[]{:S(2)}, u32[]{:S(2)}) %collective-permute-start.3) | collective-permute-done | bytes 524320 | tf_op jit(solution)/shard_map/ppermute | solution.py:332
  37.0 8.9 %collective-permute-done.4.refs_5_ = f32[2,256,256]{2,1,0:T(8,128)S(1)} collective-permute-done((f32[2,256,256]{2,1,0:T(8,128)S(1)}, f32[2,256,256]{2,1,0:T(8,128)S(1)}, u32[]{:S(2)}, u32[]{:S(2)}) %collective-permute-start.4) | collective-permute-done | bytes 524320 | tf_op jit(solution)/shard_map/ppermute | solution.py:332
  45.9 10.5 %shard_map.89 = (f32[2,256,256]{2,1,0:T(8,128)S(1)}, f32[2,256,256]{2,1,0:T(8,128)S(1)}, f32[2,256,256]{2,1,0:T(8,128)S(1)}, f32[2,256,256]{2,1,0:T(8,128)S(1)}) custom-call(f32[2,256,256]{2,1,0:T(8,128)S(1)} %get-tuple-element.19.refs_0_, f32[2,256,256]{2,1,0:T(8,128)S(1)} %collective-permute-done.refs_1_, ...), custom_call_target="tpu_custom_call" | custom-call | tf_op jit(solution)/shard_map/pallas_call | solution.py:301
  57.4 1.7 %collective-permute-start.13 = (f32[2,256,256]{2,1,0:T(8,128)S(1)}, f32[2,256,256]{2,1,0:T(8,128)S(1)}, u32[]{:S(2)}, u32[]{:S(2)}) collective-permute-start(f32[2,256,256]{2,1,0:T(8,128)S(1)} %get-tuple-element.28), channel_id=1, source_target_pairs={{0,24},{1,25},{2,26},{3,27},{4,28},{5,29},{6,30},{7,31},{8,16},{9,... | collective-permute-start | bytes 1572872 | tf_op jit(solution)/shard_map/ppermute | solution.py:332
  59.1 3.2 %collective-permute-start.14 = (f32[2,256,256]{2,1,0:T(8,128)S(1)}, f32[2,256,256]{2,1,0:T(8,128)S(1)}, u32[]{:S(2)}, u32[]{:S(2)}) collective-permute-start(f32[2,256,256]{2,1,0:T(8,128)S(1)} %get-tuple-element.25.refs_0_), channel_id=1, source_target_pairs={{1,3},{2,0},{3,5},{4,2},{5,7},{6,4},{9,11},{10,8},{11,13},{12,10},... | collective-permute-start | bytes 1572872 | tf_op jit(solution)/shard_map/ppermute | solution.py:332
  63.0 7.4 %collective-permute-done.11.refs_1_ = f32[2,256,256]{2,1,0:T(8,128)S(1)} collective-permute-done((f32[2,256,256]{2,1,0:T(8,128)S(1)}, f32[2,256,256]{2,1,0:T(8,128)S(1)}, u32[]{:S(2)}, u32[]{:S(2)}) %collective-permute-start.11) | collective-permute-done | bytes 524320 | tf_op jit(solution)/shard_map/ppermute | solution.py:332
  70.4 3.2 %collective-permute-start.15 = (f32[2,256,256]{2,1,0:T(8,128)S(1)}, f32[2,256,256]{2,1,0:T(8,128)S(1)}, u32[]{:S(2)}, u32[]{:S(2)}) collective-permute-start(f32[2,256,256]{2,1,0:T(8,128)S(1)} %collective-permute-done.11.refs_1_), channel_id=1, source_target_pairs={{1,3},{2,0},{3,5},{4,2},{5,7},{6,4},{9,11},{10,8},{11,13},{12,10},... | collective-permute-start | bytes 1572872 | tf_op jit(solution)/shard_map/ppermute | solution.py:332
  73.6 3.8 %collective-permute-done.12.refs_2_ = f32[2,256,256]{2,1,0:T(8,128)S(1)} collective-permute-done((f32[2,256,256]{2,1,0:T(8,128)S(1)}, f32[2,256,256]{2,1,0:T(8,128)S(1)}, u32[]{:S(2)}, u32[]{:S(2)}) %collective-permute-start.12) | collective-permute-done | bytes 524320 | tf_op jit(solution)/shard_map/ppermute | solution.py:332
  77.4 2.1 %collective-permute-start.17 = (f32[2,256,256]{2,1,0:T(8,128)S(1)}, f32[2,256,256]{2,1,0:T(8,128)S(1)}, u32[]{:S(2)}, u32[]{:S(2)}) collective-permute-start(f32[2,256,256]{2,1,0:T(8,128)S(1)} %collective-permute-done.11.refs_1_), channel_id=1, source_target_pairs={{0,2},{2,4},{4,6},{8,10},{10,12},{11,9},{12,14},{13,11},{15,13},{1... | collective-permute-start | bytes 1572872 | tf_op jit(solution)/shard_map/ppermute | solution.py:332
  79.5 3.2 %collective-permute-start.18 = (f32[2,256,256]{2,1,0:T(8,128)S(1)}, f32[2,256,256]{2,1,0:T(8,128)S(1)}, u32[]{:S(2)}, u32[]{:S(2)}) collective-permute-start(f32[2,256,256]{2,1,0:T(8,128)S(1)} %collective-permute-done.12.refs_2_), channel_id=1, source_target_pairs={{1,3},{2,0},{3,5},{4,2},{5,7},{6,4},{9,11},{10,8},{11,13},{12,10},... | collective-permute-start | bytes 1572872 | tf_op jit(solution)/shard_map/ppermute | solution.py:332
  82.7 2.1 %collective-permute-start.19 = (f32[2,256,256]{2,1,0:T(8,128)S(1)}, f32[2,256,256]{2,1,0:T(8,128)S(1)}, u32[]{:S(2)}, u32[]{:S(2)}) collective-permute-start(f32[2,256,256]{2,1,0:T(8,128)S(1)} %collective-permute-done.12.refs_2_), channel_id=1, source_target_pairs={{3,1},{5,3},{7,5},{8,10},{10,12},{11,9},{12,14},{13,11},{15,13},{1... | collective-permute-start | bytes 1572872 | tf_op jit(solution)/shard_map/ppermute | solution.py:332
  86.2 2.7 %collective-permute-done.17.refs_7_ = f32[2,256,256]{2,1,0:T(8,128)S(1)} collective-permute-done((f32[2,256,256]{2,1,0:T(8,128)S(1)}, f32[2,256,256]{2,1,0:T(8,128)S(1)}, u32[]{:S(2)}, u32[]{:S(2)}) %collective-permute-start.17) | collective-permute-done | bytes 524320 | tf_op jit(solution)/shard_map/ppermute | solution.py:332
  88.9 2.9 %shard_map.90 = (f32[4,2,256,256]{3,2,1,0:T(8,128)S(1)}, f32[4,2,256,256]{3,2,1,0:T(8,128)S(1)}) custom-call(f32[8,128]{1,0:T(8,128)S(1)} %shard_map.85.weight_ref, f32[2,256,256]{2,1,0:T(8,128)S(1)} %get-tuple-element.25.refs_0_, f32[2,256,256]{2,1,0:T(8,128)S(1)} %collective-permute-done.11.refs_1_, f32[2,256,256]{2,1,0:T(8,128)S(1)} %collective-permute-done.12.refs_2_, ...), custom_call_target="tpu_custom_call" | custom-call | tf_op jit(solution)/shard_map/pallas_call | solution.py:301
  91.8 3.8 %collective-permute-done.18.refs_2_ = f32[2,256,256]{2,1,0:T(8,128)S(1)} collective-permute-done((f32[2,256,256]{2,1,0:T(8,128)S(1)}, f32[2,256,256]{2,1,0:T(8,128)S(1)}, u32[]{:S(2)}, u32[]{:S(2)}) %collective-permute-start.18) | collective-permute-done | bytes 524320 | tf_op jit(solution)/shard_map/ppermute | solution.py:332
  95.6 1.4 %shard_map.91 = (f32[4,2,256,256]{3,2,1,0:T(8,128)S(1)}, f32[4,2,256,256]{3,2,1,0:T(8,128)S(1)}) custom-call(f32[8,128]{1,0:T(8,128)S(1)} %shard_map.85.weight_ref, f32[4,2,256,256]{3,2,1,0:T(8,128)S(1)} %get-tuple-element.29.refs_0_, f32[4,2,256,256]{3,2,1,0:T(8,128)S(1)} %get-tuple-element.30.refs_1_, f32[2,256,256]{2,1,0:T(8,128)S(1)} %collective-permute-done.18.refs_2_, ...), custom_call_target="tpu_custom_call" | custom-call | tf_op jit(solution)/shard_map/pallas_call | solution.py:301
  97.1 3.2 %collective-permute-start.21 = (f32[2,256,256]{2,1,0:T(8,128)S(1)}, f32[2,256,256]{2,1,0:T(8,128)S(1)}, u32[]{:S(2)}, u32[]{:S(2)}) collective-permute-start(f32[2,256,256]{2,1,0:T(8,128)S(1)} %collective-permute-done.13.refs_3_), channel_id=1, source_target_pairs={{1,3},{2,0},{3,5},{4,2},{5,7},{6,4},{9,11},{10,8},{11,13},{12,10},... | collective-permute-start | bytes 1572872 | tf_op jit(solution)/shard_map/ppermute | solution.py:332
  100.3 2.0 %collective-permute-start.22 = (f32[2,256,256]{2,1,0:T(8,128)S(1)}, f32[2,256,256]{2,1,0:T(8,128)S(1)}, u32[]{:S(2)}, u32[]{:S(2)}) collective-permute-start(f32[2,256,256]{2,1,0:T(8,128)S(1)} %collective-permute-done.13.refs_3_), channel_id=1, source_target_pairs={{0,2},{2,4},{3,1},{4,6},{5,3},{7,5},{11,9},{13,11},{15,13},{16,18}... | collective-permute-start | bytes 1572872 | tf_op jit(solution)/shard_map/ppermute | solution.py:332
  102.4 4.9 %collective-permute-done.21.refs_0_ = f32[2,256,256]{2,1,0:T(8,128)S(1)} collective-permute-done((f32[2,256,256]{2,1,0:T(8,128)S(1)}, f32[2,256,256]{2,1,0:T(8,128)S(1)}, u32[]{:S(2)}, u32[]{:S(2)}) %collective-permute-start.21) | collective-permute-done | bytes 524320 | tf_op jit(solution)/shard_map/ppermute | solution.py:332
  107.3 4.7 %collective-permute-start.23 = (f32[2,256,256]{2,1,0:T(8,128)S(1)}, f32[2,256,256]{2,1,0:T(8,128)S(1)}, u32[]{:S(2)}, u32[]{:S(2)}) collective-permute-start(f32[2,256,256]{2,1,0:T(8,128)S(1)} %collective-permute-done.21.refs_0_), channel_id=1, source_target_pairs={{0,1},{1,0},{2,3},{3,2},{4,5},{5,4},{6,7},{7,6},{8,9},{9,8},{10,11... | collective-permute-start | bytes 1572872 | tf_op jit(solution)/shard_map/ppermute | solution.py:332
  111.9 1.6 %collective-permute-done.22.refs_1_ = f32[2,256,256]{2,1,0:T(8,128)S(1)} collective-permute-done((f32[2,256,256]{2,1,0:T(8,128)S(1)}, f32[2,256,256]{2,1,0:T(8,128)S(1)}, u32[]{:S(2)}, u32[]{:S(2)}) %collective-permute-start.22) | collective-permute-done | bytes 524320 | tf_op jit(solution)/shard_map/ppermute | solution.py:332
  113.5 2.1 %shard_map.92 = f32[1,4,2,256,256]{4,3,2,1,0:T(8,128)} custom-call(f32[8,128]{1,0:T(8,128)S(1)} %shard_map.85.weight_ref, f32[4,2,256,256]{3,2,1,0:T(8,128)S(1)} %get-tuple-element.31.own_ref, f32[4,2,256,256]{3,2,1,0:T(8,128)S(1)} %collective-permute-done.20.partner_ref, f32[2,256,256]{2,1,0:T(8,128)S(1)} %collective-permute-done.21.refs_0_, ...), custom_call_target="tpu_custom_call" | custom-call | tf_op jit(solution)/shard_map/pallas_call | solution.py:301
  (31 shorter events, 5.7 us)
Async XLA Ops:
  2.3 4.4 %collective-permute-start.6 = (f32[128,256]{1,0:T(8,128)S(1)}, f32[128,256]{1,0:T(8,128)S(1)}, u32[]{:S(2)}, u32[]{:S(2)}) collective-permute-start(f32[128,256]{1,0:T(8,128)S(1)} %get-tuple-element.24), channel_id=1, source_target_pairs={{0,8},{1,9},{2,10},{3,11},{4,12},{5,13},{6,14},{7,15},{8,0},{9,1},... | collective-permute-start | bytes 393224 | tf_op jit(solution)/shard_map/ppermute | solution.py:332
  2.6 4.1 %collective-permute-start.7 = (f32[128,256]{1,0:T(8,128)S(1)}, f32[128,256]{1,0:T(8,128)S(1)}, u32[]{:S(2)}, u32[]{:S(2)}) collective-permute-start(f32[128,256]{1,0:T(8,128)S(1)} %get-tuple-element.24), channel_id=1, source_target_pairs={{0,16},{1,17},{2,18},{3,19},{4,20},{5,21},{6,22},{7,23},{8,24},{9,... | collective-permute-start | bytes 393224 | tf_op jit(solution)/shard_map/ppermute | solution.py:332
  3.9 6.7 %collective-permute-start.8 = (f32[128,256]{1,0:T(8,128)S(1)}, f32[128,256]{1,0:T(8,128)S(1)}, u32[]{:S(2)}, u32[]{:S(2)}) collective-permute-start(f32[128,256]{1,0:T(8,128)S(1)} %get-tuple-element.24), channel_id=1, source_target_pairs={{0,24},{1,25},{2,26},{3,27},{4,28},{5,29},{6,30},{7,31},{8,16},{9,... | collective-permute-start | bytes 393224 | tf_op jit(solution)/shard_map/ppermute | solution.py:332
  10.5 9.2 %collective-permute-start.9 = (f32[3,128,256]{2,1,0:T(8,128)S(1)}, f32[3,128,256]{2,1,0:T(8,128)S(1)}, u32[]{:S(2)}, u32[]{:S(2)}) collective-permute-start(f32[3,128,256]{2,1,0:T(8,128)S(1)} %shard_map.87.near_ref), channel_id=1, source_target_pairs={{0,2},{1,3},{2,0},{3,1},{4,6},{5,7},{6,4},{7,5},{8,10},{9,11},{10,... | collective-permute-start | bytes 1179656 | tf_op jit(solution)/shard_map/ppermute | solution.py:332
  11.9 13.1 %collective-permute-start = (f32[2,256,256]{2,1,0:T(8,128)S(1)}, f32[2,256,256]{2,1,0:T(8,128)S(1)}, u32[]{:S(2)}, u32[]{:S(2)}) collective-permute-start(f32[2,256,256]{2,1,0:T(8,128)S(1)} %get-tuple-element.20), channel_id=1, source_target_pairs={{0,8},{2,10},{4,12},{6,14},{8,0},{10,2},{12,4},{14,6},{16,24},{18,... | collective-permute-start | bytes 1572872 | tf_op jit(solution)/shard_map/ppermute | solution.py:332
  12.6 14.6 %collective-permute-start.1 = (f32[2,256,256]{2,1,0:T(8,128)S(1)}, f32[2,256,256]{2,1,0:T(8,128)S(1)}, u32[]{:S(2)}, u32[]{:S(2)}) collective-permute-start(f32[2,256,256]{2,1,0:T(8,128)S(1)} %get-tuple-element.21), channel_id=1, source_target_pairs={{0,16},{2,18},{4,20},{6,22},{8,24},{10,26},{12,28},{14,30},{16,0},... | collective-permute-start | bytes 1572872 | tf_op jit(solution)/shard_map/ppermute | solution.py:332
  19.8 26.0 %collective-permute-start.10 = (f32[3,256,256]{2,1,0:T(8,128)S(1)}, f32[3,256,256]{2,1,0:T(8,128)S(1)}, u32[]{:S(2)}, u32[]{:S(2)}) collective-permute-start(f32[3,256,256]{2,1,0:T(8,128)S(1)} %shard_map.88.refs_8_), channel_id=1, source_target_pairs={{0,1},{1,0},{2,3},{3,2},{4,5},{5,4},{6,7},{7,6},{8,9},{9,8},{10,11... | collective-permute-start | bytes 2359304 | tf_op jit(solution)/shard_map/ppermute | solution.py:332
  22.3 14.7 %collective-permute-start.3 = (f32[2,256,256]{2,1,0:T(8,128)S(1)}, f32[2,256,256]{2,1,0:T(8,128)S(1)}, u32[]{:S(2)}, u32[]{:S(2)}) collective-permute-start(f32[2,256,256]{2,1,0:T(8,128)S(1)} %get-tuple-element.20), channel_id=1, source_target_pairs={{1,9},{3,11},{5,13},{7,15},{9,1},{11,3},{13,5},{15,7},{17,25},{19,... | collective-permute-start | bytes 1572872 | tf_op jit(solution)/shard_map/ppermute | solution.py:332
  24.3 7.1 %collective-permute-start.2 = (f32[2,256,256]{2,1,0:T(8,128)S(1)}, f32[2,256,256]{2,1,0:T(8,128)S(1)}, u32[]{:S(2)}, u32[]{:S(2)}) collective-permute-start(f32[2,256,256]{2,1,0:T(8,128)S(1)} %get-tuple-element.22), channel_id=1, source_target_pairs={{0,24},{2,26},{4,28},{6,30},{8,16},{10,18},{12,20},{14,22},{16,8},... | collective-permute-start | bytes 1572872 | tf_op jit(solution)/shard_map/ppermute | solution.py:332
  25.1 20.8 %collective-permute-start.4 = (f32[2,256,256]{2,1,0:T(8,128)S(1)}, f32[2,256,256]{2,1,0:T(8,128)S(1)}, u32[]{:S(2)}, u32[]{:S(2)}) collective-permute-start(f32[2,256,256]{2,1,0:T(8,128)S(1)} %get-tuple-element.21), channel_id=1, source_target_pairs={{1,17},{3,19},{5,21},{7,23},{9,25},{11,27},{13,29},{15,31},{17,1},... | collective-permute-start | bytes 1572872 | tf_op jit(solution)/shard_map/ppermute | solution.py:332
  27.2 18.7 %collective-permute-start.5 = (f32[2,256,256]{2,1,0:T(8,128)S(1)}, f32[2,256,256]{2,1,0:T(8,128)S(1)}, u32[]{:S(2)}, u32[]{:S(2)}) collective-permute-start(f32[2,256,256]{2,1,0:T(8,128)S(1)} %get-tuple-element.22), channel_id=1, source_target_pairs={{1,25},{3,27},{5,29},{7,31},{9,17},{11,19},{13,21},{15,23},{17,9},... | collective-permute-start | bytes 1572872 | tf_op jit(solution)/shard_map/ppermute | solution.py:332
  45.9 38.9 %copy-start = (f32[8]{0:T(128)S(1)}, f32[8]{0:T(128)}, u32[]{:S(2)}) copy-start(f32[8]{0:T(128)} %value_ref.1) | copy-start | bytes 100
  45.9 38.9 %copy-start.1 = (s32[8]{0:T(128)S(1)}, s32[8]{0:T(128)}, u32[]{:S(2)}) copy-start(s32[8]{0:T(128)} %offset_ref.1) | copy-start | bytes 100
  56.4 14.0 %collective-permute-start.11 = (f32[2,256,256]{2,1,0:T(8,128)S(1)}, f32[2,256,256]{2,1,0:T(8,128)S(1)}, u32[]{:S(2)}, u32[]{:S(2)}) collective-permute-start(f32[2,256,256]{2,1,0:T(8,128)S(1)} %get-tuple-element.26), channel_id=1, source_target_pairs={{0,8},{1,9},{2,10},{3,11},{4,12},{5,13},{6,14},{7,15},{8,0},{9,1},... | collective-permute-start | bytes 1572872 | tf_op jit(solution)/shard_map/ppermute | solution.py:332
  57.2 20.2 %collective-permute-start.12 = (f32[2,256,256]{2,1,0:T(8,128)S(1)}, f32[2,256,256]{2,1,0:T(8,128)S(1)}, u32[]{:S(2)}, u32[]{:S(2)}) collective-permute-start(f32[2,256,256]{2,1,0:T(8,128)S(1)} %get-tuple-element.27), channel_id=1, source_target_pairs={{0,16},{1,17},{2,18},{3,19},{4,20},{5,21},{6,22},{7,23},{8,24},{9,... | collective-permute-start | bytes 1572872 | tf_op jit(solution)/shard_map/ppermute | solution.py:332
  57.4 22.0 %collective-permute-start.13 = (f32[2,256,256]{2,1,0:T(8,128)S(1)}, f32[2,256,256]{2,1,0:T(8,128)S(1)}, u32[]{:S(2)}, u32[]{:S(2)}) collective-permute-start(f32[2,256,256]{2,1,0:T(8,128)S(1)} %get-tuple-element.28), channel_id=1, source_target_pairs={{0,24},{1,25},{2,26},{3,27},{4,28},{5,29},{6,30},{7,31},{8,16},{9,... | collective-permute-start | bytes 1572872 | tf_op jit(solution)/shard_map/ppermute | solution.py:332
  59.1 23.6 %collective-permute-start.14 = (f32[2,256,256]{2,1,0:T(8,128)S(1)}, f32[2,256,256]{2,1,0:T(8,128)S(1)}, u32[]{:S(2)}, u32[]{:S(2)}) collective-permute-start(f32[2,256,256]{2,1,0:T(8,128)S(1)} %get-tuple-element.25.refs_0_), channel_id=1, source_target_pairs={{1,3},{2,0},{3,5},{4,2},{5,7},{6,4},{9,11},{10,8},{11,13},{12,10},... | collective-permute-start | bytes 1572872 | tf_op jit(solution)/shard_map/ppermute | solution.py:332
  62.3 23.1 %collective-permute-start.16 = (f32[2,256,256]{2,1,0:T(8,128)S(1)}, f32[2,256,256]{2,1,0:T(8,128)S(1)}, u32[]{:S(2)}, u32[]{:S(2)}) collective-permute-start(f32[2,256,256]{2,1,0:T(8,128)S(1)} %get-tuple-element.25.refs_0_), channel_id=1, source_target_pairs={{0,2},{2,4},{3,1},{4,6},{5,3},{7,5},{8,10},{10,12},{12,14},{19,17}... | collective-permute-start | bytes 1572872 | tf_op jit(solution)/shard_map/ppermute | solution.py:332
  70.4 15.8 %collective-permute-start.15 = (f32[2,256,256]{2,1,0:T(8,128)S(1)}, f32[2,256,256]{2,1,0:T(8,128)S(1)}, u32[]{:S(2)}, u32[]{:S(2)}) collective-permute-start(f32[2,256,256]{2,1,0:T(8,128)S(1)} %collective-permute-done.11.refs_1_), channel_id=1, source_target_pairs={{1,3},{2,0},{3,5},{4,2},{5,7},{6,4},{9,11},{10,8},{11,13},{12,10},... | collective-permute-start | bytes 1572872 | tf_op jit(solution)/shard_map/ppermute | solution.py:332
  77.4 11.6 %collective-permute-start.17 = (f32[2,256,256]{2,1,0:T(8,128)S(1)}, f32[2,256,256]{2,1,0:T(8,128)S(1)}, u32[]{:S(2)}, u32[]{:S(2)}) collective-permute-start(f32[2,256,256]{2,1,0:T(8,128)S(1)} %collective-permute-done.11.refs_1_), channel_id=1, source_target_pairs={{0,2},{2,4},{4,6},{8,10},{10,12},{11,9},{12,14},{13,11},{15,13},{1... | collective-permute-start | bytes 1572872 | tf_op jit(solution)/shard_map/ppermute | solution.py:332
  79.5 16.1 %collective-permute-start.18 = (f32[2,256,256]{2,1,0:T(8,128)S(1)}, f32[2,256,256]{2,1,0:T(8,128)S(1)}, u32[]{:S(2)}, u32[]{:S(2)}) collective-permute-start(f32[2,256,256]{2,1,0:T(8,128)S(1)} %collective-permute-done.12.refs_2_), channel_id=1, source_target_pairs={{1,3},{2,0},{3,5},{4,2},{5,7},{6,4},{9,11},{10,8},{11,13},{12,10},... | collective-permute-start | bytes 1572872 | tf_op jit(solution)/shard_map/ppermute | solution.py:332
  82.7 12.9 %collective-permute-start.19 = (f32[2,256,256]{2,1,0:T(8,128)S(1)}, f32[2,256,256]{2,1,0:T(8,128)S(1)}, u32[]{:S(2)}, u32[]{:S(2)}) collective-permute-start(f32[2,256,256]{2,1,0:T(8,128)S(1)} %collective-permute-done.12.refs_2_), channel_id=1, source_target_pairs={{3,1},{5,3},{7,5},{8,10},{10,12},{11,9},{12,14},{13,11},{15,13},{1... | collective-permute-start | bytes 1572872 | tf_op jit(solution)/shard_map/ppermute | solution.py:332
  97.0 16.6 %collective-permute-start.20 = (f32[4,2,256,256]{3,2,1,0:T(8,128)S(1)}, f32[4,2,256,256]{3,2,1,0:T(8,128)S(1)}, u32[]{:S(2)}, u32[]{:S(2)}) collective-permute-start(f32[4,2,256,256]{3,2,1,0:T(8,128)S(1)} %get-tuple-element.32), channel_id=1, source_target_pairs={{0,1},{1,0},{2,3},{3,2},{4,5},{5,4},{6,7},{7,6},{8,9},{9,8},{10,11... | collective-permute-start | bytes 6291464 | tf_op jit(solution)/shard_map/ppermute | solution.py:332
  97.1 10.2 %collective-permute-start.21 = (f32[2,256,256]{2,1,0:T(8,128)S(1)}, f32[2,256,256]{2,1,0:T(8,128)S(1)}, u32[]{:S(2)}, u32[]{:S(2)}) collective-permute-start(f32[2,256,256]{2,1,0:T(8,128)S(1)} %collective-permute-done.13.refs_3_), channel_id=1, source_target_pairs={{1,3},{2,0},{3,5},{4,2},{5,7},{6,4},{9,11},{10,8},{11,13},{12,10},... | collective-permute-start | bytes 1572872 | tf_op jit(solution)/shard_map/ppermute | solution.py:332
  100.3 13.2 %collective-permute-start.22 = (f32[2,256,256]{2,1,0:T(8,128)S(1)}, f32[2,256,256]{2,1,0:T(8,128)S(1)}, u32[]{:S(2)}, u32[]{:S(2)}) collective-permute-start(f32[2,256,256]{2,1,0:T(8,128)S(1)} %collective-permute-done.13.refs_3_), channel_id=1, source_target_pairs={{0,2},{2,4},{3,1},{4,6},{5,3},{7,5},{11,9},{13,11},{15,13},{16,18}... | collective-permute-start | bytes 1572872 | tf_op jit(solution)/shard_map/ppermute | solution.py:332
  107.3 6.3 %collective-permute-start.23 = (f32[2,256,256]{2,1,0:T(8,128)S(1)}, f32[2,256,256]{2,1,0:T(8,128)S(1)}, u32[]{:S(2)}, u32[]{:S(2)}) collective-permute-start(f32[2,256,256]{2,1,0:T(8,128)S(1)} %collective-permute-done.21.refs_0_), channel_id=1, source_target_pairs={{0,1},{1,0},{2,3},{3,2},{4,5},{5,4},{6,7},{7,6},{8,9},{9,8},{10,11... | collective-permute-start | bytes 1572872 | tf_op jit(solution)/shard_map/ppermute | solution.py:332
